TPU v7x, 32 devices: a whole 2x2x4 slice. The times are simulated.
32 devices in a mesh: gx: 4 (over y, x), gy: 2 (over core), gz: 4 (over z).
Axes of the slice: x: 2, y: 2, z: 4, core: 2. Of those that a mesh axis runs over, the one named last changes fastest.
Arguments:
- volume: bfloat16 [32, 64, 64, 32], P('gx', 'gy', 'gz'), may hold values from -6 to 6
- conv_in: bfloat16 [3, 3, 3, 32, 32], replicated, may hold values from -0.21875 to 0.21875
- conv_out: bfloat16 [3, 3, 3, 32, 32], replicated, may hold values from -0.21875 to 0.21875
- norm_gain: float32 [256], replicated, may hold values from 0.1 to 1.9
- q_weight: bfloat16 [256, 256], replicated, may hold values from -3 to 3
- kv_weight: bfloat16 [256, 512], replicated, may hold values from -0.375 to 0.375
- out_weight: bfloat16 [256, 256], replicated, may hold values from -0.375 to 0.375
- up_weight: bfloat16 [256, 256], replicated, may hold values from -0.375 to 0.375
Outputs:
- joined_out: bfloat16 [32, 64, 64, 32], P('gx', 'gy', 'gz')
All inputs are finite; a program needn't handle non-finite values.
Results may differ from a plain program's by a relative error of at most 0.012.
The roundings to bfloat16 on the way count: a program that leaves them out, or rounds other values in their place, can miss the bound.
Values may be sent and summed in bfloat16 or wider, within the bound.
No kernel may reach another device: no remote copies, remote signals or barrier semaphores. Data moves between devices by JAX's collectives and lax.ppermute only.
A program may use at most 64 MiB of HBM per device.

v0:
```python
import math

import jax
import jax.numpy as jnp
from jax import lax
from jax.sharding import PartitionSpec as P

HEADS = 8


def with_halo(cells, sides, width):
    for axis, dim in sides:
        count = lax.axis_size(axis)
        ends = count - 1
        head = lax.slice_in_dim(cells, 0, width, axis=dim)
        tail = lax.slice_in_dim(cells, cells.shape[dim] - width, cells.shape[dim], axis=dim)
        cells = jnp.concatenate(
            [
                lax.ppermute(tail, axis, [(i, (i + 1) % count) for i in range(ends)]),
                cells,
                lax.ppermute(head, axis, [((i + 1) % count, i) for i in range(ends)]),
            ],
            axis=dim,
        )
    return cells


def convolve(padded, kernel):
    return lax.conv_general_dilated(
        padded[None],
        kernel,
        (1, 1, 1),
        "VALID",
        dimension_numbers=("NDHWC", "DHWIO", "NDHWC"),
        preferred_element_type=jnp.float32,
    )[0]


def pad_brick(brick):
    return with_halo(brick, (("gx", 0), ("gy", 1), ("gz", 2)), 1)


def tokenize(volume_map):
    extent_x, extent_y, extent_z, channels = volume_map.shape
    grid_cells = volume_map.reshape(
        extent_x // 8, 2, 4, extent_y // 8, 2, 4, extent_z // 8, 2, 4, channels
    ).mean(axis=(2, 5, 8))
    grid_cells = grid_cells.transpose(0, 2, 4, 1, 3, 5, 6)
    return grid_cells.reshape(extent_x // 8 * (extent_y // 8) * (extent_z // 8), 8 * channels)


def spread_cells(token_rows, extent_x, extent_y, extent_z):
    channels = token_rows.shape[1] // 8
    grid_cells = token_rows.reshape(
        extent_x // 8, extent_y // 8, extent_z // 8, 2, 2, 2, channels
    ).transpose(0, 3, 1, 4, 2, 5, 6)
    grid_cells = jnp.broadcast_to(
        grid_cells[:, :, None, :, :, None, :, :, None, :],
        (extent_x // 8, 2, 4, extent_y // 8, 2, 4, extent_z // 8, 2, 4, channels),
    )
    return grid_cells.reshape(extent_x, extent_y, extent_z, channels)


def layer_norm(tokens, norm_gain):
    center = tokens - tokens.mean(axis=1, keepdims=True)
    spread = (center * center).mean(axis=1, keepdims=True)
    return (center * lax.rsqrt(spread + 1e-05) * norm_gain).astype(jnp.bfloat16)


def make_folder(queries, running, shard_piece):
    scaling = queries.shape[-1] ** (-0.5)
    key_count = shard_piece.shape[2]
    block_rows = math.gcd(key_count, 1024)

    def advance(position, state):
        peak_score, denominator, numerator = state
        head_keys = lax.dynamic_slice_in_dim(shard_piece[0], position * block_rows, block_rows, 1)
        head_values = lax.dynamic_slice_in_dim(shard_piece[1], position * block_rows, block_rows, 1)
        scores = (
            jnp.einsum("hqd,hkd->hqk", queries, head_keys, preferred_element_type=jnp.float32)
            * scaling
        )
        new_peak = jnp.maximum(peak_score, scores.max(axis=-1))
        rescale = jnp.exp(peak_score - new_peak)
        weights = jnp.exp(scores - new_peak[..., None])
        denominator = denominator * rescale + weights.sum(axis=-1)
        numerator = numerator * rescale[..., None] + jnp.einsum(
            "hqk,hkd->hqd",
            weights.astype(jnp.bfloat16),
            head_values,
            preferred_element_type=jnp.float32,
        )
        return (new_peak, denominator, numerator)

    return lax.fori_loop(0, key_count // block_rows, advance, running)


def start_state(queries):
    heads_here, query_count, head_size = queries.shape
    return (
        jnp.full((heads_here, query_count), -1e30, jnp.float32),
        jnp.zeros((heads_here, query_count), jnp.float32),
        jnp.zeros((heads_here, query_count, head_size), jnp.float32),
    )


def finish(running):
    return (running[2] / running[1][..., None]).astype(jnp.bfloat16)


def on_device(volume, conv_in, conv_out, norm_gain, q_weight, kv_weight, out_weight, up_weight):
    extent_x, extent_y, extent_z, channels = volume.shape
    encoded = jax.nn.relu(convolve(pad_brick(volume), conv_in)).astype(jnp.bfloat16)
    tokens = tokenize(encoded.astype(jnp.float32))
    normed = layer_norm(tokens, norm_gain)
    queries = jnp.dot(normed, q_weight, preferred_element_type=jnp.float32).astype(jnp.bfloat16)
    key_value = jnp.dot(normed, kv_weight, preferred_element_type=jnp.float32).astype(jnp.bfloat16)
    token_count, width = tokens.shape
    head_size = width // HEADS
    packed = (
        jnp.concatenate([queries, key_value], axis=1)
        .reshape(token_count, 3, HEADS, head_size)
        .transpose(1, 2, 0, 3)
    )
    arranged = lax.all_to_all(packed, "gz", split_axis=1, concat_axis=2, tiled=True)
    head_queries = arranged[0]
    running = make_folder(
        head_queries,
        start_state(head_queries),
        lax.all_gather(arranged[1:], ("gx", "gy"), axis=2, tiled=True),
    )
    returned = lax.all_to_all(finish(running), "gz", split_axis=1, concat_axis=0, tiled=True)
    attended = returned.transpose(1, 0, 2).reshape(token_count, width)
    mixture = (tokens + jnp.dot(attended, out_weight, preferred_element_type=jnp.float32)).astype(
        jnp.bfloat16
    )
    upward = jnp.dot(mixture, up_weight, preferred_element_type=jnp.float32)
    joined = (
        encoded.astype(jnp.float32) + spread_cells(upward, extent_x, extent_y, extent_z)
    ).astype(jnp.bfloat16)
    return convolve(pad_brick(joined), conv_out).astype(jnp.bfloat16)


def solution(mesh):
    placed = (P("gx", "gy", "gz", None), P(), P(), P(), P(), P(), P(), P())
    return jax.shard_map(
        on_device, mesh=mesh, in_specs=placed, out_specs=P("gx", "gy", "gz", None), check_vma=False
    )
```

profile of v0, /device:TPU:0, one launch (start us, length us, event | category | flops | bytes accessed | tf_op | source)
XLA Modules:
  0.0 124.4 jit_solution(1911006101393436707)
XLA Ops:
  0.0 2.0 %copy.101 = bf16[8,32,16,32]{1,3,2,0:T(8,128)(2,1)S(1)} copy(bf16[8,32,16,32]{3,2,1,0:T(8,128)(2,1)} %param.8) | data formatting | bytes 524288 | tf_op args[0]
  2.0 4.9 %collective-permute-start = (bf16[1,32,16,32]{1,3,2,0:T(8,128)(2,1)S(1)}, bf16[1,32,16,32]{1,3,2,0:T(8,128)(2,1)S(1)}, u32[]{:S(2)}, u32[]{:S(2)}) collective-permute-start(bf16[1,32,16,32]{1,3,2,0:T(8,128)(2,1)S(1)} %get-tuple-element.36), channel_id=1, source_target_pairs={{0,8},{8,16},{16,24},{1,9},{9,17},{17,25},{2,10},{10,18},{18,26},{... | collective-permute-start | bytes 98312 | tf_op jit(solution)/shard_map/ppermute | solution.py:19
  9.6 4.8 %collective-permute-done.1 = bf16[1,32,16,32]{1,3,2,0:T(8,128)(2,1)S(1)} collective-permute-done((bf16[1,32,16,32]{1,3,2,0:T(8,128)(2,1)S(1)}, bf16[1,32,16,32]{1,3,2,0:T(8,128)(2,1)S(1)}, u32[]{:S(2)}, u32[]{:S(2)}) %collective-permute-start.1) | collective-permute-done | bytes 32800 | tf_op jit(solution)/shard_map/ppermute | solution.py:21
  16.4 2.3 %copy.104 = bf16[10,1,16,32]{3,2,1,0:T(8,128)(2,1)S(1)} copy(bf16[10,1,16,32]{1,3,2,0:T(8,128)(2,1)} %get-tuple-element.32) | data formatting | bytes 20480 | tf_op jit(solution)/shard_map/slice | solution.py:16
  24.1 2.1 %copy.107 = bf16[10,1,16,32]{1,3,2,0:T(8,128)(2,1)} copy(bf16[10,1,16,32]{3,2,1,0:T(8,128)(2,1)S(1)} %collective-permute-done.3) | data formatting | bytes 20480 | tf_op jit(solution)/shard_map/ppermute | solution.py:21
  27.4 3.5 %collective-permute-start.4 = (bf16[10,34,1,32]{1,3,2,0:T(8,128)(2,1)S(1)}, bf16[10,34,1,32]{1,3,2,0:T(8,128)(2,1)S(1)}, u32[]{:S(2)}, u32[]{:S(2)}) collective-permute-start(bf16[10,34,1,32]{1,3,2,0:T(8,128)(2,1)S(1)} %get-tuple-element.17), channel_id=1, source_target_pairs={{0,1},{1,2},{2,3},{4,5},{5,6},{6,7},{8,9},{9,10},{10,11},{12,13},{... | collective-permute-start | bytes 65288 | tf_op jit(solution)/shard_map/ppermute | solution.py:19
  33.1 4.1 %collective-permute-done.5 = bf16[10,34,1,32]{1,3,2,0:T(8,128)(2,1)S(1)} collective-permute-done((bf16[10,34,1,32]{1,3,2,0:T(8,128)(2,1)S(1)}, bf16[10,34,1,32]{1,3,2,0:T(8,128)(2,1)S(1)}, u32[]{:S(2)}, u32[]{:S(2)}) %collective-permute-start.5) | collective-permute-done | bytes 21792 | tf_op jit(solution)/shard_map/ppermute | solution.py:21
  38.9 3.1 %copy.109 = bf16[10,34,1,8,3,32]{5,3,4,1,0,2:T(8,128)(2,1)} copy(bf16[10,34,1,8,3,32]{1,5,4,3,2,0:T(8,128)(2,1)S(1)} %bitcast.88) | data formatting | bytes 1044480 | tf_op jit(solution)/shard_map/conv_general_dilated | solution.py:29
  42.0 1.9 %slice.79 = bf16[10,34,1,7,2,32]{5,3,4,1,0,2:T(8,128)(2,1)S(1)} slice(bf16[10,34,1,8,3,32]{5,3,4,1,0,2:T(8,128)(2,1)} %copy.109), slice={[0:10], [0:34], [0:1], [1:8], [0:2], [0:32]} | slice | bytes 609280 | tf_op jit(solution)/shard_map/conv_general_dilated | solution.py:29
  44.0 4.4 %maximum_convert_fusion = bf16[8,32,8,3,32]{4,2,3,1,0:T(8,128)(2,1)S(1)} fusion(pred[8,3]{0,1:T(4,128)(4,1)S(1)} %copy-done.10, bf16[3,3,3,32,32]{4,3,2,1,0:T(8,128)(2,1)S(1)} %copy-done.6, bf16[10,34,1,7,2,32]{5,3,4,1,0,2:T(8,128)(2,1)S(1)} %slice.79, bf16[10,34,1,8,3,32]{5,3,4,1,0,2:T(8,128)(2,1)S(1)} %copy-done.3), kind=kOutput, calls=%fused_computation.16 | convolution fusion | flops 342939648 | bytes 1275416 | tf_op jit(solution)/shard_map/conv_general_dilated | solution.py:29
  50.3 2.2 %reduce_sum.37 = f32[2,4,2,2,2,32]{5,2,1,4,3,0:T(2,128)S(1)} reduce(f32[2,4,4,2,4,2,2,4,32]{8,4,3,2,7,6,5,1,0:T(4,128)} %bitcast.85, f32[]{:T(128)} %constant.12.clone.1), dimensions={1,4,7}, to_apply=%region_0.1 | reduce | flops 129024 | bytes 532484 | tf_op jit(solution)/shard_map/reduce_sum | solution.py:47
  54.0 9.3 %all_to_all.33 = bf16[4,2,768]{2,1,0:T(2,128)(2,1)S(1)} all-to-all(bf16[4,2,768]{2,1,0:T(2,128)(2,1)S(1)} %reshape.145), channel_id=1, replica_groups=mesh['gx'=4,'gy'=2,'gz'=4] {'gz'}, dimensions={0} | all-to-all | bytes 24576 | tf_op jit(solution)/shard_map/all_to_all | solution.py:125
  63.5 9.6 %all_gather.3 = bf16[2,2,256,32]{3,1,0,2:T(2,128)(2,1)S(1)} all-gather(bf16[2,2,32,32]{3,1,0,2:T(2,128)(2,1)S(1)} %copy.118), channel_id=1, replica_groups=mesh['gx'=4,'gy'=2,'gz'=4] {'gx','gy'}, dimensions={2}, use_global_device_ids=true | all-gather | bytes 73728 | tf_op jit(solution)/shard_map/all_gather | solution.py:130
  74.1 7.9 %all_to_all.34 = bf16[4,2,256]{2,1,0:T(2,128)(2,1)S(1)} all-to-all(bf16[4,2,256]{2,1,0:T(2,128)(2,1)S(1)} %reshape.147), channel_id=1, replica_groups=mesh['gx'=4,'gy'=2,'gz'=4] {'gz'}, dimensions={0} | all-to-all | bytes 8192 | tf_op jit(solution)/shard_map/all_to_all | solution.py:132
  83.5 2.2 %collective-permute-start.6 = (bf16[1,32,16,32]{3,1,2,0:T(8,128)(2,1)S(1)}, bf16[1,32,16,32]{3,1,2,0:T(8,128)(2,1)S(1)}, u32[]{:S(2)}, u32[]{:S(2)}) collective-permute-start(bf16[1,32,16,32]{3,1,2,0:T(8,128)(2,1)S(1)} %get-tuple-element.34), channel_id=1, source_target_pairs={{0,8},{8,16},{16,24},{1,9},{9,17},{17,25},{2,10},{10,18},{18,26},{... | collective-permute-start | bytes 98312 | tf_op jit(solution)/shard_map/ppermute | solution.py:19
  88.2 4.7 %collective-permute-done.7 = bf16[1,32,16,32]{3,1,2,0:T(8,128)(2,1)S(1)} collective-permute-done((bf16[1,32,16,32]{3,1,2,0:T(8,128)(2,1)S(1)}, bf16[1,32,16,32]{3,1,2,0:T(8,128)(2,1)S(1)}, u32[]{:S(2)}, u32[]{:S(2)}) %collective-permute-start.7) | collective-permute-done | bytes 32800 | tf_op jit(solution)/shard_map/ppermute | solution.py:21
  95.7 1.9 %collective-permute-done.9 = bf16[10,1,16,32]{3,1,2,0:T(2,128)(2,1)S(1)} collective-permute-done((bf16[10,1,16,32]{3,1,2,0:T(2,128)(2,1)S(1)}, bf16[10,1,16,32]{3,1,2,0:T(2,128)(2,1)S(1)}, u32[]{:S(2)}, u32[]{:S(2)}) %collective-permute-start.9) | collective-permute-done | bytes 10272 | tf_op jit(solution)/shard_map/ppermute | solution.py:21
  97.6 2.5 %collective-permute-start.10 = (bf16[10,34,1,32]{3,1,2,0:T(8,128)(2,1)S(1)}, bf16[10,34,1,32]{3,1,2,0:T(8,128)(2,1)S(1)}, u32[]{:S(2)}, u32[]{:S(2)}) collective-permute-start(bf16[10,34,1,32]{3,1,2,0:T(8,128)(2,1)S(1)} %get-tuple-element.19), channel_id=1, source_target_pairs={{0,1},{1,2},{2,3},{4,5},{5,6},{6,7},{8,9},{9,10},{10,11},{12,13},{... | collective-permute-start | bytes 65288 | tf_op jit(solution)/shard_map/ppermute | solution.py:19
  102.6 4.1 %collective-permute-done.11 = bf16[10,34,1,32]{3,1,2,0:T(8,128)(2,1)S(1)} collective-permute-done((bf16[10,34,1,32]{3,1,2,0:T(8,128)(2,1)S(1)}, bf16[10,34,1,32]{3,1,2,0:T(8,128)(2,1)S(1)}, u32[]{:S(2)}, u32[]{:S(2)}) %collective-permute-start.11) | collective-permute-done | bytes 21792 | tf_op jit(solution)/shard_map/ppermute | solution.py:21
  106.7 2.1 %maximum_bitcast_fusion = bf16[10,34,1,18,32]{4,1,3,0,2:T(8,128)(2,1)S(1)} fusion(bf16[10,34,1,32]{3,1,2,0:T(8,128)(2,1)S(1)} %collective-permute-done.11, bf16[10,1,16,32]{3,1,2,0:T(2,128)(2,1)S(1)} %collective-permute-done.9, bf16[1,32,16,32]{3,1,2,0:T(8,128)(2,1)S(1)} %collective-permute-done.7, bf16[8,32,16,32]{3,1,2,0:T(8,128)(2,1)S(1)} %fusion.16, ...), kind=kLoop, calls=%fused_computation.19 | loop fusion | flops 2741760 | bytes 783360 | tf_op jit(solution)/shard_map/broadcast_in_dim | solution.py:30
  108.8 2.6 %copy.133 = bf16[10,34,1,18,32]{1,4,3,2,0:T(8,128)(2,1)} copy(bf16[10,34,1,18,32]{4,1,3,0,2:T(8,128)(2,1)S(1)} %maximum_bitcast_fusion) | data formatting | bytes 783360
  113.1 3.1 %copy.128 = bf16[10,34,1,8,3,32]{5,3,4,1,0,2:T(8,128)(2,1)} copy(bf16[10,34,1,8,3,32]{1,5,4,3,2,0:T(8,128)(2,1)S(1)} %bitcast.87) | data formatting | bytes 1044480 | tf_op jit(solution)/shard_map/conv_general_dilated | solution.py:29
  116.3 1.9 %slice.87 = bf16[10,34,1,7,2,32]{5,3,4,1,0,2:T(8,128)(2,1)S(1)} slice(bf16[10,34,1,8,3,32]{5,3,4,1,0,2:T(8,128)(2,1)} %copy.128), slice={[0:10], [0:34], [0:1], [1:8], [0:2], [0:32]} | slice | bytes 609280 | tf_op jit(solution)/shard_map/conv_general_dilated | solution.py:29
  118.3 4.3 %select_convert_fusion = bf16[8,32,8,3,32]{4,2,3,1,0:T(8,128)(2,1)S(1)} fusion(pred[8,3]{0,1:T(4,128)(4,1)S(1)} %copy-done.10, bf16[3,3,3,32,32]{4,3,2,1,0:T(8,128)(2,1)S(1)} %copy-done.7, bf16[10,34,1,7,2,32]{5,3,4,1,0,2:T(8,128)(2,1)S(1)} %slice.87, bf16[10,34,1,8,3,32]{5,3,4,1,0,2:T(8,128)(2,1)S(1)} %copy-done.2), kind=kOutput, calls=%fused_computation.15 | convolution fusion | flops 342743040 | bytes 1275416 | tf_op jit(solution)/shard_map/conv_general_dilated | solution.py:29
  (95 shorter events, 32.8 us)
Async XLA Ops:
  0.0 53.6 %copy-start = (bf16[256,512]{1,0:T(8,128)(2,1)S(1)}, bf16[256,512]{1,0:T(8,128)(2,1)}, u32[]{:S(2)}) copy-start(bf16[256,512]{1,0:T(8,128)(2,1)} %param.13) | copy-start | bytes 786436
  2.0 7.6 %collective-permute-start = (bf16[1,32,16,32]{1,3,2,0:T(8,128)(2,1)S(1)}, bf16[1,32,16,32]{1,3,2,0:T(8,128)(2,1)S(1)}, u32[]{:S(2)}, u32[]{:S(2)}) collective-permute-start(bf16[1,32,16,32]{1,3,2,0:T(8,128)(2,1)S(1)} %get-tuple-element.36), channel_id=1, source_target_pairs={{0,8},{8,16},{16,24},{1,9},{9,17},{17,25},{2,10},{10,18},{18,26},{... | collective-permute-start | bytes 98312 | tf_op jit(solution)/shard_map/ppermute | solution.py:19
  6.9 7.5 %collective-permute-start.1 = (bf16[1,32,16,32]{1,3,2,0:T(8,128)(2,1)S(1)}, bf16[1,32,16,32]{1,3,2,0:T(8,128)(2,1)S(1)}, u32[]{:S(2)}, u32[]{:S(2)}) collective-permute-start(bf16[1,32,16,32]{1,3,2,0:T(8,128)(2,1)S(1)} %get-tuple-element.37), channel_id=1, source_target_pairs={{8,0},{16,8},{24,16},{9,1},{17,9},{25,17},{10,2},{18,10},{26,18},{... | collective-permute-start | bytes 98312 | tf_op jit(solution)/shard_map/ppermute | solution.py:21
  18.7 3.6 %collective-permute-start.2 = (bf16[10,1,16,32]{3,2,1,0:T(8,128)(2,1)S(1)}, bf16[10,1,16,32]{3,2,1,0:T(8,128)(2,1)S(1)}, u32[]{:S(2)}, u32[]{:S(2)}) collective-permute-start(bf16[10,1,16,32]{3,2,1,0:T(8,128)(2,1)S(1)} %copy.104), channel_id=1, source_target_pairs={{0,4},{1,5},{2,6},{3,7},{8,12},{9,13},{10,14},{11,15},{16,20},{17,... | collective-permute-start | bytes 30728 | tf_op jit(solution)/shard_map/ppermute | solution.py:19
  21.0 3.1 %collective-permute-start.3 = (bf16[10,1,16,32]{3,2,1,0:T(8,128)(2,1)S(1)}, bf16[10,1,16,32]{3,2,1,0:T(8,128)(2,1)S(1)}, u32[]{:S(2)}, u32[]{:S(2)}) collective-permute-start(bf16[10,1,16,32]{3,2,1,0:T(8,128)(2,1)S(1)} %copy.105), channel_id=1, source_target_pairs={{4,0},{5,1},{6,2},{7,3},{12,8},{13,9},{14,10},{15,11},{20,16},{21,... | collective-permute-start | bytes 30728 | tf_op jit(solution)/shard_map/ppermute | solution.py:21
  26.2 11.0 %copy-start.1 = (bf16[10,1,16,32]{1,3,2,0:T(8,128)(2,1)S(1)}, bf16[10,1,16,32]{1,3,2,0:T(8,128)(2,1)}, u32[]{:S(2)}) copy-start(bf16[10,1,16,32]{1,3,2,0:T(8,128)(2,1)} %copy.107) | copy-start | bytes 30724
  27.4 5.7 %collective-permute-start.4 = (bf16[10,34,1,32]{1,3,2,0:T(8,128)(2,1)S(1)}, bf16[10,34,1,32]{1,3,2,0:T(8,128)(2,1)S(1)}, u32[]{:S(2)}, u32[]{:S(2)}) collective-permute-start(bf16[10,34,1,32]{1,3,2,0:T(8,128)(2,1)S(1)} %get-tuple-element.17), channel_id=1, source_target_pairs={{0,1},{1,2},{2,3},{4,5},{5,6},{6,7},{8,9},{9,10},{10,11},{12,13},{... | collective-permute-start | bytes 65288 | tf_op jit(solution)/shard_map/ppermute | solution.py:19
  30.9 6.3 %collective-permute-start.5 = (bf16[10,34,1,32]{1,3,2,0:T(8,128)(2,1)S(1)}, bf16[10,34,1,32]{1,3,2,0:T(8,128)(2,1)S(1)}, u32[]{:S(2)}, u32[]{:S(2)}) collective-permute-start(bf16[10,34,1,32]{1,3,2,0:T(8,128)(2,1)S(1)} %get-tuple-element.18), channel_id=1, source_target_pairs={{1,0},{2,1},{3,2},{5,4},{6,5},{7,6},{9,8},{10,9},{11,10},{13,12},{... | collective-permute-start | bytes 65288 | tf_op jit(solution)/shard_map/ppermute | solution.py:21
  42.0 2.0 %copy-start.3 = (bf16[10,34,1,8,3,32]{5,3,4,1,0,2:T(8,128)(2,1)S(1)}, bf16[10,34,1,8,3,32]{5,3,4,1,0,2:T(8,128)(2,1)}, u32[]{:S(2)}) copy-start(bf16[10,34,1,8,3,32]{5,3,4,1,0,2:T(8,128)(2,1)} %copy.109) | copy-start | bytes 1566724
  42.0 2.0 %copy-start.6 = (bf16[3,3,3,32,32]{4,3,2,1,0:T(8,128)(2,1)S(1)}, bf16[3,3,3,32,32]{4,3,2,1,0:T(8,128)(2,1)}, u32[]{:S(2)}) copy-start(bf16[3,3,3,32,32]{4,3,2,1,0:T(8,128)(2,1)} %param.9) | copy-start | bytes 165892
  42.0 2.0 %copy-start.10 = (pred[8,3]{0,1:T(4,128)(4,1)S(1)}, pred[8,3]{0,1:T(4,128)(4,1)}, u32[]{:S(2)}) copy-start(pred[8,3]{0,1:T(4,128)(4,1)} %constant.42) | copy-start | bytes 76
  48.7 4.7 %copy-start.8 = (bf16[256,256]{1,0:T(8,128)(2,1)S(1)}, bf16[256,256]{1,0:T(8,128)(2,1)}, u32[]{:S(2)}) copy-start(bf16[256,256]{1,0:T(8,128)(2,1)} %param.12) | copy-start | bytes 393220
  48.7 4.7 %copy-start.9 = (f32[256]{0:T(256)S(1)}, f32[256]{0:T(256)}, u32[]{:S(2)}) copy-start(f32[256]{0:T(256)} %param.11) | copy-start | bytes 3076
  50.3 31.9 %copy-start.4 = (bf16[256,256]{1,0:T(8,128)(2,1)S(1)}, bf16[256,256]{1,0:T(8,128)(2,1)}, u32[]{:S(2)}) copy-start(bf16[256,256]{1,0:T(8,128)(2,1)} %param.15) | copy-start | bytes 393220
  50.3 31.9 %copy-start.5 = (bf16[256,256]{1,0:T(8,128)(2,1)S(1)}, bf16[256,256]{1,0:T(8,128)(2,1)}, u32[]{:S(2)}) copy-start(bf16[256,256]{1,0:T(8,128)(2,1)} %param.14) | copy-start | bytes 393220
  83.5 4.7 %collective-permute-start.6 = (bf16[1,32,16,32]{3,1,2,0:T(8,128)(2,1)S(1)}, bf16[1,32,16,32]{3,1,2,0:T(8,128)(2,1)S(1)}, u32[]{:S(2)}, u32[]{:S(2)}) collective-permute-start(bf16[1,32,16,32]{3,1,2,0:T(8,128)(2,1)S(1)} %get-tuple-element.34), channel_id=1, source_target_pairs={{0,8},{8,16},{16,24},{1,9},{9,17},{17,25},{2,10},{10,18},{18,26},{... | collective-permute-start | bytes 98312 | tf_op jit(solution)/shard_map/ppermute | solution.py:19
  85.7 7.2 %collective-permute-start.7 = (bf16[1,32,16,32]{3,1,2,0:T(8,128)(2,1)S(1)}, bf16[1,32,16,32]{3,1,2,0:T(8,128)(2,1)S(1)}, u32[]{:S(2)}, u32[]{:S(2)}) collective-permute-start(bf16[1,32,16,32]{3,1,2,0:T(8,128)(2,1)S(1)} %get-tuple-element.35), channel_id=1, source_target_pairs={{8,0},{16,8},{24,16},{9,1},{17,9},{25,17},{10,2},{18,10},{26,18},{... | collective-permute-start | bytes 98312 | tf_op jit(solution)/shard_map/ppermute | solution.py:21
  93.1 2.6 %collective-permute-start.8 = (bf16[10,1,16,32]{3,1,2,0:T(2,128)(2,1)S(1)}, bf16[10,1,16,32]{3,1,2,0:T(2,128)(2,1)S(1)}, u32[]{:S(2)}, u32[]{:S(2)}) collective-permute-start(bf16[10,1,16,32]{3,1,2,0:T(2,128)(2,1)S(1)} %get-tuple-element.28), channel_id=1, source_target_pairs={{0,4},{1,5},{2,6},{3,7},{8,12},{9,13},{10,14},{11,15},{16,20},{17,... | collective-permute-start | bytes 30728 | tf_op jit(solution)/shard_map/ppermute | solution.py:19
  94.4 3.2 %collective-permute-start.9 = (bf16[10,1,16,32]{3,1,2,0:T(2,128)(2,1)S(1)}, bf16[10,1,16,32]{3,1,2,0:T(2,128)(2,1)S(1)}, u32[]{:S(2)}, u32[]{:S(2)}) collective-permute-start(bf16[10,1,16,32]{3,1,2,0:T(2,128)(2,1)S(1)} %get-tuple-element.30), channel_id=1, source_target_pairs={{4,0},{5,1},{6,2},{7,3},{12,8},{13,9},{14,10},{15,11},{20,16},{21,... | collective-permute-start | bytes 30728 | tf_op jit(solution)/shard_map/ppermute | solution.py:21
  97.6 4.9 %collective-permute-start.10 = (bf16[10,34,1,32]{3,1,2,0:T(8,128)(2,1)S(1)}, bf16[10,34,1,32]{3,1,2,0:T(8,128)(2,1)S(1)}, u32[]{:S(2)}, u32[]{:S(2)}) collective-permute-start(bf16[10,34,1,32]{3,1,2,0:T(8,128)(2,1)S(1)} %get-tuple-element.19), channel_id=1, source_target_pairs={{0,1},{1,2},{2,3},{4,5},{5,6},{6,7},{8,9},{9,10},{10,11},{12,13},{... | collective-permute-start | bytes 65288 | tf_op jit(solution)/shard_map/ppermute | solution.py:19
  100.1 6.6 %collective-permute-start.11 = (bf16[10,34,1,32]{3,1,2,0:T(8,128)(2,1)S(1)}, bf16[10,34,1,32]{3,1,2,0:T(8,128)(2,1)S(1)}, u32[]{:S(2)}, u32[]{:S(2)}) collective-permute-start(bf16[10,34,1,32]{3,1,2,0:T(8,128)(2,1)S(1)} %get-tuple-element.20), channel_id=1, source_target_pairs={{1,0},{2,1},{3,2},{5,4},{6,5},{7,6},{9,8},{10,9},{11,10},{13,12},{... | collective-permute-start | bytes 65288 | tf_op jit(solution)/shard_map/ppermute | solution.py:21
  116.3 2.0 %copy-start.2 = (bf16[10,34,1,8,3,32]{5,3,4,1,0,2:T(8,128)(2,1)S(1)}, bf16[10,34,1,8,3,32]{5,3,4,1,0,2:T(8,128)(2,1)}, u32[]{:S(2)}) copy-start(bf16[10,34,1,8,3,32]{5,3,4,1,0,2:T(8,128)(2,1)} %copy.128) | copy-start | bytes 1566724
  116.3 2.0 %copy-start.7 = (bf16[3,3,3,32,32]{4,3,2,1,0:T(8,128)(2,1)S(1)}, bf16[3,3,3,32,32]{4,3,2,1,0:T(8,128)(2,1)}, u32[]{:S(2)}) copy-start(bf16[3,3,3,32,32]{4,3,2,1,0:T(8,128)(2,1)} %param.10) | copy-start | bytes 165892
where the time goes:
time: 125 us; the launch traced here: 124 us
  local copies, waits for them, and re-layouts  29.4 us (24%)
  blocking collectives  26.7 us (21%)
  waiting for transfers between devices  24.6 us (20%)
  starting transfers between devices  23.8 us (19%)
  matrix products  9.77 us (8%)
  other arithmetic  9.75 us (8%)
    ppermute x6, waiting for transfers between devices, with_halo(): lax.ppermute(head, axis, [((i + 1) % count, i) for i in range(ends)])  20.3 us
    ppermute x6, starting transfers between devices, with_halo(): lax.ppermute(tail, axis, [(i, (i + 1) % count) for i in range(ends)])  15.6 us
    conv_general_dilated x4, local copies, waits for them, and re-layouts, convolve(): lax.conv_general_dilated(padded[None], kernel, (1, 1, 1), 'VALID', dimens...  9.95 us
    all_gather x1, blocking collectives, on_device(): lax.all_gather(arranged[1:], ('gx', 'gy'), axis=2, tiled=True)  9.56 us
    all_to_all x1, blocking collectives, on_device(): lax.all_to_all(packed, 'gz', split_axis=1, concat_axis=2, tiled=True)  9.26 us
    conv_general_dilated x2, matrix products, convolve(): lax.conv_general_dilated(padded[None], kernel, (1, 1, 1), 'VALID', dimens...  8.72 us
    ppermute x6, starting transfers between devices, with_halo(): lax.ppermute(head, axis, [((i + 1) % count, i) for i in range(ends)])  8.15 us
    all_to_all x1, blocking collectives, on_device(): lax.all_to_all(finish(running), 'gz', split_axis=1, concat_axis=0, tiled=...  7.91 us
  transfers between devices with their start and end apart: 12, of which 10 were waited for; matrix products, arithmetic and copies ran while one was open for 2% of the time, Pallas kernels for 0%

commit v1 on v0

v1 whole, which is shorter than its diff:
```python
import numpy as np

import jax
import jax.numpy as jnp
from jax import lax
from jax.experimental import pallas as pl
from jax.experimental.pallas import tpu as pltpu
from jax.sharding import PartitionSpec as P

HEADS = 8
AXES = ("gx", "gy", "gz")
OUT_Z = 6
IN_Z = 8

f32 = jnp.float32
bf16 = jnp.bfloat16


def exchange(low, high, axis):
    count = lax.axis_size(axis)
    if count == 1:
        return low, low
    if count == 2:
        mine = jnp.where(lax.axis_index(axis) == 0, high, low)
        other = lax.ppermute(mine, axis, [(0, 1), (1, 0)])
        return other, other
    below = lax.ppermute(high, axis, [(i, (i + 1) % count) for i in range(count)])
    above = lax.ppermute(low, axis, [((i + 1) % count, i) for i in range(count)])
    return below, above


def call(body, outs, scratch=(), in_smem=0, total=0):
    specs = [pl.BlockSpec(memory_space=pltpu.SMEM)] * in_smem + [
        pl.BlockSpec(memory_space=pltpu.VMEM)
    ] * (total - in_smem)
    return pl.pallas_call(
        body,
        out_shape=outs,
        in_specs=specs,
        scratch_shapes=list(scratch),
        name=body.__name__,
    )


def band_weights(kernel_in, kernel_out, up_weight, chan):
    width = up_weight.shape[0]

    def spread_weights(kin, kout, up, first, second, upx):
        for source, target in ((kin, first), (kout, second)):
            target[...] = jnp.zeros(target.shape, target.dtype)
            for tap in range(9):
                block = source[tap]
                for z in range(OUT_Z):
                    target[tap, z * chan : (z + 3) * chan, z * chan : (z + 1) * chan] = block
        for a in range(2):
            pieces = []
            for b in range(2):
                for c in range(2):
                    start = (a * 4 + b * 2 + c) * chan
                    pieces += [up[:, start : start + chan]] * 4
            upx[a] = jnp.concatenate(pieces, axis=1)

    banded = jax.ShapeDtypeStruct((9, IN_Z * chan, OUT_Z * chan), bf16)
    return call(
        spread_weights,
        (banded, banded, jax.ShapeDtypeStruct((2, width, 16 * chan), bf16)),
        total=3,
    )(
        kernel_in.reshape(9, 3 * chan, chan),
        kernel_out.reshape(9, 3 * chan, chan),
        up_weight,
    )


def pack_rows(volume, below, above):
    bx, by, bz, chan = volume.shape
    lanes = (bz + 4) * chan

    def pack(vol, zm, zp, rows, ylow, yhigh):
        own = vol[...].reshape(bx * by, bz * chan)
        full = jnp.concatenate([zm[...], own, zp[...]], axis=1)
        rows[...] = full
        planes = full.astype(f32).reshape(bx, by, lanes)
        ylow[...] = planes[:, :2].reshape(bx * 2, lanes).astype(bf16)
        yhigh[...] = planes[:, by - 2 :].reshape(bx * 2, lanes).astype(bf16)

    face = jax.ShapeDtypeStruct((bx * 2, lanes), bf16)
    return call(
        pack, (jax.ShapeDtypeStruct((bx * by, lanes), bf16), face, face), total=3
    )(volume, below, above)


def banded_conv(source, weights, sums, blocks, rows, stride, chan):
    outs = []
    for block in range(blocks):
        start = block * OUT_Z * chan
        for dy in range(3):
            total = None
            for dx in range(3):
                piece = source[dx * stride : dx * stride + rows, start : start + IN_Z * chan]
                part = jnp.dot(
                    piece.astype(bf16), weights[dx * 3 + dy], preferred_element_type=f32
                )
                total = part if total is None else total + part
            sums[dy, :rows, :] = total
        outs.append(sums[0, 0:rows, :] + sums[1, 1 : rows + 1, :] + sums[2, 2 : rows + 2, :])
    return outs


def encode(pos, rows_z, yfaces, xbelow, xabove, weights, shape, counts):
    bx, by, bz, chan = shape
    nx, ny, nz = counts
    lanes = (bz + 4) * chan
    stride = by + 8
    tall = (bx + 2) * stride
    blocks = (bz + 2) // OUT_Z
    ti, tj, tk = bx // 8, by // 8, bz // 8
    tokens = ti * tj * tk
    width = 8 * chan
    yparts = len(yfaces)

    def encode_rows(pos_ref, vz, *refs):
        yrefs = refs[:yparts]
        xm, xp, w, enc, tok, grid, sums, plane_sum = refs[yparts:]
        lane = lax.broadcasted_iota(jnp.int32, (1, lanes), 1)
        z_ok = ((lane >= 2 * chan) | (pos_ref[2] > 0)) & (
            (lane < (bz + 2) * chan) | (pos_ref[2] < nz - 1)
        )
        y_lo, y_hi = pos_ref[1] > 0, pos_ref[1] < ny - 1
        x_lo, x_hi = pos_ref[0] > 0, pos_ref[0] < nx - 1

        def put(row, value, ok=None):
            good = z_ok if ok is None else z_ok & ok
            grid[row : row + value.shape[0], :] = jnp.where(good, value.astype(f32), 0.0)

        for p in range(bx):
            base = (p + 2) * stride
            put(base + 2, vz[p * by : (p + 1) * by, :])
            ym = yrefs[0][...].astype(f32)[2 * p : 2 * p + 2]
            yp = yrefs[-1][...].astype(f32)[2 * p : 2 * p + 2]
            put(base, ym, y_lo)
            put(base + by + 2, yp, y_hi)
        for ref, first, ok in ((xm, 0, x_lo), (xp, bx + 2, x_hi)):
            tail = ref[2 * by :, :].astype(f32)
            for q in range(2):
                base = (first + q) * stride
                put(base + 2, ref[q * by : (q + 1) * by, :], ok)
                put(base, tail[2 * q : 2 * q + 2], ok & y_lo)
                last = 4 * (yparts - 1) + 2 * q
                put(base + by + 2, tail[last : last + 2], ok & y_hi)
        outs = banded_conv(grid, w, sums, blocks, tall, stride, chan)
        encoded = jnp.maximum(jnp.concatenate(outs, axis=1), 0.0).astype(bf16)
        enc[...] = encoded
        cells = encoded.astype(f32)
        rows_of = {}
        for i in range(ti):
            features = {}
            for a in range(2):
                x0 = 1 + 8 * i + 4 * a
                acc = cells[x0 * stride : (x0 + 1) * stride]
                for q in range(1, 4):
                    acc = acc + cells[(x0 + q) * stride : (x0 + q + 1) * stride]
                for g in range(2 * tk):
                    at = (1 + 4 * g) * chan
                    plane_sum[g] = acc[:, at : at + 4 * chan]
                for b in range(2):
                    for g in range(2 * tk):
                        part = None
                        for q in range(4):
                            line = plane_sum[g, pl.ds(1 + 4 * b + q, tj, stride=8), :]
                            part = line if part is None else part + line
                        s = part[:, :chan]
                        for q in range(1, 4):
                            s = s + part[:, q * chan : (q + 1) * chan]
                        features[a, b, g] = s * (1.0 / 64.0)
            for k in range(tk):
                rows_of[i, k] = jnp.concatenate(
                    [features[a, b, 2 * k + c] for a in range(2) for b in range(2) for c in range(2)],
                    axis=1,
                )
        tok[...] = jnp.concatenate(
            [rows_of[i, k] for i in range(ti) for k in range(tk)], axis=0
        ).astype(tok.dtype)

    return call(
        encode_rows,
        (
            jax.ShapeDtypeStruct((tall, (bz + 2) * chan), bf16),
            jax.ShapeDtypeStruct((tokens, width), f32),
        ),
        scratch=[
            pltpu.VMEM(((bx + 4) * stride, lanes), f32),
            pltpu.VMEM((3, tall + 8, OUT_Z * chan), f32),
            pltpu.VMEM((2 * tk, stride, 4 * chan), f32),
        ],
        in_smem=1,
        total=5 + yparts,
    )(pos, rows_z, *yfaces, xbelow, xabove, weights)


def sub_blocks(extent):
    out = [(0, 1, -1, extent // 8 - 1, 1)]
    for s in range(extent // 4):
        out.append((1 + 4 * s, 4, 0, s // 2, s % 2))
    out.append((extent + 1, 1, 1, 0, 0))
    return out


def attend_and_join(
    pos, gathered, gain, q_weight, kv_weight, out_weight, upx, encoded, weights, shape, counts
):
    bx, by, bz, chan = shape
    nx, ny, nz = counts
    stride = by + 8
    tall, low = (bx + 2) * stride, bx * stride
    ti, tj, tk = bx // 8, by // 8, bz // 8
    tokens = ti * tj * tk
    width = 8 * chan
    every = gathered.shape[0]
    asked = 27 * tokens
    head_size = width // HEADS
    wide = (bz + 2) * chan
    blocks = -(-bz // OUT_Z)
    padded = (blocks * OUT_Z + 2) * chan

    xs = sub_blocks(bx)
    zs = [(-1, tk - 1, (7 * chan, 8 * chan))]
    zs += [(0, k, (0, 8 * chan)) for k in range(tk)]
    zs += [(1, 0, (0, chan))]
    pick = np.zeros((len(xs) * len(zs) * stride, asked), np.float32)
    for xi, (_, _, dx, i, _) in enumerate(xs):
        for zi, (dz, k, _) in enumerate(zs):
            for first, many, dy, j, _ in sub_blocks(by):
                near = ((dx + 1) * 3 + dy + 1) * 3 + dz + 1
                row = (xi * len(zs) + zi) * stride + first
                pick[row : row + many, near * tokens + (i * tk + k) * tj + j] = 1.0

    def attend(
        pos_ref, g, gain_ref, qw, kvw, ow, upx_ref, sel, enc, w, out, normed_all, mine, mine_n, grid, sums
    ):
        t = g[...].astype(f32)
        center = t - jnp.mean(t, axis=1, keepdims=True)
        spread = jnp.mean(center * center, axis=1, keepdims=True)
        normed = (center * lax.rsqrt(spread + 1e-05) * gain_ref[...]).astype(bf16)
        normed_all[...] = normed.astype(f32)
        kv = jnp.dot(normed, kvw[...], preferred_element_type=f32).astype(bf16)
        keys, values = kv[:, :width], kv[:, width:]
        near = 0
        for dx in (-1, 0, 1):
            x = jnp.clip(pos_ref[0] + dx, 0, nx - 1)
            for dy in (-1, 0, 1):
                y = jnp.clip(pos_ref[1] + dy, 0, ny - 1)
                for dz in (-1, 0, 1):
                    z = jnp.clip(pos_ref[2] + dz, 0, nz - 1)
                    at = pl.multiple_of(((x * ny + y) * nz + z) * tokens, 8)
                    mine[near * tokens : (near + 1) * tokens, :] = g[pl.ds(at, tokens), :]
                    mine_n[near * tokens : (near + 1) * tokens, :] = normed_all[pl.ds(at, tokens), :]
                    near += 1
        q = jnp.dot(mine_n[...].astype(bf16), qw[...], preferred_element_type=f32).astype(bf16)
        lane = lax.broadcasted_iota(jnp.int32, (1, width), 1) // head_size
        attended = jnp.zeros((asked, width), f32)
        for h in range(HEADS):
            here = lane == h
            q_h = jnp.where(here, q, jnp.zeros_like(q))
            scores = (
                lax.dot_general(q_h, keys, (((1,), (1,)), ((), ())), preferred_element_type=f32)
                * head_size ** (-0.5)
            )
            e = jnp.exp(scores - jnp.max(scores, axis=1, keepdims=True))
            total = jnp.sum(e, axis=1, keepdims=True)
            num = jnp.dot(e.astype(bf16), values, preferred_element_type=f32)
            attended = jnp.where(here, num / total, attended)
        mixture = (
            mine[...] + jnp.dot(attended.astype(bf16), ow[...], preferred_element_type=f32)
        ).astype(bf16)
        picked = jnp.dot(sel[...], mixture, preferred_element_type=f32).astype(bf16)

        row = lax.broadcasted_iota(jnp.int32, (stride, 1), 0)
        second_half = ((row + 3) // 4) % 2 == 0
        y_ok = ((row > 0) | (pos_ref[1] > 0)) & ((row < by + 1) | (pos_ref[1] < ny - 1))
        zl = lax.broadcasted_iota(jnp.int32, (1, wide), 1)
        z_ok = ((zl >= chan) | (pos_ref[2] > 0)) & ((zl < (bz + 1) * chan) | (pos_ref[2] < nz - 1))
        ok = y_ok & z_ok
        x_lo, x_hi = pos_ref[0] > 0, pos_ref[0] < nx - 1
        if padded > wide:
            grid[:, wide:] = jnp.zeros((tall, padded - wide), f32)
        step = len(zs) * stride
        for xi, (first, many, _, _, a) in enumerate(xs):
            raised = jnp.dot(
                picked[xi * step : (xi + 1) * step], upx_ref[a], preferred_element_type=f32
            )
            parts = []
            for zi, (_, _, (l0, l1)) in enumerate(zs):
                block = raised[zi * stride : (zi + 1) * stride]
                half = block.shape[1] // 2
                chosen = jnp.where(second_half, block[:, half:], block[:, :half])
                parts.append(chosen[:, l0:l1])
            upward = jnp.concatenate(parts, axis=1)
            for x in range(first, first + many):
                good = ok
                if x == 0:
                    good = ok & x_lo
                if x == bx + 1:
                    good = ok & x_hi
                cells = enc[x * stride : (x + 1) * stride, :].astype(f32)
                grid[x * stride : (x + 1) * stride, :wide] = jnp.where(good, cells + upward, 0.0)
        outs = banded_conv(grid, w, sums, blocks, low, stride, chan)
        final = jnp.concatenate(outs, axis=1)[:, : bz * chan].astype(bf16)
        for x in range(bx):
            out[x] = final[x * stride : x * stride + by].reshape(by, bz, chan)

    return call(
        attend,
        jax.ShapeDtypeStruct(shape, bf16),
        scratch=[
            pltpu.VMEM((every, width), f32),
            pltpu.VMEM((asked, width), f32),
            pltpu.VMEM((asked, width), f32),
            pltpu.VMEM((tall, padded), f32),
            pltpu.VMEM((3, low + 8, OUT_Z * chan), f32),
        ],
        in_smem=1,
        total=10,
    )(
        pos, gathered, gain, q_weight, kv_weight, out_weight, upx, jnp.asarray(pick, bf16), encoded, weights
    )


def on_device(volume, conv_in, conv_out, norm_gain, q_weight, kv_weight, out_weight, up_weight):
    shape = volume.shape
    bx, by, bz, chan = shape
    counts = tuple(lax.axis_size(axis) for axis in AXES)
    pos = jnp.stack([lax.axis_index(axis) for axis in AXES]).astype(jnp.int32)
    first_w, second_w, upx = band_weights(conv_in, conv_out, up_weight, chan)

    z_below, z_above = exchange(
        volume[:, :, :2].reshape(bx * by, 2 * chan),
        volume[:, :, bz - 2 :].reshape(bx * by, 2 * chan),
        "gz",
    )
    rows, y_low, y_high = pack_rows(volume, z_below, z_above)
    y_below, y_above = exchange(y_low, y_high, "gy")
    yfaces = [y_below] if counts[1] <= 2 else [y_below, y_above]
    x_below, x_above = exchange(
        jnp.concatenate([rows[: 2 * by]] + [face[:4] for face in yfaces], axis=0),
        jnp.concatenate([rows[(bx - 2) * by :]] + [face[(bx - 2) * 2 :] for face in yfaces], axis=0),
        "gx",
    )
    encoded, tokens = encode(pos, rows, yfaces, x_below, x_above, first_w, shape, counts)

    devices = counts[0] * counts[1] * counts[2]
    copies = jnp.broadcast_to(tokens[None], (devices,) + tokens.shape)
    gathered = lax.all_to_all(copies, AXES, 0, 0, tiled=True).reshape(-1, tokens.shape[1])
    return attend_and_join(
        pos, gathered, norm_gain[None], q_weight, kv_weight, out_weight, upx, encoded, second_w, shape, counts
    )


def solution(mesh):
    placed = (P("gx", "gy", "gz", None), P(), P(), P(), P(), P(), P(), P())
    return jax.shard_map(
        on_device, mesh=mesh, in_specs=placed, out_specs=P("gx", "gy", "gz", None), check_vma=False
    )
```

time: 125 us -> 50 us (0.40)
  local copies, waits for them, and re-layouts: 29.4 us -> 5.2 us
  waiting for transfers between devices: 24.6 us -> 4.58 us
  Pallas kernels: 0 us -> 16.4 us
  starting transfers between devices: 23.8 us -> 8.23 us
  blocking collectives: 26.7 us -> 13.7 us
  matrix products: 9.77 us -> 0 us
  other arithmetic: 9.75 us -> 1.42 us
    ppermute x12 -> x5, waiting for transfers between devices: 24.6 us -> 4.58 us  [the longest x2 2.57 us: exchange(): lax.ppermute(high, axis, [(i, (i + 1) % count) for i in range(count)])]
    pallas_call x0 -> x4, Pallas kernels: none -> 16.4 us  [the longest x1 6.45 us: attend_and_join(): call(attend, jax.ShapeDtypeStruct(shape, bf16), scratch=[pltpu.VMEM((ever...]
    ppermute x12 -> x5, starting transfers between devices: 23.8 us -> 8.23 us  [the longest x2 4.86 us: exchange(): lax.ppermute(high, axis, [(i, (i + 1) % count) for i in range(count)])]
    conv_general_dilated x4 -> x0, local copies, waits for them, and re-layouts: 9.95 us -> none  [convolve(): lax.conv_general_dilated(padded[None], kernel, (1, 1, 1), 'VALID', dimens...]
    all_gather x1 -> x0, blocking collectives: 9.56 us -> none  [on_device(): lax.all_gather(arranged[1:], ('gx', 'gy'), axis=2, tiled=True)]
    conv_general_dilated x2 -> x0, matrix products: 8.72 us -> none  [convolve(): lax.conv_general_dilated(padded[None], kernel, (1, 1, 1), 'VALID', dimens...]
    unnamed x30 -> x10, local copies, waits for them, and re-layouts: 5.44 us -> 1.87 us
    all_to_all x2 -> x1, blocking collectives: 17.2 us -> 13.7 us  [on_device(): lax.all_to_all(copies, AXES, 0, 0, tiled=True).reshape(-1, tokens.shape[1])]
  transfers between devices with their start and end apart: 12 -> 5, of which waited for: 10 -> 3; matrix products, arithmetic and copies ran while one was open for 2% -> 3% of each run, Pallas kernels for 0% -> 6%
where the time goes in v1:
time: 50 us; the launch traced here: 49.6 us
  Pallas kernels  16.4 us (33%)
  blocking collectives  13.7 us (27%)
  starting transfers between devices  8.23 us (16%)
  local copies, waits for them, and re-layouts  5.2 us (10%)
  waiting for transfers between devices  4.58 us (9%)
  other arithmetic  1.42 us (3%)
    all_to_all x1, blocking collectives, on_device(): lax.all_to_all(copies, AXES, 0, 0, tiled=True).reshape(-1, tokens.shape[1])  13.7 us
    pallas_call x1, Pallas kernels, attend_and_join(): call(attend, jax.ShapeDtypeStruct(shape, bf16), scratch=[pltpu.VMEM((ever...  6.45 us
    ppermute x2, starting transfers between devices, exchange(): lax.ppermute(high, axis, [(i, (i + 1) % count) for i in range(count)])  4.86 us
    pallas_call x1, Pallas kernels, encode(): call(encode_rows, (jax.ShapeDtypeStruct((tall, (bz + 2) * chan), bf16), j...  4.25 us
    ppermute x2, starting transfers between devices, exchange(): lax.ppermute(low, axis, [((i + 1) % count, i) for i in range(count)])  3.37 us
    pallas_call x1, Pallas kernels, band_weights(): call(spread_weights, (banded, banded, jax.ShapeDtypeStruct((2, width, 16...  3.17 us
    ppermute x2, waiting for transfers between devices, exchange(): lax.ppermute(high, axis, [(i, (i + 1) % count) for i in range(count)])  2.57 us
    pallas_call x1, Pallas kernels, pack_rows(): call(pack, (jax.ShapeDtypeStruct((bx * by, lanes), bf16), face, face), to...  2.56 us
  transfers between devices with their start and end apart: 5, of which 3 were waited for; matrix products, arithmetic and copies ran while one was open for 3% of the time, Pallas kernels for 6%

profile of v1, /device:TPU:0, one launch (start us, length us, event | category | flops | bytes accessed | tf_op | source)
XLA Modules:
  0.0 49.6 jit_solution(4096352447604117549)
XLA Ops:
  0.0 1.5 %fusion = (bf16[8,32,2,32]{3,2,1,0:T(2,128)(2,1)S(1)}, bf16[8,32,2,32]{3,2,1,0:T(2,128)(2,1)S(1)}) fusion(bf16[8,32,16,32]{3,2,1,0:T(8,128)(2,1)} %vol.1), kind=kLoop, calls=%fused_computation.4 | loop fusion | bytes 131072 | tf_op jit(solution)/shard_map/slice | solution.py:337
  1.5 0.1 reshape.21
  1.6 3.1 %collective-permute-start = (bf16[256,64]{1,0:T(8,128)(2,1)S(1)}, bf16[256,64]{1,0:T(8,128)(2,1)S(1)}, u32[]{:S(2)}, u32[]{:S(2)}) collective-permute-start(bf16[256,64]{1,0:T(8,128)(2,1)S(1)} %reshape.21), channel_id=1, source_target_pairs={{0,1},{1,2},{2,3},{3,0},{4,5},{5,6},{6,7},{7,4},{8,9},{9,10},{10,1... | collective-permute-start | bytes 98312 | tf_op jit(solution)/shard_map/ppermute | solution.py:27
  4.7 0.1 reshape.22
  4.8 2.1 %collective-permute-start.1 = (bf16[256,64]{1,0:T(8,128)(2,1)S(1)}, bf16[256,64]{1,0:T(8,128)(2,1)S(1)}, u32[]{:S(2)}, u32[]{:S(2)}) collective-permute-start(bf16[256,64]{1,0:T(8,128)(2,1)S(1)} %reshape.22), channel_id=1, source_target_pairs={{1,0},{2,1},{3,2},{0,3},{5,4},{6,5},{7,6},{4,7},{9,8},{10,9},{11,1... | collective-permute-start | bytes 98312 | tf_op jit(solution)/shard_map/ppermute | solution.py:28
  6.9 3.2 %spread_weights.1 = (bf16[9,256,192]{2,1,0:T(8,128)(2,1)}, bf16[9,256,192]{2,1,0:T(8,128)(2,1)}, bf16[2,256,512]{2,1,0:T(8,128)(2,1)}) custom-call(bf16[9,96,32]{2,1,0:T(8,128)(2,1)} %bitcast.8, bf16[9,96,32]{2,1,0:T(8,128)(2,1)} %bitcast.9, bf16[256,256]{1,0:T(8,128)(2,1)} %up.1), custom_call_target="tpu_custom_call" | custom-call | tf_op jit(solution)/shard_map/spread_weights/pallas_call | solution.py:64
  10.1 0.0 collective-permute-done.zm
  10.1 0.0 collective-permute-done.1.zp
  10.1 0.6 %copy-done.2 = bf16[256,64]{1,0:T(8,128)(2,1)} copy-done((bf16[256,64]{1,0:T(8,128)(2,1)}, bf16[256,64]{1,0:T(8,128)(2,1)S(1)}, u32[]{:S(2)}) %copy-start.2) | copy-done | bytes 32792
  10.7 0.6 %copy-done.3 = bf16[256,64]{1,0:T(8,128)(2,1)} copy-done((bf16[256,64]{1,0:T(8,128)(2,1)}, bf16[256,64]{1,0:T(8,128)(2,1)S(1)}, u32[]{:S(2)}) %copy-start.3) | copy-done | bytes 32792
  11.3 2.6 %pack.1 = (bf16[256,640]{1,0:T(8,128)(2,1)}, bf16[16,640]{1,0:T(8,128)(2,1)}, bf16[16,640]{1,0:T(8,128)(2,1)}) custom-call(bf16[8,32,16,32]{3,2,1,0:T(8,128)(2,1)} %vol.1, bf16[256,64]{1,0:T(8,128)(2,1)} %copy-done.2, bf16[256,64]{1,0:T(8,128)(2,1)} %copy-done.3), custom_call_target="tpu_custom_call" | custom-call | tf_op jit(solution)/shard_map/pack/pallas_call | solution.py:88
  13.9 0.7 %broadcast_select_fusion = bf16[16,640]{1,0:T(8,128)(2,1)S(1)} fusion(bf16[16,640]{1,0:T(8,128)(2,1)} %get-tuple-element.14, bf16[16,640]{1,0:T(8,128)(2,1)} %get-tuple-element.15, pred[]{:T(512)S(6)} %eq.3), kind=kLoop, calls=%fused_computation.2 | loop fusion | flops 10240 | bytes 61441 | tf_op jit(solution)/shard_map/jit(_where)/select_n | solution.py:24
  14.6 0.9 %fusion.1 = (bf16[64,640]{1,0:T(8,128)(2,1)S(1)}, bf16[64,640]{1,0:T(8,128)(2,1)S(1)}) fusion(bf16[256,640]{1,0:T(8,128)(2,1)} %get-tuple-element.13.vz), kind=kLoop, calls=%fused_computation.5 | loop fusion | bytes 327680 | tf_op jit(solution)/shard_map/slice | solution.py:345
  15.6 0.2 collective-permute-done.2.refs_0_
  15.8 1.8 %collective-permute-start.3 = (bf16[68,640]{1,0:T(8,128)(2,1)S(1)}, bf16[68,640]{1,0:T(8,128)(2,1)S(1)}, u32[]{:S(2)}, u32[]{:S(2)}) collective-permute-start(bf16[68,640]{1,0:T(8,128)(2,1)S(1)} %pad_maximum_fusion), channel_id=1, source_target_pairs={{0,8},{8,16},{16,24},{24,0},{1,9},{9,17},{17,25},{25,1},{2,10},{10... | collective-permute-start | bytes 261128 | tf_op jit(solution)/shard_map/ppermute | solution.py:27
  17.6 1.3 %collective-permute-start.4 = (bf16[68,640]{1,0:T(8,128)(2,1)S(1)}, bf16[68,640]{1,0:T(8,128)(2,1)S(1)}, u32[]{:S(2)}, u32[]{:S(2)}) collective-permute-start(bf16[68,640]{1,0:T(8,128)(2,1)S(1)} %pad_maximum_fusion.1), channel_id=1, source_target_pairs={{8,0},{16,8},{24,16},{0,24},{9,1},{17,9},{25,17},{1,25},{10,2},{18... | collective-permute-start | bytes 261128 | tf_op jit(solution)/shard_map/ppermute | solution.py:28
  18.9 0.7 %pad_add_fusion.pos_ref = s32[3]{0:T(128)} fusion(s32[1]{0:T(128)} %bitcast.2, s32[1]{0:T(128)} %bitcast.1, s32[1]{0:T(128)} %bitcast), kind=kLoop, calls=%fused_computation.3 | loop fusion | flops 6 | bytes 24 | tf_op jit(solution)/shard_map/stack | solution.py:333
  19.5 2.6 %collective-permute-done.3.refs_1_ = bf16[68,640]{1,0:T(8,128)(2,1)S(1)} collective-permute-done((bf16[68,640]{1,0:T(8,128)(2,1)S(1)}, bf16[68,640]{1,0:T(8,128)(2,1)S(1)}, u32[]{:S(2)}, u32[]{:S(2)}) %collective-permute-start.3) | collective-permute-done | bytes 87072 | tf_op jit(solution)/shard_map/ppermute | solution.py:27
  22.1 1.8 %collective-permute-done.4.refs_2_ = bf16[68,640]{1,0:T(8,128)(2,1)S(1)} collective-permute-done((bf16[68,640]{1,0:T(8,128)(2,1)S(1)}, bf16[68,640]{1,0:T(8,128)(2,1)S(1)}, u32[]{:S(2)}, u32[]{:S(2)}) %collective-permute-start.4) | collective-permute-done | bytes 87072 | tf_op jit(solution)/shard_map/ppermute | solution.py:28
  23.9 0.6 %copy-done.1 = bf16[68,640]{1,0:T(8,128)(2,1)} copy-done((bf16[68,640]{1,0:T(8,128)(2,1)}, bf16[68,640]{1,0:T(8,128)(2,1)S(1)}, u32[]{:S(2)}) %copy-start.1) | copy-done | bytes 87064
  24.5 4.2 %encode_rows.1 = (bf16[400,576]{1,0:T(8,128)(2,1)}, f32[8,256]{1,0:T(8,128)}) custom-call(s32[3]{0:T(128)} %pad_add_fusion.pos_ref, bf16[256,640]{1,0:T(8,128)(2,1)} %get-tuple-element.13.vz, bf16[16,640]{1,0:T(8,128)(2,1)} %copy-done.4, bf16[68,640]{1,0:T(8,128)(2,1)} %copy-done, bf16[68,640]{1,0:T(8,128)(2,1)} %copy-done.1, ...), custom_call_target="tpu_custom_call" | custom-call | tf_op jit(solution)/shard_map/encode_rows/pallas_call | solution.py:185
  28.8 0.7 %broadcast_in_dim.4 = f32[32,8,256]{2,1,0:T(8,128)S(1)} broadcast(f32[8,256]{1,0:T(8,128)} %get-tuple-element.17), dimensions={1,2} | broadcast | bytes 270336 | tf_op jit(solution)/shard_map/broadcast_in_dim | solution.py:352
  29.5 13.7 %all_to_all.5 = f32[32,8,256]{2,1,0:T(8,128)} all-to-all(f32[32,8,256]{2,1,0:T(8,128)S(1)} %broadcast_in_dim.4), channel_id=1, replica_groups=mesh['gx'=4,'gy'=2,'gz'=4] {'gx','gy','gz'}, dimensions={0} | all-to-all | bytes 524288 | tf_op jit(solution)/shard_map/all_to_all | solution.py:353
  43.2 6.5 %attend.1 = bf16[8,32,16,32]{3,2,1,0:T(8,128)(2,1)} custom-call(s32[3]{0:T(128)} %pad_add_fusion.pos_ref, f32[256,256]{1,0:T(8,128)} %bitcast.7, f32[1,256]{1,0:T(1,128)} %bitcast.10, bf16[256,256]{1,0:T(8,128)(2,1)} %qw.1, bf16[256,512]{1,0:T(8,128)(2,1)} %kvw.1, bf16[256,256]{1,0:T(8,128)(2,1)} %ow.1, bf16[2,256,512]{2,1,0:T(8,128)(2,1)} %get-tuple-element.18.upx_ref, ...), custom_call_target="tpu_custom_call" | custom-call | tf_op jit(solution)/shard_map/attend/pallas_call | solution.py:312
  (11 shorter events, 0.0 us)
Async XLA Ops:
  1.6 8.5 %collective-permute-start = (bf16[256,64]{1,0:T(8,128)(2,1)S(1)}, bf16[256,64]{1,0:T(8,128)(2,1)S(1)}, u32[]{:S(2)}, u32[]{:S(2)}) collective-permute-start(bf16[256,64]{1,0:T(8,128)(2,1)S(1)} %reshape.21), channel_id=1, source_target_pairs={{0,1},{1,2},{2,3},{3,0},{4,5},{5,6},{6,7},{7,4},{8,9},{9,10},{10,1... | collective-permute-start | bytes 98312 | tf_op jit(solution)/shard_map/ppermute | solution.py:27
  4.8 5.3 %collective-permute-start.1 = (bf16[256,64]{1,0:T(8,128)(2,1)S(1)}, bf16[256,64]{1,0:T(8,128)(2,1)S(1)}, u32[]{:S(2)}, u32[]{:S(2)}) collective-permute-start(bf16[256,64]{1,0:T(8,128)(2,1)S(1)} %reshape.22), channel_id=1, source_target_pairs={{1,0},{2,1},{3,2},{0,3},{5,4},{6,5},{7,6},{4,7},{9,8},{10,9},{11,1... | collective-permute-start | bytes 98312 | tf_op jit(solution)/shard_map/ppermute | solution.py:28
  10.1 0.6 %copy-start.2 = (bf16[256,64]{1,0:T(8,128)(2,1)}, bf16[256,64]{1,0:T(8,128)(2,1)S(1)}, u32[]{:S(2)}) copy-start(bf16[256,64]{1,0:T(8,128)(2,1)S(1)} %collective-permute-done.zm) | copy-start | bytes 98308
  10.7 0.6 %copy-start.3 = (bf16[256,64]{1,0:T(8,128)(2,1)}, bf16[256,64]{1,0:T(8,128)(2,1)S(1)}, u32[]{:S(2)}) copy-start(bf16[256,64]{1,0:T(8,128)(2,1)S(1)} %collective-permute-done.1.zp) | copy-start | bytes 98308
  14.6 1.2 %collective-permute-start.2 = (bf16[16,640]{1,0:T(8,128)(2,1)S(1)}, bf16[16,640]{1,0:T(8,128)(2,1)S(1)}, u32[]{:S(2)}, u32[]{:S(2)}) collective-permute-start(bf16[16,640]{1,0:T(8,128)(2,1)S(1)} %broadcast_select_fusion), channel_id=1, source_target_pairs={{0,4},{4,0},{1,5},{5,1},{2,6},{6,2},{3,7},{7,3},{8,12},{12,8},{9,1... | collective-permute-start | bytes 61448 | tf_op jit(solution)/shard_map/ppermute | solution.py:25
  15.8 8.1 %copy-start.4 = (bf16[16,640]{1,0:T(8,128)(2,1)}, bf16[16,640]{1,0:T(8,128)(2,1)S(1)}, u32[]{:S(2)}) copy-start(bf16[16,640]{1,0:T(8,128)(2,1)S(1)} %collective-permute-done.2.refs_0_) | copy-start | bytes 61444
  15.8 6.3 %collective-permute-start.3 = (bf16[68,640]{1,0:T(8,128)(2,1)S(1)}, bf16[68,640]{1,0:T(8,128)(2,1)S(1)}, u32[]{:S(2)}, u32[]{:S(2)}) collective-permute-start(bf16[68,640]{1,0:T(8,128)(2,1)S(1)} %pad_maximum_fusion), channel_id=1, source_target_pairs={{0,8},{8,16},{16,24},{24,0},{1,9},{9,17},{17,25},{25,1},{2,10},{10... | collective-permute-start | bytes 261128 | tf_op jit(solution)/shard_map/ppermute | solution.py:27
  17.6 6.3 %collective-permute-start.4 = (bf16[68,640]{1,0:T(8,128)(2,1)S(1)}, bf16[68,640]{1,0:T(8,128)(2,1)S(1)}, u32[]{:S(2)}, u32[]{:S(2)}) collective-permute-start(bf16[68,640]{1,0:T(8,128)(2,1)S(1)} %pad_maximum_fusion.1), channel_id=1, source_target_pairs={{8,0},{16,8},{24,16},{0,24},{9,1},{17,9},{25,17},{1,25},{10,2},{18... | collective-permute-start | bytes 261128 | tf_op jit(solution)/shard_map/ppermute | solution.py:28
  22.1 1.8 %copy-start = (bf16[68,640]{1,0:T(8,128)(2,1)}, bf16[68,640]{1,0:T(8,128)(2,1)S(1)}, u32[]{:S(2)}) copy-start(bf16[68,640]{1,0:T(8,128)(2,1)S(1)} %collective-permute-done.3.refs_1_) | copy-start | bytes 261124
  23.9 0.6 %copy-start.1 = (bf16[68,640]{1,0:T(8,128)(2,1)}, bf16[68,640]{1,0:T(8,128)(2,1)S(1)}, u32[]{:S(2)}) copy-start(bf16[68,640]{1,0:T(8,128)(2,1)S(1)} %collective-permute-done.4.refs_2_) | copy-start | bytes 261124

commit v2 on v1

--- a/solution.py
+++ b/solution.py
@@ -16,28 +16,57 @@
 bf16 = jnp.bfloat16
 
 
-def exchange(low, high, axis):
+def paired(count):
+    return count > 2 and count % 2 == 0
+
+
+def sends(low, high, index, count):
+    if count <= 2:
+        return [jnp.where(index == 0, high, low)]
+    if not paired(count):
+        return [high, low]
+    even = index % 2 == 0
+    return [jnp.where(even, high, low), jnp.where(even, low, high)]
+
+
+def exchange(faces, axis):
     count = lax.axis_size(axis)
     if count == 1:
-        return low, low
+        return list(faces)
     if count == 2:
-        mine = jnp.where(lax.axis_index(axis) == 0, high, low)
-        other = lax.ppermute(mine, axis, [(0, 1), (1, 0)])
-        return other, other
-    below = lax.ppermute(high, axis, [(i, (i + 1) % count) for i in range(count)])
-    above = lax.ppermute(low, axis, [((i + 1) % count, i) for i in range(count)])
-    return below, above
-
-
-def call(body, outs, scratch=(), in_smem=0, total=0):
-    specs = [pl.BlockSpec(memory_space=pltpu.SMEM)] * in_smem + [
-        pl.BlockSpec(memory_space=pltpu.VMEM)
-    ] * (total - in_smem)
+        return [lax.ppermute(faces[0], axis, [(0, 1), (1, 0)])]
+    if not paired(count):
+        up = [(i, (i + 1) % count) for i in range(count)]
+        return [
+            lax.ppermute(faces[0], axis, up),
+            lax.ppermute(faces[1], axis, [(j, i) for i, j in up]),
+        ]
+    return [
+        lax.ppermute(faces[0], axis, [(i, i ^ 1) for i in range(count)]),
+        lax.ppermute(
+            faces[1],
+            axis,
+            [(i, (i + 1) % count if i % 2 else (i - 1) % count) for i in range(count)],
+        ),
+    ]
+
+
+def received(got, index, count):
+    if len(got) == 1:
+        return got[0], got[0]
+    if not paired(count):
+        return got[0], got[1]
+    even = index % 2 == 0
+    return jnp.where(even, got[1], got[0]), jnp.where(even, got[0], got[1])
+
+
+def call(body, outs, scratch=(), operands=0, limit=16 << 20):
     return pl.pallas_call(
         body,
         out_shape=outs,
-        in_specs=specs,
+        in_specs=[pl.BlockSpec(memory_space=pltpu.VMEM)] * operands,
         scratch_shapes=list(scratch),
+        compiler_params=pltpu.CompilerParams(vmem_limit_bytes=limit),
         name=body.__name__,
     )
 
@@ -64,7 +93,7 @@
     return call(
         spread_weights,
         (banded, banded, jax.ShapeDtypeStruct((2, width, 16 * chan), bf16)),
-        total=3,
+        operands=3,
     )(
         kernel_in.reshape(9, 3 * chan, chan),
         kernel_out.reshape(9, 3 * chan, chan),
@@ -72,22 +101,61 @@
     )
 
 
-def pack_rows(volume, below, above):
+def pack_rows(volume):
     bx, by, bz, chan = volume.shape
+
+    def pack(vol, rows):
+        rows[...] = vol[...].reshape(bx * by, bz * chan)
+
+    return call(pack, jax.ShapeDtypeStruct((bx * by, bz * chan), bf16), operands=1)(volume)
+
+
+def y_faces(rows, zgot, shape, counts):
+    bx, by, bz, chan = shape
     lanes = (bz + 4) * chan
-
-    def pack(vol, zm, zp, rows, ylow, yhigh):
-        own = vol[...].reshape(bx * by, bz * chan)
-        full = jnp.concatenate([zm[...], own, zp[...]], axis=1)
-        rows[...] = full
-        planes = full.astype(f32).reshape(bx, by, lanes)
-        ylow[...] = planes[:, :2].reshape(bx * 2, lanes).astype(bf16)
-        yhigh[...] = planes[:, by - 2 :].reshape(bx * 2, lanes).astype(bf16)
+    many = 1 if counts[1] <= 2 else 2
+    parts = len(zgot)
+
+    def y_face(own, *refs):
+        zm, zp = received([r[...].astype(f32) for r in refs[:parts]], lax.axis_index("gz"), counts[2])
+        full = jnp.concatenate([zm, own[...].astype(f32), zp], axis=1)
+        low, high = [], []
+        for x in range(bx):
+            low.append(full[x * by : x * by + 2])
+            high.append(full[(x + 1) * by - 2 : (x + 1) * by])
+        faces = sends(
+            jnp.concatenate(low, axis=0), jnp.concatenate(high, axis=0), lax.axis_index("gy"), counts[1]
+        )
+        for ref, face in zip(refs[parts:], faces):
+            ref[...] = face.astype(bf16)
 
     face = jax.ShapeDtypeStruct((bx * 2, lanes), bf16)
-    return call(
-        pack, (jax.ShapeDtypeStruct((bx * by, lanes), bf16), face, face), total=3
-    )(volume, below, above)
+    return call(y_face, (face,) * many, operands=1 + parts)(rows, *zgot)
+
+
+def x_faces(rows, zgot, ygot, shape, counts):
+    bx, by, bz, chan = shape
+    lanes = (bz + 4) * chan
+    zparts, yparts = len(zgot), len(ygot)
+    many = 1 if counts[0] <= 2 else 2
+    tall = 2 * by + 4 * yparts
+
+    def x_face(own, *refs):
+        zrefs, yrefs, outs = refs[:zparts], refs[zparts : zparts + yparts], refs[zparts + yparts :]
+        index = lax.axis_index("gz")
+
+        def face(first):
+            at = slice(first * by, (first + 2) * by)
+            zm, zp = received([r[at, :].astype(f32) for r in zrefs], index, counts[2])
+            body = jnp.concatenate([zm, own[at, :].astype(f32), zp], axis=1)
+            edges = [r[...].astype(f32)[2 * first : 2 * first + 4] for r in yrefs]
+            return jnp.concatenate([body] + edges, axis=0)
+
+        for ref, value in zip(outs, sends(face(0), face(bx - 2), lax.axis_index("gx"), counts[0])):
+            ref[...] = value.astype(bf16)
+
+    face = jax.ShapeDtypeStruct((tall, lanes), bf16)
+    return call(x_face, (face,) * many, operands=1 + zparts + yparts)(rows, *zgot, *ygot)
 
 
 def banded_conv(source, weights, sums, blocks, rows, stride, chan):
@@ -107,7 +175,7 @@
     return outs
 
 
-def encode(pos, rows_z, yfaces, xbelow, xabove, weights, shape, counts):
+def encode(rows, zgot, ygot, xgot, weights, shape, counts):
     bx, by, bz, chan = shape
     nx, ny, nz = counts
     lanes = (bz + 4) * chan
@@ -117,37 +185,41 @@
     ti, tj, tk = bx // 8, by // 8, bz // 8
     tokens = ti * tj * tk
     width = 8 * chan
-    yparts = len(yfaces)
-
-    def encode_rows(pos_ref, vz, *refs):
-        yrefs = refs[:yparts]
-        xm, xp, w, enc, tok, grid, sums, plane_sum = refs[yparts:]
+    zparts, yparts, xparts = len(zgot), len(ygot), len(xgot)
+    devices = nx * ny * nz
+
+    def encode_rows(own, *refs):
+        zrefs, refs = refs[:zparts], refs[zparts:]
+        yrefs, refs = refs[:yparts], refs[yparts:]
+        xrefs, refs = refs[:xparts], refs[xparts:]
+        w, enc, tok_copies, grid, sums, plane_sum = refs
+        ix, iy, iz = (lax.axis_index(axis) for axis in AXES)
         lane = lax.broadcasted_iota(jnp.int32, (1, lanes), 1)
-        z_ok = ((lane >= 2 * chan) | (pos_ref[2] > 0)) & (
-            (lane < (bz + 2) * chan) | (pos_ref[2] < nz - 1)
-        )
-        y_lo, y_hi = pos_ref[1] > 0, pos_ref[1] < ny - 1
-        x_lo, x_hi = pos_ref[0] > 0, pos_ref[0] < nx - 1
+        z_ok = ((lane >= 2 * chan) | (iz > 0)) & ((lane < (bz + 2) * chan) | (iz < nz - 1))
+        y_lo, y_hi = iy > 0, iy < ny - 1
+        x_lo, x_hi = ix > 0, ix < nx - 1
 
         def put(row, value, ok=None):
             good = z_ok if ok is None else z_ok & ok
-            grid[row : row + value.shape[0], :] = jnp.where(good, value.astype(f32), 0.0)
-
+            grid[row : row + value.shape[0], :] = jnp.where(good, value, 0.0)
+
+        ym, yp = received([r[...].astype(f32) for r in yrefs], iy, ny)
         for p in range(bx):
             base = (p + 2) * stride
-            put(base + 2, vz[p * by : (p + 1) * by, :])
-            ym = yrefs[0][...].astype(f32)[2 * p : 2 * p + 2]
-            yp = yrefs[-1][...].astype(f32)[2 * p : 2 * p + 2]
-            put(base, ym, y_lo)
-            put(base + by + 2, yp, y_hi)
-        for ref, first, ok in ((xm, 0, x_lo), (xp, bx + 2, x_hi)):
-            tail = ref[2 * by :, :].astype(f32)
+            at = slice(p * by, (p + 1) * by)
+            zm, zp = received([r[at, :].astype(f32) for r in zrefs], iz, nz)
+            put(base + 2, jnp.concatenate([zm, own[at, :].astype(f32), zp], axis=1))
+            put(base, ym[2 * p : 2 * p + 2], y_lo)
+            put(base + by + 2, yp[2 * p : 2 * p + 2], y_hi)
+        xm, xp = received([r[...].astype(f32) for r in xrefs], ix, nx)
+        for face, first, ok in ((xm, 0, x_lo), (xp, bx + 2, x_hi)):
             for q in range(2):
                 base = (first + q) * stride
-                put(base + 2, ref[q * by : (q + 1) * by, :], ok)
-                put(base, tail[2 * q : 2 * q + 2], ok & y_lo)
-                last = 4 * (yparts - 1) + 2 * q
-                put(base + by + 2, tail[last : last + 2], ok & y_hi)
+                put(base + 2, face[q * by : (q + 1) * by], ok)
+                at = 2 * by + 2 * q
+                low = received([face[at + 4 * i : at + 4 * i + 2] for i in range(yparts)], iy, ny)
+                put(base, low[0], ok & y_lo)
+                put(base + by + 2, low[1], ok & y_hi)
         outs = banded_conv(grid, w, sums, blocks, tall, stride, chan)
         encoded = jnp.maximum(jnp.concatenate(outs, axis=1), 0.0).astype(bf16)
         enc[...] = encoded
@@ -178,24 +250,23 @@
                     [features[a, b, 2 * k + c] for a in range(2) for b in range(2) for c in range(2)],
                     axis=1,
                 )
-        tok[...] = jnp.concatenate(
-            [rows_of[i, k] for i in range(ti) for k in range(tk)], axis=0
-        ).astype(tok.dtype)
+        own_tokens = jnp.concatenate([rows_of[i, k] for i in range(ti) for k in range(tk)], axis=0)
+        for device in range(devices):
+            tok_copies[device] = own_tokens
 
     return call(
         encode_rows,
         (
             jax.ShapeDtypeStruct((tall, (bz + 2) * chan), bf16),
-            jax.ShapeDtypeStruct((tokens, width), f32),
+            jax.ShapeDtypeStruct((devices, tokens, width), f32),
         ),
         scratch=[
             pltpu.VMEM(((bx + 4) * stride, lanes), f32),
             pltpu.VMEM((3, tall + 8, OUT_Z * chan), f32),
             pltpu.VMEM((2 * tk, stride, 4 * chan), f32),
         ],
-        in_smem=1,
-        total=5 + yparts,
-    )(pos, rows_z, *yfaces, xbelow, xabove, weights)
+        operands=2 + zparts + yparts + xparts,
+    )(rows, *zgot, *ygot, *xgot, weights)
 
 
 def sub_blocks(extent):
@@ -207,7 +278,7 @@
 
 
 def attend_and_join(
-    pos, gathered, gain, q_weight, kv_weight, out_weight, upx, encoded, weights, shape, counts
+    gathered, gain, q_weight, kv_weight, out_weight, upx, encoded, weights, shape, counts
 ):
     bx, by, bz, chan = shape
     nx, ny, nz = counts
@@ -216,7 +287,7 @@
     ti, tj, tk = bx // 8, by // 8, bz // 8
     tokens = ti * tj * tk
     width = 8 * chan
-    every = gathered.shape[0]
+    every = gathered.shape[0] * tokens
     asked = 27 * tokens
     head_size = width // HEADS
     wide = (bz + 2) * chan
@@ -236,9 +307,10 @@
                 pick[row : row + many, near * tokens + (i * tk + k) * tj + j] = 1.0
 
     def attend(
-        pos_ref, g, gain_ref, qw, kvw, ow, upx_ref, sel, enc, w, out, normed_all, mine, mine_n, grid, sums
+        g, gain_ref, qw, kvw, ow, upx_ref, sel, enc, w, out, normed_all, mine, mine_n, grid, sums
     ):
-        t = g[...].astype(f32)
+        ix, iy, iz = (lax.axis_index(axis) for axis in AXES)
+        t = g[...].reshape(every, width)
         center = t - jnp.mean(t, axis=1, keepdims=True)
         spread = jnp.mean(center * center, axis=1, keepdims=True)
         normed = (center * lax.rsqrt(spread + 1e-05) * gain_ref[...]).astype(bf16)
@@ -247,13 +319,13 @@
         keys, values = kv[:, :width], kv[:, width:]
         near = 0
         for dx in (-1, 0, 1):
-            x = jnp.clip(pos_ref[0] + dx, 0, nx - 1)
+            x = jnp.clip(ix + dx, 0, nx - 1)
             for dy in (-1, 0, 1):
-                y = jnp.clip(pos_ref[1] + dy, 0, ny - 1)
+                y = jnp.clip(iy + dy, 0, ny - 1)
                 for dz in (-1, 0, 1):
-                    z = jnp.clip(pos_ref[2] + dz, 0, nz - 1)
+                    z = jnp.clip(iz + dz, 0, nz - 1)
                     at = pl.multiple_of(((x * ny + y) * nz + z) * tokens, 8)
-                    mine[near * tokens : (near + 1) * tokens, :] = g[pl.ds(at, tokens), :]
+                    mine[near * tokens : (near + 1) * tokens, :] = g[(x * ny + y) * nz + z]
                     mine_n[near * tokens : (near + 1) * tokens, :] = normed_all[pl.ds(at, tokens), :]
                     near += 1
         q = jnp.dot(mine_n[...].astype(bf16), qw[...], preferred_element_type=f32).astype(bf16)
@@ -277,11 +349,11 @@
 
         row = lax.broadcasted_iota(jnp.int32, (stride, 1), 0)
         second_half = ((row + 3) // 4) % 2 == 0
-        y_ok = ((row > 0) | (pos_ref[1] > 0)) & ((row < by + 1) | (pos_ref[1] < ny - 1))
+        y_ok = ((row > 0) | (iy > 0)) & ((row < by + 1) | (iy < ny - 1))
         zl = lax.broadcasted_iota(jnp.int32, (1, wide), 1)
-        z_ok = ((zl >= chan) | (pos_ref[2] > 0)) & ((zl < (bz + 1) * chan) | (pos_ref[2] < nz - 1))
+        z_ok = ((zl >= chan) | (iz > 0)) & ((zl < (bz + 1) * chan) | (iz < nz - 1))
         ok = y_ok & z_ok
-        x_lo, x_hi = pos_ref[0] > 0, pos_ref[0] < nx - 1
+        x_lo, x_hi = ix > 0, ix < nx - 1
         if padded > wide:
             grid[:, wide:] = jnp.zeros((tall, padded - wide), f32)
         step = len(zs) * stride
@@ -319,10 +391,10 @@
             pltpu.VMEM((tall, padded), f32),
             pltpu.VMEM((3, low + 8, OUT_Z * chan), f32),
         ],
-        in_smem=1,
-        total=10,
+        operands=9,
+        limit=min(60, 18 + 24 * every * asked // (1 << 20)) << 20,
     )(
-        pos, gathered, gain, q_weight, kv_weight, out_weight, upx, jnp.asarray(pick, bf16), encoded, weights
+        gathered, gain, q_weight, kv_weight, out_weight, upx, jnp.asarray(pick, bf16), encoded, weights
     )
 
 
@@ -330,29 +402,23 @@
     shape = volume.shape
     bx, by, bz, chan = shape
     counts = tuple(lax.axis_size(axis) for axis in AXES)
-    pos = jnp.stack([lax.axis_index(axis) for axis in AXES]).astype(jnp.int32)
     first_w, second_w, upx = band_weights(conv_in, conv_out, up_weight, chan)
-
-    z_below, z_above = exchange(
-        volume[:, :, :2].reshape(bx * by, 2 * chan),
-        volume[:, :, bz - 2 :].reshape(bx * by, 2 * chan),
+    zgot = exchange(
+        sends(
+            volume[:, :, :2].reshape(bx * by, 2 * chan),
+            volume[:, :, bz - 2 :].reshape(bx * by, 2 * chan),
+            lax.axis_index("gz"),
+            counts[2],
+        ),
         "gz",
     )
-    rows, y_low, y_high = pack_rows(volume, z_below, z_above)
-    y_below, y_above = exchange(y_low, y_high, "gy")
-    yfaces = [y_below] if counts[1] <= 2 else [y_below, y_above]
-    x_below, x_above = exchange(
-        jnp.concatenate([rows[: 2 * by]] + [face[:4] for face in yfaces], axis=0),
-        jnp.concatenate([rows[(bx - 2) * by :]] + [face[(bx - 2) * 2 :] for face in yfaces], axis=0),
-        "gx",
-    )
-    encoded, tokens = encode(pos, rows, yfaces, x_below, x_above, first_w, shape, counts)
-
-    devices = counts[0] * counts[1] * counts[2]
-    copies = jnp.broadcast_to(tokens[None], (devices,) + tokens.shape)
-    gathered = lax.all_to_all(copies, AXES, 0, 0, tiled=True).reshape(-1, tokens.shape[1])
+    rows = pack_rows(volume)
+    ygot = exchange(y_faces(rows, zgot, shape, counts), "gy")
+    xgot = exchange(x_faces(rows, zgot, ygot, shape, counts), "gx")
+    encoded, copies = encode(rows, zgot, ygot, xgot, first_w, shape, counts)
+    gathered = lax.all_to_all(copies, AXES, 0, 0, tiled=True)
     return attend_and_join(
-        pos, gathered, norm_gain[None], q_weight, kv_weight, out_weight, upx, encoded, second_w, shape, counts
+        gathered, norm_gain[None], q_weight, kv_weight, out_weight, upx, encoded, second_w, shape, counts
     )
 
 

time: 50 us -> 41.2 us (0.82)
  Pallas kernels: 16.4 us -> 8.48 us
  local copies, waits for them, and re-layouts: 5.2 us -> 1.49 us
  waiting for transfers between devices: 4.58 us -> 6.79 us
  starting transfers between devices: 8.23 us -> 8.78 us
    slice x3 -> x0, local copies, waits for them, and re-layouts: 2.4 us -> none  [the longest x1 1.45 us: on_device(): volume[:, :, :2].reshape(bx * by, 2 * chan)]
    pallas_call x1, Pallas kernels: 3.17 us -> 0.9 us  [band_weights(): call(spread_weights, (banded, banded, jax.ShapeDtypeStruct((2, width, 16...]
    ppermute x5, waiting for transfers between devices: 4.58 us -> 6.79 us  [the longest x2 4.83 us: exchange(): lax.ppermute(faces[1], axis, [(i, (i + 1) % count if i % 2 else (i - 1) %...]
    pallas_call x1, Pallas kernels: 4.25 us -> 2.17 us  [encode(): call(encode_rows, (jax.ShapeDtypeStruct((tall, (bz + 2) * chan), bf16), j...]
    pallas_call x1 -> x3, Pallas kernels: 2.56 us -> 0.68 us  [the longest x1 0.45 us: pack_rows(): call(pack, jax.ShapeDtypeStruct((bx * by, bz * chan), bf16), operands=1)]
    pallas_call x1, Pallas kernels: 6.45 us -> 4.72 us  [attend_and_join(): call(attend, jax.ShapeDtypeStruct(shape, bf16), scratch=[pltpu.VMEM((ever...]
    select_n x1, other arithmetic: 0.74 us -> 1.53 us  [sends(): return [jnp.where(even, high, low), jnp.where(even, low, high)]]
    broadcast_in_dim x1 -> x0, local copies, waits for them, and re-layouts: 0.71 us -> none  [on_device(): copies = jnp.broadcast_to(tokens[None], (devices,) + tokens.shape)]
  transfers between devices with their start and end apart: 5 -> 5, of which waited for: 3 -> 4; matrix products, arithmetic and copies ran while one was open for 3% -> 0% of each run, Pallas kernels for 6% -> 3%
where the time goes in v2:
time: 41.2 us; the launch traced here: 41 us
  blocking collectives  13.8 us (33%)
  starting transfers between devices  8.78 us (21%)
  Pallas kernels  8.48 us (21%)
  waiting for transfers between devices  6.79 us (16%)
  other arithmetic  1.53 us (4%)
  local copies, waits for them, and re-layouts  1.49 us (4%)
    all_to_all x1, blocking collectives, on_device(): gathered = lax.all_to_all(copies, AXES, 0, 0, tiled=True)  13.8 us
    ppermute x2, waiting for transfers between devices, exchange(): lax.ppermute(faces[1], axis, [(i, (i + 1) % count if i % 2 else (i - 1) %...  4.83 us
    pallas_call x1, Pallas kernels, attend_and_join(): call(attend, jax.ShapeDtypeStruct(shape, bf16), scratch=[pltpu.VMEM((ever...  4.72 us
    ppermute x2, starting transfers between devices, exchange(): lax.ppermute(faces[0], axis, [(i, i ^ 1) for i in range(count)])  4.67 us
    ppermute x2, starting transfers between devices, exchange(): lax.ppermute(faces[1], axis, [(i, (i + 1) % count if i % 2 else (i - 1) %...  4.03 us
    pallas_call x1, Pallas kernels, encode(): call(encode_rows, (jax.ShapeDtypeStruct((tall, (bz + 2) * chan), bf16), j...  2.17 us
    select_n x1, other arithmetic, sends(): return [jnp.where(even, high, low), jnp.where(even, low, high)]  1.53 us
    unnamed x18, local copies, waits for them, and re-layouts  1.27 us
  transfers between devices with their start and end apart: 5, of which 4 were waited for; matrix products, arithmetic and copies ran while one was open for 0% of the time, Pallas kernels for 3%

profile of v2, /device:TPU:0, one launch (start us, length us, event | category | flops | bytes accessed | tf_op | source)
XLA Modules:
  0.0 41.0 jit_solution(1829202262788520401)
XLA Ops:
  0.0 1.5 %broadcast_select_fusion = (bf16[8,32,2,32]{3,2,1,0:T(2,128)(2,1)S(1)}, bf16[8,32,2,32]{3,2,1,0:T(2,128)(2,1)S(1)}) fusion(pred[]{:T(512)S(6)} %eq.5, bf16[8,32,16,32]{3,2,1,0:T(8,128)(2,1)} %vol.1), kind=kLoop, calls=%fused_computation | loop fusion | flops 32768 | bytes 131073 | tf_op jit(solution)/shard_map/jit(_where)/select_n | solution.py:29
  1.5 0.0 copy-start.3
  1.5 0.1 reshape.14
  1.7 3.1 %collective-permute-start = (bf16[256,64]{1,0:T(8,128)(2,1)S(1)}, bf16[256,64]{1,0:T(8,128)(2,1)S(1)}, u32[]{:S(2)}, u32[]{:S(2)}) collective-permute-start(bf16[256,64]{1,0:T(8,128)(2,1)S(1)} %reshape.14), channel_id=1, source_target_pairs={{0,1},{1,0},{2,3},{3,2},{4,5},{5,4},{6,7},{7,6},{8,9},{9,8},{10,11... | collective-permute-start | bytes 98312 | tf_op jit(solution)/shard_map/ppermute | solution.py:45
  4.8 0.1 reshape.15
  4.9 2.5 %collective-permute-start.1 = (bf16[256,64]{1,0:T(8,128)(2,1)S(1)}, bf16[256,64]{1,0:T(8,128)(2,1)S(1)}, u32[]{:S(2)}, u32[]{:S(2)}) collective-permute-start(bf16[256,64]{1,0:T(8,128)(2,1)S(1)} %reshape.15), channel_id=1, source_target_pairs={{0,3},{1,2},{2,1},{3,0},{4,7},{5,6},{6,5},{7,4},{8,11},{9,10},{10,... | collective-permute-start | bytes 98312 | tf_op jit(solution)/shard_map/ppermute | solution.py:46
  7.5 1.2 %copy-done = bf16[8,32,16,32]{3,2,1,0:T(8,128)(2,1)S(1)} copy-done((bf16[8,32,16,32]{3,2,1,0:T(8,128)(2,1)S(1)}, bf16[8,32,16,32]{3,2,1,0:T(8,128)(2,1)}, u32[]{:S(2)}) %copy-start) | copy-done | bytes 262168
  8.7 0.5 %pack.1.own = bf16[256,512]{1,0:T(8,128)(2,1)S(1)} custom-call(bf16[8,32,16,32]{3,2,1,0:T(8,128)(2,1)S(1)} %copy-done), custom_call_target="tpu_custom_call" | custom-call | tf_op jit(solution)/shard_map/pack/pallas_call | solution.py:110
  9.1 1.9 %collective-permute-done.1.refs_1_ = bf16[256,64]{1,0:T(8,128)(2,1)S(1)} collective-permute-done((bf16[256,64]{1,0:T(8,128)(2,1)S(1)}, bf16[256,64]{1,0:T(8,128)(2,1)S(1)}, u32[]{:S(2)}, u32[]{:S(2)}) %collective-permute-start.1) | collective-permute-done | bytes 32800 | tf_op jit(solution)/shard_map/ppermute | solution.py:46
  11.0 0.1 y_face.1
  11.2 0.1 collective-permute-start.2
  11.2 1.2 %collective-permute-done.2.refs_2_ = bf16[16,640]{1,0:T(8,128)(2,1)S(1)} collective-permute-done((bf16[16,640]{1,0:T(8,128)(2,1)S(1)}, bf16[16,640]{1,0:T(8,128)(2,1)S(1)}, u32[]{:S(2)}, u32[]{:S(2)}) %collective-permute-start.2) | collective-permute-done | bytes 20512 | tf_op jit(solution)/shard_map/ppermute | solution.py:37
  12.4 0.1 x_face.1
  12.5 1.6 %collective-permute-start.3 = (bf16[68,640]{1,0:T(8,128)(2,1)S(1)}, bf16[68,640]{1,0:T(8,128)(2,1)S(1)}, u32[]{:S(2)}, u32[]{:S(2)}) collective-permute-start(bf16[68,640]{1,0:T(8,128)(2,1)S(1)} %get-tuple-element.12), channel_id=1, source_target_pairs={{0,8},{8,0},{16,24},{24,16},{1,9},{9,1},{17,25},{25,17},{2,10},{10... | collective-permute-start | bytes 261128 | tf_op jit(solution)/shard_map/ppermute | solution.py:45
  14.1 1.5 %collective-permute-start.4 = (bf16[68,640]{1,0:T(8,128)(2,1)S(1)}, bf16[68,640]{1,0:T(8,128)(2,1)S(1)}, u32[]{:S(2)}, u32[]{:S(2)}) collective-permute-start(bf16[68,640]{1,0:T(8,128)(2,1)S(1)} %get-tuple-element.13), channel_id=1, source_target_pairs={{0,24},{8,16},{16,8},{24,0},{1,25},{9,17},{17,9},{25,1},{2,26},{10... | collective-permute-start | bytes 261128 | tf_op jit(solution)/shard_map/ppermute | solution.py:46
  15.6 0.9 %spread_weights.1 = (bf16[9,256,192]{2,1,0:T(8,128)(2,1)S(1)}, bf16[9,256,192]{2,1,0:T(8,128)(2,1)S(1)}, bf16[2,256,512]{2,1,0:T(8,128)(2,1)S(1)}) custom-call(bf16[9,96,32]{2,1,0:T(8,128)(2,1)S(1)} %bitcast.3, bf16[9,96,32]{2,1,0:T(8,128)(2,1)S(1)} %bitcast.4, bf16[256,256]{1,0:T(8,128)(2,1)S(1)} %copy-done.7), custom_call_target="tpu_custom_call" | custom-call | tf_op jit(solution)/shard_map/spread_weights/pallas_call | solution.py:93
  16.5 0.0 copy-start.1
  16.5 0.0 copy-start.5
  16.5 0.0 copy-start.6
  16.6 0.8 %collective-permute-done.3.refs_3_ = bf16[68,640]{1,0:T(8,128)(2,1)S(1)} collective-permute-done((bf16[68,640]{1,0:T(8,128)(2,1)S(1)}, bf16[68,640]{1,0:T(8,128)(2,1)S(1)}, u32[]{:S(2)}, u32[]{:S(2)}) %collective-permute-start.3) | collective-permute-done | bytes 87072 | tf_op jit(solution)/shard_map/ppermute | solution.py:45
  17.3 2.9 %collective-permute-done.4.refs_4_ = bf16[68,640]{1,0:T(8,128)(2,1)S(1)} collective-permute-done((bf16[68,640]{1,0:T(8,128)(2,1)S(1)}, bf16[68,640]{1,0:T(8,128)(2,1)S(1)}, u32[]{:S(2)}, u32[]{:S(2)}) %collective-permute-start.4) | collective-permute-done | bytes 87072 | tf_op jit(solution)/shard_map/ppermute | solution.py:46
  20.3 2.2 %encode_rows.1 = (bf16[400,576]{1,0:T(8,128)(2,1)S(1)}, f32[32,8,256]{2,1,0:T(8,128)S(1)}) custom-call(bf16[256,512]{1,0:T(8,128)(2,1)S(1)} %pack.1.own, bf16[256,64]{1,0:T(8,128)(2,1)S(1)} %collective-permute-done.refs_0_, bf16[256,64]{1,0:T(8,128)(2,1)S(1)} %collective-permute-done.1.refs_1_, bf16[16,640]{1,0:T(8,128)(2,1)S(1)} %collective-permute-done.2.refs_2_, ...), custom_call_target="tpu_custom_call" | custom-call | tf_op jit(solution)/shard_map/encode_rows/pallas_call | solution.py:257
  22.5 13.8 %all_to_all.5.g = f32[32,8,256]{2,1,0:T(8,128)S(1)} all-to-all(f32[32,8,256]{2,1,0:T(8,128)S(1)} %get-tuple-element.15), channel_id=1, replica_groups=mesh['gx'=4,'gy'=2,'gz'=4] {'gx','gy','gz'}, dimensions={0} | all-to-all | bytes 524288 | tf_op jit(solution)/shard_map/all_to_all | solution.py:419
  36.3 4.7 %attend.1 = bf16[8,32,16,32]{3,2,1,0:T(8,128)(2,1)} custom-call(f32[32,8,256]{2,1,0:T(8,128)S(1)} %all_to_all.5.g, f32[1,256]{1,0:T(1,128)S(1)} %bitcast.5, bf16[256,256]{1,0:T(8,128)(2,1)S(1)} %copy-done.5, bf16[256,512]{1,0:T(8,128)(2,1)S(1)} %copy-done.2, bf16[256,256]{1,0:T(8,128)(2,1)S(1)} %copy-done.6, ...), custom_call_target="tpu_custom_call" | custom-call | tf_op jit(solution)/shard_map/attend/pallas_call | solution.py:384
  (14 shorter events, 0.0 us)
Async XLA Ops:
  0.0 15.6 %copy-start.4 = (bf16[3,3,3,32,32]{4,3,2,1,0:T(8,128)(2,1)S(1)}, bf16[3,3,3,32,32]{4,3,2,1,0:T(8,128)(2,1)}, u32[]{:S(2)}) copy-start(bf16[3,3,3,32,32]{4,3,2,1,0:T(8,128)(2,1)} %param.11) | copy-start | bytes 165892
  1.5 14.1 %copy-start.3 = (bf16[3,3,3,32,32]{4,3,2,1,0:T(8,128)(2,1)S(1)}, bf16[3,3,3,32,32]{4,3,2,1,0:T(8,128)(2,1)}, u32[]{:S(2)}) copy-start(bf16[3,3,3,32,32]{4,3,2,1,0:T(8,128)(2,1)} %param.10) | copy-start | bytes 165892
  1.7 13.9 %copy-start.7 = (bf16[256,256]{1,0:T(8,128)(2,1)S(1)}, bf16[256,256]{1,0:T(8,128)(2,1)}, u32[]{:S(2)}) copy-start(bf16[256,256]{1,0:T(8,128)(2,1)} %up.1) | copy-start | bytes 393220
  1.7 7.5 %collective-permute-start = (bf16[256,64]{1,0:T(8,128)(2,1)S(1)}, bf16[256,64]{1,0:T(8,128)(2,1)S(1)}, u32[]{:S(2)}, u32[]{:S(2)}) collective-permute-start(bf16[256,64]{1,0:T(8,128)(2,1)S(1)} %reshape.14), channel_id=1, source_target_pairs={{0,1},{1,0},{2,3},{3,2},{4,5},{5,4},{6,7},{7,6},{8,9},{9,8},{10,11... | collective-permute-start | bytes 98312 | tf_op jit(solution)/shard_map/ppermute | solution.py:45
  4.9 6.1 %collective-permute-start.1 = (bf16[256,64]{1,0:T(8,128)(2,1)S(1)}, bf16[256,64]{1,0:T(8,128)(2,1)S(1)}, u32[]{:S(2)}, u32[]{:S(2)}) collective-permute-start(bf16[256,64]{1,0:T(8,128)(2,1)S(1)} %reshape.15), channel_id=1, source_target_pairs={{0,3},{1,2},{2,1},{3,0},{4,7},{5,6},{6,5},{7,4},{8,11},{9,10},{10,... | collective-permute-start | bytes 98312 | tf_op jit(solution)/shard_map/ppermute | solution.py:46
  7.5 1.2 %copy-start = (bf16[8,32,16,32]{3,2,1,0:T(8,128)(2,1)S(1)}, bf16[8,32,16,32]{3,2,1,0:T(8,128)(2,1)}, u32[]{:S(2)}) copy-start(bf16[8,32,16,32]{3,2,1,0:T(8,128)(2,1)} %vol.1) | copy-start | bytes 786436
  11.2 1.3 %collective-permute-start.2 = (bf16[16,640]{1,0:T(8,128)(2,1)S(1)}, bf16[16,640]{1,0:T(8,128)(2,1)S(1)}, u32[]{:S(2)}, u32[]{:S(2)}) collective-permute-start(bf16[16,640]{1,0:T(8,128)(2,1)S(1)} %y_face.1), channel_id=1, source_target_pairs={{0,4},{4,0},{1,5},{5,1},{2,6},{6,2},{3,7},{7,3},{8,12},{12,8},{9,1... | collective-permute-start | bytes 61448 | tf_op jit(solution)/shard_map/ppermute | solution.py:37
  12.5 4.8 %collective-permute-start.3 = (bf16[68,640]{1,0:T(8,128)(2,1)S(1)}, bf16[68,640]{1,0:T(8,128)(2,1)S(1)}, u32[]{:S(2)}, u32[]{:S(2)}) collective-permute-start(bf16[68,640]{1,0:T(8,128)(2,1)S(1)} %get-tuple-element.12), channel_id=1, source_target_pairs={{0,8},{8,0},{16,24},{24,16},{1,9},{9,1},{17,25},{25,17},{2,10},{10... | collective-permute-start | bytes 261128 | tf_op jit(solution)/shard_map/ppermute | solution.py:45
  14.1 6.2 %collective-permute-start.4 = (bf16[68,640]{1,0:T(8,128)(2,1)S(1)}, bf16[68,640]{1,0:T(8,128)(2,1)S(1)}, u32[]{:S(2)}, u32[]{:S(2)}) collective-permute-start(bf16[68,640]{1,0:T(8,128)(2,1)S(1)} %get-tuple-element.13), channel_id=1, source_target_pairs={{0,24},{8,16},{16,8},{24,0},{1,25},{9,17},{17,9},{25,1},{2,26},{10... | collective-permute-start | bytes 261128 | tf_op jit(solution)/shard_map/ppermute | solution.py:46
  16.5 19.8 %copy-start.1 = (bf16[640,216]{1,0:T(8,128)(2,1)S(1)}, bf16[640,216]{1,0:T(8,128)(2,1)}, u32[]{:S(2)}) copy-start(bf16[640,216]{1,0:T(8,128)(2,1)} %constant.20.clone.sel) | copy-start | bytes 829444
  16.5 19.8 %copy-start.2 = (bf16[256,512]{1,0:T(8,128)(2,1)S(1)}, bf16[256,512]{1,0:T(8,128)(2,1)}, u32[]{:S(2)}) copy-start(bf16[256,512]{1,0:T(8,128)(2,1)} %kvw.1) | copy-start | bytes 786436
  16.5 19.8 %copy-start.5 = (bf16[256,256]{1,0:T(8,128)(2,1)S(1)}, bf16[256,256]{1,0:T(8,128)(2,1)}, u32[]{:S(2)}) copy-start(bf16[256,256]{1,0:T(8,128)(2,1)} %qw.1) | copy-start | bytes 393220
  16.5 19.7 %copy-start.6 = (bf16[256,256]{1,0:T(8,128)(2,1)S(1)}, bf16[256,256]{1,0:T(8,128)(2,1)}, u32[]{:S(2)}) copy-start(bf16[256,256]{1,0:T(8,128)(2,1)} %ow.1) | copy-start | bytes 393220
  16.5 19.7 %copy-start.8 = (f32[256]{0:T(256)S(1)}, f32[256]{0:T(256)}, u32[]{:S(2)}) copy-start(f32[256]{0:T(256)} %param.12) | copy-start | bytes 3076

commit v3 on v2

--- a/solution.py
+++ b/solution.py
@@ -101,13 +101,48 @@
     )
 
 
-def pack_rows(volume):
+def pack_rows(volume, counts):
     bx, by, bz, chan = volume.shape
-
-    def pack(vol, rows):
-        rows[...] = vol[...].reshape(bx * by, bz * chan)
-
-    return call(pack, jax.ShapeDtypeStruct((bx * by, bz * chan), bf16), operands=1)(volume)
+    many = 1 if counts[2] <= 2 else 2
+    half = bx * by // 2
+
+    def pack(vol, rows, *refs):
+        outs, (here, arrived) = refs[:many], refs[many:]
+        copies = [pltpu.make_async_copy(vol.at[x], here.at[x], arrived.at[x]) for x in range(bx)]
+        for copy in copies:
+            copy.start()
+        for x in range(bx):
+            copies[x].wait()
+            rows[x * by : (x + 1) * by, :] = here[x].reshape(by, bz * chan)
+
+        def beside(start):
+            return jnp.concatenate(
+                [rows[:half, start : start + 2 * chan], rows[half:, start : start + 2 * chan]], axis=1
+            )
+
+        faces = sends(beside(0), beside((bz - 2) * chan), lax.axis_index("gz"), counts[2])
+        for ref, face in zip(outs, faces):
+            ref[...] = face
+
+    return pl.pallas_call(
+        pack,
+        out_shape=(jax.ShapeDtypeStruct((bx * by, bz * chan), bf16),)
+        + (jax.ShapeDtypeStruct((half, 4 * chan), bf16),) * many,
+        in_specs=[pl.BlockSpec(memory_space=pltpu.HBM)],
+        scratch_shapes=[pltpu.VMEM(volume.shape, bf16), pltpu.SemaphoreType.DMA((bx,))],
+        compiler_params=pltpu.CompilerParams(vmem_limit_bytes=16 << 20),
+        name="pack",
+    )(pltpu.with_memory_space_constraint(volume, pltpu.HBM))
+
+
+def full_rows(own, zrefs, plane, shape, count):
+    bx, by, bz, chan = shape
+    side, at = divmod(plane, bx // 2)
+    parts = [
+        r[at * by : (at + 1) * by, side * 2 * chan : (side + 1) * 2 * chan].astype(f32) for r in zrefs
+    ]
+    zm, zp = received(parts, lax.axis_index("gz"), count)
+    return jnp.concatenate([zm, own[plane * by : (plane + 1) * by, :].astype(f32), zp], axis=1)
 
 
 def y_faces(rows, zgot, shape, counts):
@@ -117,12 +152,11 @@
     parts = len(zgot)
 
     def y_face(own, *refs):
-        zm, zp = received([r[...].astype(f32) for r in refs[:parts]], lax.axis_index("gz"), counts[2])
-        full = jnp.concatenate([zm, own[...].astype(f32), zp], axis=1)
         low, high = [], []
         for x in range(bx):
-            low.append(full[x * by : x * by + 2])
-            high.append(full[(x + 1) * by - 2 : (x + 1) * by])
+            full = full_rows(own, refs[:parts], x, shape, counts[2])
+            low.append(full[:2])
+            high.append(full[by - 2 :])
         faces = sends(
             jnp.concatenate(low, axis=0), jnp.concatenate(high, axis=0), lax.axis_index("gy"), counts[1]
         )
@@ -142,14 +176,11 @@
 
     def x_face(own, *refs):
         zrefs, yrefs, outs = refs[:zparts], refs[zparts : zparts + yparts], refs[zparts + yparts :]
-        index = lax.axis_index("gz")
 
         def face(first):
-            at = slice(first * by, (first + 2) * by)
-            zm, zp = received([r[at, :].astype(f32) for r in zrefs], index, counts[2])
-            body = jnp.concatenate([zm, own[at, :].astype(f32), zp], axis=1)
+            body = [full_rows(own, zrefs, first + q, shape, counts[2]) for q in range(2)]
             edges = [r[...].astype(f32)[2 * first : 2 * first + 4] for r in yrefs]
-            return jnp.concatenate([body] + edges, axis=0)
+            return jnp.concatenate(body + edges, axis=0)
 
         for ref, value in zip(outs, sends(face(0), face(bx - 2), lax.axis_index("gx"), counts[0])):
             ref[...] = value.astype(bf16)
@@ -158,80 +189,135 @@
     return call(x_face, (face,) * many, operands=1 + zparts + yparts)(rows, *zgot, *ygot)
 
 
-def banded_conv(source, weights, sums, blocks, rows, stride, chan):
+def banded_conv(source, weights, sums, blocks, starts, rows, stride, chan):
     outs = []
+    tall = rows * len(starts)
     for block in range(blocks):
-        start = block * OUT_Z * chan
+        lane = block * OUT_Z * chan
         for dy in range(3):
             total = None
             for dx in range(3):
-                piece = source[dx * stride : dx * stride + rows, start : start + IN_Z * chan]
+                pieces = [
+                    source[at + dx * stride : at + dx * stride + rows, lane : lane + IN_Z * chan]
+                    for at in starts
+                ]
+                piece = pieces[0] if len(pieces) == 1 else jnp.concatenate(pieces, axis=0)
                 part = jnp.dot(
                     piece.astype(bf16), weights[dx * 3 + dy], preferred_element_type=f32
                 )
                 total = part if total is None else total + part
-            sums[dy, :rows, :] = total
-        outs.append(sums[0, 0:rows, :] + sums[1, 1 : rows + 1, :] + sums[2, 2 : rows + 2, :])
+            sums[dy, :tall, :] = total
+        outs.append(sums[0, 0:tall, :] + sums[1, 1 : tall + 1, :] + sums[2, 2 : tall + 2, :])
     return outs
 
 
-def encode(rows, zgot, ygot, xgot, weights, shape, counts):
+def put_plane(grid, row, own, zrefs, yrefs, plane, shape, counts):
+    bx, by, bz, chan = shape
+    nx, ny, nz = counts
+    iy, iz = lax.axis_index("gy"), lax.axis_index("gz")
+    lane = lax.broadcasted_iota(jnp.int32, (1, (bz + 4) * chan), 1)
+    z_ok = ((lane >= 2 * chan) | (iz > 0)) & ((lane < (bz + 2) * chan) | (iz < nz - 1))
+    full = full_rows(own, zrefs, plane, shape, nz)
+    grid[row + 2 : row + 2 + by, :] = jnp.where(z_ok, full, 0.0)
+    ym, yp = received(
+        [r[...].astype(f32)[2 * plane : 2 * plane + 2] for r in yrefs], iy, ny
+    )
+    grid[row : row + 2, :] = jnp.where(z_ok & (iy > 0), ym, 0.0)
+    grid[row + by + 2 : row + by + 4, :] = jnp.where(z_ok & (iy < ny - 1), yp, 0.0)
+
+
+def relu_rows(outs):
+    return jnp.maximum(jnp.concatenate(outs, axis=1), 0.0).astype(bf16)
+
+
+def encode_inner(rows, zgot, ygot, weights, shape, counts):
+    bx, by, bz, chan = shape
+    lanes = (bz + 4) * chan
+    stride = by + 8
+    tall = (bx - 2) * stride
+    groups = bx // 4
+    zparts, yparts = len(zgot), len(ygot)
+
+    def encode_middle(own, *refs):
+        zrefs, refs = refs[:zparts], refs[zparts:]
+        yrefs, (w, enc, partial, grid, sums) = refs[:yparts], refs[yparts:]
+        for p in range(bx):
+            put_plane(grid, p * stride, own, zrefs, yrefs, p, shape, counts)
+        outs = banded_conv(grid, w, sums, (bz + 2) // OUT_Z, [0], tall, stride, chan)
+        encoded = relu_rows(outs)
+        enc[...] = encoded
+        cells = encoded.astype(f32)
+        for group in range(groups):
+            total = None
+            for x in range(max(1, 4 * group), min(bx - 1, 4 * group + 4)):
+                plane = cells[(x - 1) * stride : x * stride]
+                total = plane if total is None else total + plane
+            partial[group * stride : (group + 1) * stride, :] = total
+
+    return call(
+        encode_middle,
+        (
+            jax.ShapeDtypeStruct((tall, (bz + 2) * chan), bf16),
+            jax.ShapeDtypeStruct((groups * stride, (bz + 2) * chan), f32),
+        ),
+        scratch=[
+            pltpu.VMEM((bx * stride, lanes), f32),
+            pltpu.VMEM((3, tall + 8, OUT_Z * chan), f32),
+        ],
+        operands=2 + zparts + yparts,
+    )(rows, *zgot, *ygot, weights)
+
+
+def encode_outer(rows, zgot, ygot, xgot, weights, partial, shape, counts):
     bx, by, bz, chan = shape
     nx, ny, nz = counts
     lanes = (bz + 4) * chan
     stride = by + 8
-    tall = (bx + 2) * stride
-    blocks = (bz + 2) // OUT_Z
+    tall = 4 * stride
+    groups = bx // 4
     ti, tj, tk = bx // 8, by // 8, bz // 8
     tokens = ti * tj * tk
     width = 8 * chan
     zparts, yparts, xparts = len(zgot), len(ygot), len(xgot)
     devices = nx * ny * nz
 
-    def encode_rows(own, *refs):
+    def encode_ends(own, *refs):
         zrefs, refs = refs[:zparts], refs[zparts:]
         yrefs, refs = refs[:yparts], refs[yparts:]
         xrefs, refs = refs[:xparts], refs[xparts:]
-        w, enc, tok_copies, grid, sums, plane_sum = refs
+        w, part_ref, enc, tok_copies, grid, sums, plane_sum = refs
         ix, iy, iz = (lax.axis_index(axis) for axis in AXES)
         lane = lax.broadcasted_iota(jnp.int32, (1, lanes), 1)
         z_ok = ((lane >= 2 * chan) | (iz > 0)) & ((lane < (bz + 2) * chan) | (iz < nz - 1))
-        y_lo, y_hi = iy > 0, iy < ny - 1
-        x_lo, x_hi = ix > 0, ix < nx - 1
-
-        def put(row, value, ok=None):
-            good = z_ok if ok is None else z_ok & ok
-            grid[row : row + value.shape[0], :] = jnp.where(good, value, 0.0)
-
-        ym, yp = received([r[...].astype(f32) for r in yrefs], iy, ny)
-        for p in range(bx):
-            base = (p + 2) * stride
-            at = slice(p * by, (p + 1) * by)
-            zm, zp = received([r[at, :].astype(f32) for r in zrefs], iz, nz)
-            put(base + 2, jnp.concatenate([zm, own[at, :].astype(f32), zp], axis=1))
-            put(base, ym[2 * p : 2 * p + 2], y_lo)
-            put(base + by + 2, yp[2 * p : 2 * p + 2], y_hi)
+        for slot, plane in ((2, 0), (3, 1), (4, bx - 2), (5, bx - 1)):
+            put_plane(grid, slot * stride, own, zrefs, yrefs, plane, shape, counts)
         xm, xp = received([r[...].astype(f32) for r in xrefs], ix, nx)
-        for face, first, ok in ((xm, 0, x_lo), (xp, bx + 2, x_hi)):
+        for face, first, ok in ((xm, 0, ix > 0), (xp, 6, ix < nx - 1)):
+            good = z_ok & ok
             for q in range(2):
                 base = (first + q) * stride
-                put(base + 2, face[q * by : (q + 1) * by], ok)
+                grid[base + 2 : base + 2 + by, :] = jnp.where(good, face[q * by : (q + 1) * by], 0.0)
                 at = 2 * by + 2 * q
-                low = received([face[at + 4 * i : at + 4 * i + 2] for i in range(yparts)], iy, ny)
-                put(base, low[0], ok & y_lo)
-                put(base + by + 2, low[1], ok & y_hi)
-        outs = banded_conv(grid, w, sums, blocks, tall, stride, chan)
-        encoded = jnp.maximum(jnp.concatenate(outs, axis=1), 0.0).astype(bf16)
+                ym, yp = received([face[at + 4 * i : at + 4 * i + 2] for i in range(yparts)], iy, ny)
+                grid[base : base + 2, :] = jnp.where(good & (iy > 0), ym, 0.0)
+                grid[base + by + 2 : base + by + 4, :] = jnp.where(good & (iy < ny - 1), yp, 0.0)
+        outs = banded_conv(
+            grid, w, sums, (bz + 2) // OUT_Z, [0, 4 * stride], 2 * stride, stride, chan
+        )
+        encoded = relu_rows(outs)
         enc[...] = encoded
-        cells = encoded.astype(f32)
+        first_plane = encoded[stride : 2 * stride].astype(f32)
+        last_plane = encoded[2 * stride : 3 * stride].astype(f32)
         rows_of = {}
         for i in range(ti):
             features = {}
             for a in range(2):
-                x0 = 1 + 8 * i + 4 * a
-                acc = cells[x0 * stride : (x0 + 1) * stride]
-                for q in range(1, 4):
-                    acc = acc + cells[(x0 + q) * stride : (x0 + q + 1) * stride]
+                group = 2 * i + a
+                acc = part_ref[group * stride : (group + 1) * stride, :]
+                if group == 0:
+                    acc = acc + first_plane
+                if group == groups - 1:
+                    acc = acc + last_plane
                 for g in range(2 * tk):
                     at = (1 + 4 * g) * chan
                     plane_sum[g] = acc[:, at : at + 4 * chan]
@@ -255,18 +341,19 @@
             tok_copies[device] = own_tokens
 
     return call(
-        encode_rows,
+        encode_ends,
         (
             jax.ShapeDtypeStruct((tall, (bz + 2) * chan), bf16),
             jax.ShapeDtypeStruct((devices, tokens, width), f32),
         ),
         scratch=[
-            pltpu.VMEM(((bx + 4) * stride, lanes), f32),
+            pltpu.VMEM((8 * stride, lanes), f32),
             pltpu.VMEM((3, tall + 8, OUT_Z * chan), f32),
             pltpu.VMEM((2 * tk, stride, 4 * chan), f32),
         ],
-        operands=2 + zparts + yparts + xparts,
-    )(rows, *zgot, *ygot, *xgot, weights)
+        operands=3 + zparts + yparts + xparts,
+        limit=(16 if devices <= 64 else 32) << 20,
+    )(rows, *zgot, *ygot, *xgot, weights, partial)
 
 
 def sub_blocks(extent):
@@ -278,7 +365,7 @@
 
 
 def attend_and_join(
-    gathered, gain, q_weight, kv_weight, out_weight, upx, encoded, weights, shape, counts
+    gathered, gain, q_weight, kv_weight, out_weight, upx, inner, outer, weights, shape, counts
 ):
     bx, by, bz, chan = shape
     nx, ny, nz = counts
@@ -288,7 +375,17 @@
     tokens = ti * tj * tk
     width = 8 * chan
     every = gathered.shape[0] * tokens
-    asked = 27 * tokens
+    runs, place = [], {}
+    for dx in (-1, 0, 1):
+        for dy in (-1, 0, 1):
+            for dz in (-1, 0, 1):
+                for i in {-1: [ti - 1], 0: range(ti), 1: [0]}[dx]:
+                    for k in {-1: [tk - 1], 0: range(tk), 1: [0]}[dz]:
+                        j0, j1 = {-1: (tj - 1, tj), 0: (0, tj), 1: (0, 1)}[dy]
+                        runs.append(((dx, dy, dz), (i * tk + k) * tj + j0, j1 - j0))
+                        for j in range(j0, j1):
+                            place[dx, dy, dz, i, j, k] = len(place)
+    asked = -(-len(place) // 16) * 16
     head_size = width // HEADS
     wide = (bz + 2) * chan
     blocks = -(-bz // OUT_Z)
@@ -302,12 +399,11 @@
     for xi, (_, _, dx, i, _) in enumerate(xs):
         for zi, (dz, k, _) in enumerate(zs):
             for first, many, dy, j, _ in sub_blocks(by):
-                near = ((dx + 1) * 3 + dy + 1) * 3 + dz + 1
                 row = (xi * len(zs) + zi) * stride + first
-                pick[row : row + many, near * tokens + (i * tk + k) * tj + j] = 1.0
+                pick[row : row + many, place[dx, dy, dz, i, j, k]] = 1.0
 
     def attend(
-        g, gain_ref, qw, kvw, ow, upx_ref, sel, enc, w, out, normed_all, mine, mine_n, grid, sums
+        g, gain_ref, qw, kvw, ow, upx_ref, sel, enc_in, enc_out, w, out, normed_all, mine, mine_n, grid, sums
     ):
         ix, iy, iz = (lax.axis_index(axis) for axis in AXES)
         t = g[...].reshape(every, width)
@@ -317,17 +413,23 @@
         normed_all[...] = normed.astype(f32)
         kv = jnp.dot(normed, kvw[...], preferred_element_type=f32).astype(bf16)
         keys, values = kv[:, :width], kv[:, width:]
-        near = 0
-        for dx in (-1, 0, 1):
-            x = jnp.clip(ix + dx, 0, nx - 1)
-            for dy in (-1, 0, 1):
+        blocks_of = {}
+        row = 0
+        for (dx, dy, dz), first, many in runs:
+            if (dx, dy, dz) not in blocks_of:
+                x = jnp.clip(ix + dx, 0, nx - 1)
                 y = jnp.clip(iy + dy, 0, ny - 1)
-                for dz in (-1, 0, 1):
-                    z = jnp.clip(iz + dz, 0, nz - 1)
-                    at = pl.multiple_of(((x * ny + y) * nz + z) * tokens, 8)
-                    mine[near * tokens : (near + 1) * tokens, :] = g[(x * ny + y) * nz + z]
-                    mine_n[near * tokens : (near + 1) * tokens, :] = normed_all[pl.ds(at, tokens), :]
-                    near += 1
+                z = jnp.clip(iz + dz, 0, nz - 1)
+                device = (x * ny + y) * nz + z
+                at = pl.multiple_of(device * tokens, 8)
+                blocks_of[dx, dy, dz] = g[device], normed_all[pl.ds(at, tokens), :]
+            block, normed_block = blocks_of[dx, dy, dz]
+            mine[row : row + many, :] = block[first : first + many]
+            mine_n[row : row + many, :] = normed_block[first : first + many]
+            row += many
+        if asked > row:
+            mine[row:, :] = jnp.zeros((asked - row, width), f32)
+            mine_n[row:, :] = jnp.zeros((asked - row, width), f32)
         q = jnp.dot(mine_n[...].astype(bf16), qw[...], preferred_element_type=f32).astype(bf16)
         lane = lax.broadcasted_iota(jnp.int32, (1, width), 1) // head_size
         attended = jnp.zeros((asked, width), f32)
@@ -374,9 +476,10 @@
                     good = ok & x_lo
                 if x == bx + 1:
                     good = ok & x_hi
-                cells = enc[x * stride : (x + 1) * stride, :].astype(f32)
+                ref, at = (enc_in, x - 2) if 2 <= x < bx else (enc_out, x if x < 2 else x - bx + 2)
+                cells = ref[at * stride : (at + 1) * stride, :].astype(f32)
                 grid[x * stride : (x + 1) * stride, :wide] = jnp.where(good, cells + upward, 0.0)
-        outs = banded_conv(grid, w, sums, blocks, low, stride, chan)
+        outs = banded_conv(grid, w, sums, blocks, [0], low, stride, chan)
         final = jnp.concatenate(outs, axis=1)[:, : bz * chan].astype(bf16)
         for x in range(bx):
             out[x] = final[x * stride : x * stride + by].reshape(by, bz, chan)
@@ -391,10 +494,10 @@
             pltpu.VMEM((tall, padded), f32),
             pltpu.VMEM((3, low + 8, OUT_Z * chan), f32),
         ],
-        operands=9,
+        operands=10,
         limit=min(60, 18 + 24 * every * asked // (1 << 20)) << 20,
     )(
-        gathered, gain, q_weight, kv_weight, out_weight, upx, jnp.asarray(pick, bf16), encoded, weights
+        gathered, gain, q_weight, kv_weight, out_weight, upx, jnp.asarray(pick, bf16), inner, outer, weights
     )
 
 
@@ -403,22 +506,16 @@
     bx, by, bz, chan = shape
     counts = tuple(lax.axis_size(axis) for axis in AXES)
     first_w, second_w, upx = band_weights(conv_in, conv_out, up_weight, chan)
-    zgot = exchange(
-        sends(
-            volume[:, :, :2].reshape(bx * by, 2 * chan),
-            volume[:, :, bz - 2 :].reshape(bx * by, 2 * chan),
-            lax.axis_index("gz"),
-            counts[2],
-        ),
-        "gz",
-    )
-    rows = pack_rows(volume)
+    rows, *zfaces = pack_rows(volume, counts)
+    zgot = exchange(zfaces, "gz")
+    rows, first_w, second_w, upx = lax.optimization_barrier((rows, first_w, second_w, upx))
     ygot = exchange(y_faces(rows, zgot, shape, counts), "gy")
     xgot = exchange(x_faces(rows, zgot, ygot, shape, counts), "gx")
-    encoded, copies = encode(rows, zgot, ygot, xgot, first_w, shape, counts)
+    inner, partial = encode_inner(rows, zgot, ygot, first_w, shape, counts)
+    outer, copies = encode_outer(rows, zgot, ygot, xgot, first_w, partial, shape, counts)
     gathered = lax.all_to_all(copies, AXES, 0, 0, tiled=True)
     return attend_and_join(
-        gathered, norm_gain[None], q_weight, kv_weight, out_weight, upx, encoded, second_w, shape, counts
+        gathered, norm_gain[None], q_weight, kv_weight, out_weight, upx, inner, outer, second_w, shape, counts
     )
 
 

time: 41.2 us -> 41.1 us (level)
  Pallas kernels: 8.48 us -> 11.4 us
  other arithmetic: 1.53 us -> 0 us
  waiting for transfers between devices: 6.79 us -> 6.06 us
  local copies, waits for them, and re-layouts: 1.49 us -> 0.93 us
    pallas_call x2 -> x3, Pallas kernels: 2.62 us -> 4.4 us  [the longest x1 2.03 us: pack_rows(): pl.pallas_call(pack, out_shape=(jax.ShapeDtypeStruct((bx * by, bz * chan)...]
    select_n x1 -> x0, other arithmetic: 1.53 us -> none  [sends(): return [jnp.where(even, high, low), jnp.where(even, low, high)]]
    pallas_call x1, Pallas kernels: 4.72 us -> 5.83 us  [attend_and_join(): call(attend, jax.ShapeDtypeStruct(shape, bf16), scratch=[pltpu.VMEM((ever...]
    ppermute x2, waiting for transfers between devices: 4.83 us -> 4.35 us  [exchange(): lax.ppermute(faces[1], axis, [(i, (i + 1) % count if i % 2 else (i - 1) %...]
    unnamed x18 -> x16, local copies, waits for them, and re-layouts: 1.27 us -> 0.93 us
  transfers between devices with their start and end apart: 5 -> 5, of which waited for: 4 -> 4; matrix products, arithmetic and copies ran while one was open for 0% -> 0% of each run, Pallas kernels for 3% -> 5%
where the time goes in v3:
time: 41.1 us; the launch traced here: 41 us
  blocking collectives  13.8 us (34%)
  Pallas kernels  11.4 us (28%)
  starting transfers between devices  8.71 us (21%)
  waiting for transfers between devices  6.06 us (15%)
  local copies, waits for them, and re-layouts  0.93 us (2%)
    all_to_all x1, blocking collectives, on_device(): gathered = lax.all_to_all(copies, AXES, 0, 0, tiled=True)  13.8 us
    pallas_call x1, Pallas kernels, attend_and_join(): call(attend, jax.ShapeDtypeStruct(shape, bf16), scratch=[pltpu.VMEM((ever...  5.83 us
    ppermute x2, starting transfers between devices, exchange(): lax.ppermute(faces[0], axis, [(i, i ^ 1) for i in range(count)])  4.67 us
    ppermute x2, waiting for transfers between devices, exchange(): lax.ppermute(faces[1], axis, [(i, (i + 1) % count if i % 2 else (i - 1) %...  4.35 us
    ppermute x2, starting transfers between devices, exchange(): lax.ppermute(faces[1], axis, [(i, (i + 1) % count if i % 2 else (i - 1) %...  3.97 us
    pallas_call x1, Pallas kernels, pack_rows(): pl.pallas_call(pack, out_shape=(jax.ShapeDtypeStruct((bx * by, bz * chan)...  2.03 us
    pallas_call x1, Pallas kernels, encode_inner(): call(encode_middle, (jax.ShapeDtypeStruct((tall, (bz + 2) * chan), bf16),...  1.2 us
    ppermute x1, waiting for transfers between devices, exchange(): return [lax.ppermute(faces[0], axis, [(0, 1), (1, 0)])]  1.18 us
  transfers between devices with their start and end apart: 5, of which 4 were waited for; matrix products, arithmetic and copies ran while one was open for 0% of the time, Pallas kernels for 5%

profile of v3, /device:TPU:0, one launch (start us, length us, event | category | flops | bytes accessed | tf_op | source)
XLA Modules:
  0.0 41.0 jit_solution(15852645487310161419)
XLA Ops:
  0.0 2.0 %pack.1 = (bf16[256,512]{1,0:T(8,128)(2,1)S(1)}, bf16[128,128]{1,0:T(8,128)(2,1)S(1)}, bf16[128,128]{1,0:T(8,128)(2,1)S(1)}) custom-call(bf16[8,32,16,32]{3,2,1,0:T(8,128)(2,1)} %vol.1), custom_call_target="tpu_custom_call" | custom-call | tf_op jit(solution)/shard_map/pack/pallas_call | solution.py:127
  2.0 3.1 %collective-permute-start = (bf16[128,128]{1,0:T(8,128)(2,1)S(1)}, bf16[128,128]{1,0:T(8,128)(2,1)S(1)}, u32[]{:S(2)}, u32[]{:S(2)}) collective-permute-start(bf16[128,128]{1,0:T(8,128)(2,1)S(1)} %get-tuple-element.26), channel_id=1, source_target_pairs={{0,1},{1,0},{2,3},{3,2},{4,5},{5,4},{6,7},{7,6},{8,9},{9,8},{10,11... | collective-permute-start | bytes 98312 | tf_op jit(solution)/shard_map/ppermute | solution.py:45
  5.2 2.5 %collective-permute-start.1 = (bf16[128,128]{1,0:T(8,128)(2,1)S(1)}, bf16[128,128]{1,0:T(8,128)(2,1)S(1)}, u32[]{:S(2)}, u32[]{:S(2)}) collective-permute-start(bf16[128,128]{1,0:T(8,128)(2,1)S(1)} %get-tuple-element.27), channel_id=1, source_target_pairs={{0,3},{1,2},{2,1},{3,0},{4,7},{5,6},{6,5},{7,4},{8,11},{9,10},{10,... | collective-permute-start | bytes 98312 | tf_op jit(solution)/shard_map/ppermute | solution.py:46
  7.6 0.0 copy-done.2
  7.6 0.0 copy-done.1
  7.6 0.9 %copy-done.6 = bf16[256,256]{1,0:T(8,128)(2,1)S(1)} copy-done((bf16[256,256]{1,0:T(8,128)(2,1)S(1)}, bf16[256,256]{1,0:T(8,128)(2,1)}, u32[]{:S(2)}) %copy-start.6) | copy-done | bytes 131096
  8.5 0.9 %spread_weights.1 = (bf16[9,256,192]{2,1,0:T(8,128)(2,1)S(1)}, bf16[9,256,192]{2,1,0:T(8,128)(2,1)S(1)}, bf16[2,256,512]{2,1,0:T(8,128)(2,1)S(1)}) custom-call(bf16[9,96,32]{2,1,0:T(8,128)(2,1)S(1)} %bitcast.3, bf16[9,96,32]{2,1,0:T(8,128)(2,1)S(1)} %bitcast.4, bf16[256,256]{1,0:T(8,128)(2,1)S(1)} %copy-done.6), custom_call_target="tpu_custom_call" | custom-call | tf_op jit(solution)/shard_map/spread_weights/pallas_call | solution.py:93
  9.4 0.0 collective-permute-done.refs_0_
  9.5 1.4 %collective-permute-done.1.refs_1_ = bf16[128,128]{1,0:T(8,128)(2,1)S(1)} collective-permute-done((bf16[128,128]{1,0:T(8,128)(2,1)S(1)}, bf16[128,128]{1,0:T(8,128)(2,1)S(1)}, u32[]{:S(2)}, u32[]{:S(2)}) %collective-permute-start.1) | collective-permute-done | bytes 32800 | tf_op jit(solution)/shard_map/ppermute | solution.py:46
  10.9 0.1 y_face.1
  11.0 0.1 collective-permute-start.2
  11.1 1.2 %collective-permute-done.2.refs_2_ = bf16[16,640]{1,0:T(8,128)(2,1)S(1)} collective-permute-done((bf16[16,640]{1,0:T(8,128)(2,1)S(1)}, bf16[16,640]{1,0:T(8,128)(2,1)S(1)}, u32[]{:S(2)}, u32[]{:S(2)}) %collective-permute-start.2) | collective-permute-done | bytes 20512 | tf_op jit(solution)/shard_map/ppermute | solution.py:37
  12.2 0.1 x_face.1
  12.4 1.6 %collective-permute-start.3 = (bf16[68,640]{1,0:T(8,128)(2,1)S(1)}, bf16[68,640]{1,0:T(8,128)(2,1)S(1)}, u32[]{:S(2)}, u32[]{:S(2)}) collective-permute-start(bf16[68,640]{1,0:T(8,128)(2,1)S(1)} %get-tuple-element.28), channel_id=1, source_target_pairs={{0,8},{8,0},{16,24},{24,16},{1,9},{9,1},{17,25},{25,17},{2,10},{10... | collective-permute-start | bytes 261128 | tf_op jit(solution)/shard_map/ppermute | solution.py:45
  13.9 1.5 %collective-permute-start.4 = (bf16[68,640]{1,0:T(8,128)(2,1)S(1)}, bf16[68,640]{1,0:T(8,128)(2,1)S(1)}, u32[]{:S(2)}, u32[]{:S(2)}) collective-permute-start(bf16[68,640]{1,0:T(8,128)(2,1)S(1)} %get-tuple-element.29), channel_id=1, source_target_pairs={{0,24},{8,16},{16,8},{24,0},{1,25},{9,17},{17,9},{25,1},{2,26},{10... | collective-permute-start | bytes 261128 | tf_op jit(solution)/shard_map/ppermute | solution.py:46
  15.4 1.2 %encode_middle.1 = (bf16[240,576]{1,0:T(8,128)(2,1)S(1)}, f32[80,576]{1,0:T(8,128)S(1)}) custom-call(bf16[256,512]{1,0:T(8,128)(2,1)S(1)} %get-tuple-element.25.own, bf16[128,128]{1,0:T(8,128)(2,1)S(1)} %collective-permute-done.refs_0_, bf16[128,128]{1,0:T(8,128)(2,1)S(1)} %collective-permute-done.1.refs_1_, ...), custom_call_target="tpu_custom_call" | custom-call | tf_op jit(solution)/shard_map/encode_middle/pallas_call | solution.py:257
  16.6 0.5 %collective-permute-done.3.refs_3_ = bf16[68,640]{1,0:T(8,128)(2,1)S(1)} collective-permute-done((bf16[68,640]{1,0:T(8,128)(2,1)S(1)}, bf16[68,640]{1,0:T(8,128)(2,1)S(1)}, u32[]{:S(2)}, u32[]{:S(2)}) %collective-permute-start.3) | collective-permute-done | bytes 87072 | tf_op jit(solution)/shard_map/ppermute | solution.py:45
  17.2 2.9 %collective-permute-done.4.refs_4_ = bf16[68,640]{1,0:T(8,128)(2,1)S(1)} collective-permute-done((bf16[68,640]{1,0:T(8,128)(2,1)S(1)}, bf16[68,640]{1,0:T(8,128)(2,1)S(1)}, u32[]{:S(2)}, u32[]{:S(2)}) %collective-permute-start.4) | collective-permute-done | bytes 87072 | tf_op jit(solution)/shard_map/ppermute | solution.py:46
  20.1 0.0 copy-start.7
  20.1 1.2 %encode_ends.1 = (bf16[160,576]{1,0:T(8,128)(2,1)S(1)}, f32[32,8,256]{2,1,0:T(8,128)S(1)}) custom-call(bf16[256,512]{1,0:T(8,128)(2,1)S(1)} %get-tuple-element.25.own, bf16[128,128]{1,0:T(8,128)(2,1)S(1)} %collective-permute-done.refs_0_, bf16[128,128]{1,0:T(8,128)(2,1)S(1)} %collective-permute-done.1.refs_1_, ...), custom_call_target="tpu_custom_call" | custom-call | tf_op jit(solution)/shard_map/encode_ends/pallas_call | solution.py:343
  21.3 13.8 %all_to_all.5.g = f32[32,8,256]{2,1,0:T(8,128)S(1)} all-to-all(f32[32,8,256]{2,1,0:T(8,128)S(1)} %get-tuple-element.32), channel_id=1, replica_groups=mesh['gx'=4,'gy'=2,'gz'=4] {'gx','gy','gz'}, dimensions={0} | all-to-all | bytes 524288 | tf_op jit(solution)/shard_map/all_to_all | solution.py:516
  35.1 0.0 copy-done.5
  35.1 0.0 copy-done.7
  35.1 5.8 %attend.1 = bf16[8,32,16,32]{3,2,1,0:T(8,128)(2,1)} custom-call(f32[32,8,256]{2,1,0:T(8,128)S(1)} %all_to_all.5.g, f32[1,256]{1,0:T(1,128)S(1)} %bitcast.5, bf16[256,256]{1,0:T(8,128)(2,1)S(1)} %copy-done.4, bf16[256,512]{1,0:T(8,128)(2,1)S(1)} %copy-done, bf16[256,256]{1,0:T(8,128)(2,1)S(1)} %copy-done.5, ...), custom_call_target="tpu_custom_call" | custom-call | tf_op jit(solution)/shard_map/attend/pallas_call | solution.py:487
  (10 shorter events, 0.0 us)
Async XLA Ops:
  0.0 7.6 %copy-start.2 = (bf16[3,3,3,32,32]{4,3,2,1,0:T(8,128)(2,1)S(1)}, bf16[3,3,3,32,32]{4,3,2,1,0:T(8,128)(2,1)}, u32[]{:S(2)}) copy-start(bf16[3,3,3,32,32]{4,3,2,1,0:T(8,128)(2,1)} %param.11) | copy-start | bytes 165892
  0.0 7.6 %copy-start.1 = (bf16[3,3,3,32,32]{4,3,2,1,0:T(8,128)(2,1)S(1)}, bf16[3,3,3,32,32]{4,3,2,1,0:T(8,128)(2,1)}, u32[]{:S(2)}) copy-start(bf16[3,3,3,32,32]{4,3,2,1,0:T(8,128)(2,1)} %param.10) | copy-start | bytes 165892
  2.0 7.4 %collective-permute-start = (bf16[128,128]{1,0:T(8,128)(2,1)S(1)}, bf16[128,128]{1,0:T(8,128)(2,1)S(1)}, u32[]{:S(2)}, u32[]{:S(2)}) collective-permute-start(bf16[128,128]{1,0:T(8,128)(2,1)S(1)} %get-tuple-element.26), channel_id=1, source_target_pairs={{0,1},{1,0},{2,3},{3,2},{4,5},{5,4},{6,7},{7,6},{8,9},{9,8},{10,11... | collective-permute-start | bytes 98312 | tf_op jit(solution)/shard_map/ppermute | solution.py:45
  5.2 5.7 %collective-permute-start.1 = (bf16[128,128]{1,0:T(8,128)(2,1)S(1)}, bf16[128,128]{1,0:T(8,128)(2,1)S(1)}, u32[]{:S(2)}, u32[]{:S(2)}) collective-permute-start(bf16[128,128]{1,0:T(8,128)(2,1)S(1)} %get-tuple-element.27), channel_id=1, source_target_pairs={{0,3},{1,2},{2,1},{3,0},{4,7},{5,6},{6,5},{7,4},{8,11},{9,10},{10,... | collective-permute-start | bytes 98312 | tf_op jit(solution)/shard_map/ppermute | solution.py:46
  7.6 0.9 %copy-start.6 = (bf16[256,256]{1,0:T(8,128)(2,1)S(1)}, bf16[256,256]{1,0:T(8,128)(2,1)}, u32[]{:S(2)}) copy-start(bf16[256,256]{1,0:T(8,128)(2,1)} %up.1) | copy-start | bytes 393220
  11.0 1.3 %collective-permute-start.2 = (bf16[16,640]{1,0:T(8,128)(2,1)S(1)}, bf16[16,640]{1,0:T(8,128)(2,1)S(1)}, u32[]{:S(2)}, u32[]{:S(2)}) collective-permute-start(bf16[16,640]{1,0:T(8,128)(2,1)S(1)} %y_face.1), channel_id=1, source_target_pairs={{0,4},{4,0},{1,5},{5,1},{2,6},{6,2},{3,7},{7,3},{8,12},{12,8},{9,1... | collective-permute-start | bytes 61448 | tf_op jit(solution)/shard_map/ppermute | solution.py:37
  12.4 4.8 %collective-permute-start.3 = (bf16[68,640]{1,0:T(8,128)(2,1)S(1)}, bf16[68,640]{1,0:T(8,128)(2,1)S(1)}, u32[]{:S(2)}, u32[]{:S(2)}) collective-permute-start(bf16[68,640]{1,0:T(8,128)(2,1)S(1)} %get-tuple-element.28), channel_id=1, source_target_pairs={{0,8},{8,0},{16,24},{24,16},{1,9},{9,1},{17,25},{25,17},{2,10},{10... | collective-permute-start | bytes 261128 | tf_op jit(solution)/shard_map/ppermute | solution.py:45
  13.9 6.2 %collective-permute-start.4 = (bf16[68,640]{1,0:T(8,128)(2,1)S(1)}, bf16[68,640]{1,0:T(8,128)(2,1)S(1)}, u32[]{:S(2)}, u32[]{:S(2)}) collective-permute-start(bf16[68,640]{1,0:T(8,128)(2,1)S(1)} %get-tuple-element.29), channel_id=1, source_target_pairs={{0,24},{8,16},{16,8},{24,0},{1,25},{9,17},{17,9},{25,1},{2,26},{10... | collective-permute-start | bytes 261128 | tf_op jit(solution)/shard_map/ppermute | solution.py:46
  20.1 15.0 %copy-start = (bf16[256,512]{1,0:T(8,128)(2,1)S(1)}, bf16[256,512]{1,0:T(8,128)(2,1)}, u32[]{:S(2)}) copy-start(bf16[256,512]{1,0:T(8,128)(2,1)} %kvw.1) | copy-start | bytes 786436
  20.1 15.0 %copy-start.3 = (bf16[640,80]{1,0:T(8,128)(2,1)S(1)}, bf16[640,80]{1,0:T(8,128)(2,1)}, u32[]{:S(2)}) copy-start(bf16[640,80]{1,0:T(8,128)(2,1)} %constant.2.clone.sel) | copy-start | bytes 307204
  20.1 15.0 %copy-start.4 = (bf16[256,256]{1,0:T(8,128)(2,1)S(1)}, bf16[256,256]{1,0:T(8,128)(2,1)}, u32[]{:S(2)}) copy-start(bf16[256,256]{1,0:T(8,128)(2,1)} %qw.1) | copy-start | bytes 393220
  20.1 15.0 %copy-start.5 = (bf16[256,256]{1,0:T(8,128)(2,1)S(1)}, bf16[256,256]{1,0:T(8,128)(2,1)}, u32[]{:S(2)}) copy-start(bf16[256,256]{1,0:T(8,128)(2,1)} %ow.1) | copy-start | bytes 393220
  20.1 15.0 %copy-start.7 = (f32[256]{0:T(256)S(1)}, f32[256]{0:T(256)}, u32[]{:S(2)}) copy-start(f32[256]{0:T(256)} %param.12) | copy-start | bytes 3076

commit v4 on v3

--- a/solution.py
+++ b/solution.py
@@ -11,6 +11,7 @@
 AXES = ("gx", "gy", "gz")
 OUT_Z = 6
 IN_Z = 8
+GROUPS = 2
 
 f32 = jnp.float32
 bf16 = jnp.bfloat16
@@ -60,7 +61,7 @@
     return jnp.where(even, got[1], got[0]), jnp.where(even, got[0], got[1])
 
 
-def call(body, outs, scratch=(), operands=0, limit=16 << 20):
+def call(body, outs, scratch=(), operands=0, limit=16 << 20, **more):
     return pl.pallas_call(
         body,
         out_shape=outs,
@@ -68,6 +69,7 @@
         scratch_shapes=list(scratch),
         compiler_params=pltpu.CompilerParams(vmem_limit_bytes=limit),
         name=body.__name__,
+        **more,
     )
 
 
@@ -101,38 +103,67 @@
     )
 
 
-def pack_rows(volume, counts):
+def y_faces(volume, counts):
     bx, by, bz, chan = volume.shape
-    many = 1 if counts[2] <= 2 else 2
-    half = bx * by // 2
-
-    def pack(vol, rows, *refs):
+    many = 1 if counts[1] <= 2 else 2
+
+    def y_face(vol, *refs):
         outs, (here, arrived) = refs[:many], refs[many:]
-        copies = [pltpu.make_async_copy(vol.at[x], here.at[x], arrived.at[x]) for x in range(bx)]
+        copies = [
+            pltpu.make_async_copy(vol.at[:, pl.ds(y, 2)], here.at[side], arrived.at[side])
+            for side, y in enumerate((0, by - 2))
+        ]
         for copy in copies:
             copy.start()
-        for x in range(bx):
-            copies[x].wait()
-            rows[x * by : (x + 1) * by, :] = here[x].reshape(by, bz * chan)
-
-        def beside(start):
-            return jnp.concatenate(
-                [rows[:half, start : start + 2 * chan], rows[half:, start : start + 2 * chan]], axis=1
-            )
-
-        faces = sends(beside(0), beside((bz - 2) * chan), lax.axis_index("gz"), counts[2])
-        for ref, face in zip(outs, faces):
-            ref[...] = face
+        for copy in copies:
+            copy.wait()
+        low, high = (here[side].astype(f32).reshape(bx * 2, bz * chan) for side in range(2))
+        for ref, face in zip(outs, sends(low, high, lax.axis_index("gy"), counts[1])):
+            ref[...] = face.astype(bf16)
 
     return pl.pallas_call(
-        pack,
-        out_shape=(jax.ShapeDtypeStruct((bx * by, bz * chan), bf16),)
-        + (jax.ShapeDtypeStruct((half, 4 * chan), bf16),) * many,
+        y_face,
+        out_shape=(jax.ShapeDtypeStruct((bx * 2, bz * chan), bf16),) * many,
         in_specs=[pl.BlockSpec(memory_space=pltpu.HBM)],
-        scratch_shapes=[pltpu.VMEM(volume.shape, bf16), pltpu.SemaphoreType.DMA((bx,))],
+        scratch_shapes=[pltpu.VMEM((2, bx, 2, bz, chan), bf16), pltpu.SemaphoreType.DMA((2,))],
         compiler_params=pltpu.CompilerParams(vmem_limit_bytes=16 << 20),
-        name="pack",
+        name="y_face",
     )(pltpu.with_memory_space_constraint(volume, pltpu.HBM))
+
+
+def pack_rows(volume):
+    bx, by, bz, chan = volume.shape
+
+    def pack(vol, rows):
+        rows[...] = vol[...].reshape(bx * by, bz * chan)
+
+    return call(pack, jax.ShapeDtypeStruct((bx * by, bz * chan), bf16), operands=1)(volume)
+
+
+def z_faces(rows, ygot, shape, counts):
+    bx, by, bz, chan = shape
+    many = 1 if counts[2] <= 2 else 2
+    yparts = len(ygot)
+    half = bx * by // 2
+
+    def z_face(own, *refs):
+        yvals, outs = [r[...].astype(f32) for r in refs[:yparts]], refs[yparts:]
+
+        def face(start):
+            sides = []
+            for side in range(2):
+                at = slice(start, start + 2 * chan)
+                body = own[side * half : (side + 1) * half, at].astype(f32)
+                edges = [v[side * bx : (side + 1) * bx, at] for v in yvals]
+                sides.append(jnp.concatenate([body] + edges, axis=0))
+            return jnp.concatenate(sides, axis=1)
+
+        faces = sends(face(0), face((bz - 2) * chan), lax.axis_index("gz"), counts[2])
+        for ref, value in zip(outs, faces):
+            ref[...] = value.astype(bf16)
+
+    out = jax.ShapeDtypeStruct((half + bx * yparts, 4 * chan), bf16)
+    return call(z_face, (out,) * many, operands=1 + yparts)(rows, *ygot)
 
 
 def full_rows(own, zrefs, plane, shape, count):
@@ -145,26 +176,22 @@
     return jnp.concatenate([zm, own[plane * by : (plane + 1) * by, :].astype(f32), zp], axis=1)
 
 
-def y_faces(rows, zgot, shape, counts):
-    bx, by, bz, chan = shape
-    lanes = (bz + 4) * chan
-    many = 1 if counts[1] <= 2 else 2
-    parts = len(zgot)
-
-    def y_face(own, *refs):
-        low, high = [], []
-        for x in range(bx):
-            full = full_rows(own, refs[:parts], x, shape, counts[2])
-            low.append(full[:2])
-            high.append(full[by - 2 :])
-        faces = sends(
-            jnp.concatenate(low, axis=0), jnp.concatenate(high, axis=0), lax.axis_index("gy"), counts[1]
-        )
-        for ref, face in zip(refs[parts:], faces):
-            ref[...] = face.astype(bf16)
-
-    face = jax.ShapeDtypeStruct((bx * 2, lanes), bf16)
-    return call(y_face, (face,) * many, operands=1 + parts)(rows, *zgot)
+def full_edges(yrefs, zrefs, plane, shape, count):
+    bx, by, bz, chan = shape
+    side, at = divmod(plane, bx // 2)
+    out = []
+    for i, ref in enumerate(yrefs):
+        first = i * bx + 2 * at
+        parts = [
+            r[bx * by // 2 :, :].astype(f32)[
+                first : first + 2, side * 2 * chan : (side + 1) * 2 * chan
+            ]
+            for r in zrefs
+        ]
+        zm, zp = received(parts, lax.axis_index("gz"), count)
+        own = ref[...].astype(f32)[2 * plane : 2 * plane + 2]
+        out.append(jnp.concatenate([zm, own, zp], axis=1))
+    return out
 
 
 def x_faces(rows, zgot, ygot, shape, counts):
@@ -179,8 +206,10 @@
 
         def face(first):
             body = [full_rows(own, zrefs, first + q, shape, counts[2]) for q in range(2)]
-            edges = [r[...].astype(f32)[2 * first : 2 * first + 4] for r in yrefs]
-            return jnp.concatenate(body + edges, axis=0)
+            edges = [full_edges(yrefs, zrefs, first + q, shape, counts[2]) for q in range(2)]
+            return jnp.concatenate(
+                body + [edges[q][i] for i in range(yparts) for q in range(2)], axis=0
+            )
 
         for ref, value in zip(outs, sends(face(0), face(bx - 2), lax.axis_index("gx"), counts[0])):
             ref[...] = value.astype(bf16)
@@ -189,7 +218,7 @@
     return call(x_face, (face,) * many, operands=1 + zparts + yparts)(rows, *zgot, *ygot)
 
 
-def banded_conv(source, weights, sums, blocks, starts, rows, stride, chan):
+def banded_conv(source, weights, sums, blocks, starts, rows, stride, chan, first_sum=0):
     outs = []
     tall = rows * len(starts)
     for block in range(blocks):
@@ -206,8 +235,11 @@
                     piece.astype(bf16), weights[dx * 3 + dy], preferred_element_type=f32
                 )
                 total = part if total is None else total + part
-            sums[dy, :tall, :] = total
-        outs.append(sums[0, 0:tall, :] + sums[1, 1 : tall + 1, :] + sums[2, 2 : tall + 2, :])
+            sums[first_sum + block * 3 + dy, :tall, :] = total
+        at = first_sum + block * 3
+        outs.append(
+            sums[at, 0:tall, :] + sums[at + 1, 1 : tall + 1, :] + sums[at + 2, 2 : tall + 2, :]
+        )
     return outs
 
 
@@ -219,9 +251,7 @@
     z_ok = ((lane >= 2 * chan) | (iz > 0)) & ((lane < (bz + 2) * chan) | (iz < nz - 1))
     full = full_rows(own, zrefs, plane, shape, nz)
     grid[row + 2 : row + 2 + by, :] = jnp.where(z_ok, full, 0.0)
-    ym, yp = received(
-        [r[...].astype(f32)[2 * plane : 2 * plane + 2] for r in yrefs], iy, ny
-    )
+    ym, yp = received(full_edges(yrefs, zrefs, plane, shape, nz), iy, ny)
     grid[row : row + 2, :] = jnp.where(z_ok & (iy > 0), ym, 0.0)
     grid[row + by + 2 : row + by + 4, :] = jnp.where(z_ok & (iy < ny - 1), yp, 0.0)
 
@@ -262,7 +292,7 @@
         ),
         scratch=[
             pltpu.VMEM((bx * stride, lanes), f32),
-            pltpu.VMEM((3, tall + 8, OUT_Z * chan), f32),
+            pltpu.VMEM((3 * ((bz + 2) // OUT_Z), tall + 8, OUT_Z * chan), f32),
         ],
         operands=2 + zparts + yparts,
     )(rows, *zgot, *ygot, weights)
@@ -348,7 +378,7 @@
         ),
         scratch=[
             pltpu.VMEM((8 * stride, lanes), f32),
-            pltpu.VMEM((3, tall + 8, OUT_Z * chan), f32),
+            pltpu.VMEM((3 * ((bz + 2) // OUT_Z), tall + 8, OUT_Z * chan), f32),
             pltpu.VMEM((2 * tk, stride, 4 * chan), f32),
         ],
         operands=3 + zparts + yparts + xparts,
@@ -370,7 +400,8 @@
     bx, by, bz, chan = shape
     nx, ny, nz = counts
     stride = by + 8
-    tall, low = (bx + 2) * stride, bx * stride
+    tall = (bx + 2) * stride
+    planes = bx // GROUPS
     ti, tj, tk = bx // 8, by // 8, bz // 8
     tokens = ti * tj * tk
     width = 8 * chan
@@ -403,7 +434,7 @@
                 pick[row : row + many, place[dx, dy, dz, i, j, k]] = 1.0
 
     def attend(
-        g, gain_ref, qw, kvw, ow, upx_ref, sel, enc_in, enc_out, w, out, normed_all, mine, mine_n, grid, sums
+        g, gain_ref, qw, kvw, ow, upx_ref, sel, enc_in, enc_out, w, out, normed_all, mine, mine_n, grid, sums, done, sent
     ):
         ix, iy, iz = (lax.axis_index(axis) for axis in AXES)
         t = g[...].reshape(every, width)
@@ -432,18 +463,19 @@
             mine_n[row:, :] = jnp.zeros((asked - row, width), f32)
         q = jnp.dot(mine_n[...].astype(bf16), qw[...], preferred_element_type=f32).astype(bf16)
         lane = lax.broadcasted_iota(jnp.int32, (1, width), 1) // head_size
+        stacked = jnp.concatenate(
+            [jnp.where(lane == h, q, jnp.zeros_like(q)) for h in range(HEADS)], axis=0
+        )
+        scores = (
+            lax.dot_general(stacked, keys, (((1,), (1,)), ((), ())), preferred_element_type=f32)
+            * head_size ** (-0.5)
+        )
+        e = jnp.exp(scores - jnp.max(scores, axis=1, keepdims=True))
+        total = jnp.sum(e, axis=1, keepdims=True)
+        ratio = jnp.dot(e.astype(bf16), values, preferred_element_type=f32) / total
         attended = jnp.zeros((asked, width), f32)
         for h in range(HEADS):
-            here = lane == h
-            q_h = jnp.where(here, q, jnp.zeros_like(q))
-            scores = (
-                lax.dot_general(q_h, keys, (((1,), (1,)), ((), ())), preferred_element_type=f32)
-                * head_size ** (-0.5)
-            )
-            e = jnp.exp(scores - jnp.max(scores, axis=1, keepdims=True))
-            total = jnp.sum(e, axis=1, keepdims=True)
-            num = jnp.dot(e.astype(bf16), values, preferred_element_type=f32)
-            attended = jnp.where(here, num / total, attended)
+            attended = jnp.where(lane == h, ratio[h * asked : (h + 1) * asked], attended)
         mixture = (
             mine[...] + jnp.dot(attended.astype(bf16), ow[...], preferred_element_type=f32)
         ).astype(bf16)
@@ -479,10 +511,20 @@
                 ref, at = (enc_in, x - 2) if 2 <= x < bx else (enc_out, x if x < 2 else x - bx + 2)
                 cells = ref[at * stride : (at + 1) * stride, :].astype(f32)
                 grid[x * stride : (x + 1) * stride, :wide] = jnp.where(good, cells + upward, 0.0)
-        outs = banded_conv(grid, w, sums, blocks, [0], low, stride, chan)
-        final = jnp.concatenate(outs, axis=1)[:, : bz * chan].astype(bf16)
-        for x in range(bx):
-            out[x] = final[x * stride : x * stride + by].reshape(by, bz, chan)
+        copies = []
+        for part in range(GROUPS):
+            first = part * planes
+            outs = banded_conv(
+                grid, w, sums, blocks, [first * stride], planes * stride, stride, chan, part * 3 * blocks
+            )
+            final = jnp.concatenate(outs, axis=1)[:, : bz * chan].astype(bf16)
+            for x in range(planes):
+                done[first + x] = final[x * stride : x * stride + by].reshape(by, bz, chan)
+            span = pl.ds(first, planes)
+            copies.append(pltpu.make_async_copy(done.at[span], out.at[span], sent.at[part]))
+            copies[-1].start()
+        for copy in copies:
+            copy.wait()
 
     return call(
         attend,
@@ -492,10 +534,13 @@
             pltpu.VMEM((asked, width), f32),
             pltpu.VMEM((asked, width), f32),
             pltpu.VMEM((tall, padded), f32),
-            pltpu.VMEM((3, low + 8, OUT_Z * chan), f32),
+            pltpu.VMEM((GROUPS * 3 * blocks, planes * stride + 8, OUT_Z * chan), f32),
+            pltpu.VMEM(shape, bf16),
+            pltpu.SemaphoreType.DMA((GROUPS,)),
         ],
+        out_specs=pl.BlockSpec(memory_space=pltpu.HBM),
         operands=10,
-        limit=min(60, 18 + 24 * every * asked // (1 << 20)) << 20,
+        limit=min(60, 18 + 16 * HEADS * every * asked // (1 << 20)) << 20,
     )(
         gathered, gain, q_weight, kv_weight, out_weight, upx, jnp.asarray(pick, bf16), inner, outer, weights
     )
@@ -506,10 +551,10 @@
     bx, by, bz, chan = shape
     counts = tuple(lax.axis_size(axis) for axis in AXES)
     first_w, second_w, upx = band_weights(conv_in, conv_out, up_weight, chan)
-    rows, *zfaces = pack_rows(volume, counts)
-    zgot = exchange(zfaces, "gz")
+    ygot = exchange(y_faces(volume, counts), "gy")
+    rows = pack_rows(volume)
+    zgot = exchange(z_faces(rows, ygot, shape, counts), "gz")
     rows, first_w, second_w, upx = lax.optimization_barrier((rows, first_w, second_w, upx))
-    ygot = exchange(y_faces(rows, zgot, shape, counts), "gy")
     xgot = exchange(x_faces(rows, zgot, ygot, shape, counts), "gx")
     inner, partial = encode_inner(rows, zgot, ygot, first_w, shape, counts)
     outer, copies = encode_outer(rows, zgot, ygot, xgot, first_w, partial, shape, counts)

time: 41.1 us -> 38.1 us (0.927)
  Pallas kernels: 11.4 us -> 9.49 us
  local copies, waits for them, and re-layouts: 0.93 us -> 0.04 us
  waiting for transfers between devices: 6.06 us -> 5.47 us
    pallas_call x1, Pallas kernels: 5.83 us -> 4.4 us  [attend_and_join(): call(attend, jax.ShapeDtypeStruct(shape, bf16), scratch=[pltpu.VMEM((ever...]
    unnamed x16 -> x18, local copies, waits for them, and re-layouts: 0.93 us -> 0.04 us
    ppermute x1, waiting for transfers between devices: 1.18 us -> 0.38 us  [exchange(): return [lax.ppermute(faces[0], axis, [(0, 1), (1, 0)])]]
    ppermute x2, waiting for transfers between devices: 0.54 us -> 1.2 us  [exchange(): lax.ppermute(faces[0], axis, [(i, i ^ 1) for i in range(count)])]
    ppermute x1, starting transfers between devices: 0.07 us -> 0.57 us  [exchange(): return [lax.ppermute(faces[0], axis, [(0, 1), (1, 0)])]]
    pallas_call x2 -> x3, Pallas kernels: 2.14 us -> 1.68 us  [the longest x1 1.14 us: y_faces(): pl.pallas_call(y_face, out_shape=(jax.ShapeDtypeStruct((bx * 2, bz * chan...]
    ppermute x2, waiting for transfers between devices: 4.35 us -> 3.89 us  [exchange(): lax.ppermute(faces[1], axis, [(i, (i + 1) % count if i % 2 else (i - 1) %...]
  transfers between devices with their start and end apart: 5 -> 5, of which waited for: 4 -> 4; matrix products, arithmetic and copies ran while one was open for 0% -> 0% of each run, Pallas kernels for 5% -> 7%
where the time goes in v4:
time: 38.1 us; the launch traced here: 38 us
  blocking collectives  13.8 us (36%)
  Pallas kernels  9.49 us (25%)
  starting transfers between devices  9.06 us (24%)
  waiting for transfers between devices  5.47 us (14%)
    all_to_all x1, blocking collectives, on_device(): gathered = lax.all_to_all(copies, AXES, 0, 0, tiled=True)  13.8 us
    ppermute x2, starting transfers between devices, exchange(): lax.ppermute(faces[0], axis, [(i, i ^ 1) for i in range(count)])  4.53 us
    pallas_call x1, Pallas kernels, attend_and_join(): call(attend, jax.ShapeDtypeStruct(shape, bf16), scratch=[pltpu.VMEM((ever...  4.4 us
    ppermute x2, starting transfers between devices, exchange(): lax.ppermute(faces[1], axis, [(i, (i + 1) % count if i % 2 else (i - 1) %...  3.97 us
    ppermute x2, waiting for transfers between devices, exchange(): lax.ppermute(faces[1], axis, [(i, (i + 1) % count if i % 2 else (i - 1) %...  3.89 us
    ppermute x2, waiting for transfers between devices, exchange(): lax.ppermute(faces[0], axis, [(i, i ^ 1) for i in range(count)])  1.2 us
    pallas_call x1, Pallas kernels, encode_inner(): call(encode_middle, (jax.ShapeDtypeStruct((tall, (bz + 2) * chan), bf16),...  1.2 us
    pallas_call x1, Pallas kernels, encode_outer(): call(encode_ends, (jax.ShapeDtypeStruct((tall, (bz + 2) * chan), bf16), j...  1.18 us
  transfers between devices with their start and end apart: 5, of which 4 were waited for; matrix products, arithmetic and copies ran while one was open for 0% of the time, Pallas kernels for 7%

profile of v4, /device:TPU:0, one launch (start us, length us, event | category | flops | bytes accessed | tf_op | source)
XLA Modules:
  0.0 38.0 jit_solution(8385011982239080835)
XLA Ops:
  0.0 1.1 %y_face.1 = bf16[16,512]{1,0:T(8,128)(2,1)S(1)} custom-call(bf16[8,32,16,32]{3,2,1,0:T(8,128)(2,1)} %vol.3), custom_call_target="tpu_custom_call" | custom-call | tf_op jit(solution)/shard_map/y_face/pallas_call | solution.py:124
  1.2 0.6 %collective-permute-start = (bf16[16,512]{1,0:T(8,128)(2,1)S(1)}, bf16[16,512]{1,0:T(8,128)(2,1)S(1)}, u32[]{:S(2)}, u32[]{:S(2)}) collective-permute-start(bf16[16,512]{1,0:T(8,128)(2,1)S(1)} %y_face.1), channel_id=1, source_target_pairs={{0,4},{4,0},{1,5},{5,1},{2,6},{6,2},{3,7},{7,3},{8,12},{12,8},{9,1... | collective-permute-start | bytes 49160 | tf_op jit(solution)/shard_map/ppermute | solution.py:38
  1.7 0.0 copy-done
  1.7 0.5 %pack.1.own = bf16[256,512]{1,0:T(8,128)(2,1)S(1)} custom-call(bf16[8,32,16,32]{3,2,1,0:T(8,128)(2,1)S(1)} %copy-done), custom_call_target="tpu_custom_call" | custom-call | tf_op jit(solution)/shard_map/pack/pallas_call | solution.py:140
  2.2 0.4 collective-permute-done.refs_0_.refs_2_
  2.6 0.1 z_face.1
  2.7 3.0 %collective-permute-start.1 = (bf16[136,128]{1,0:T(8,128)(2,1)S(1)}, bf16[136,128]{1,0:T(8,128)(2,1)S(1)}, u32[]{:S(2)}, u32[]{:S(2)}) collective-permute-start(bf16[136,128]{1,0:T(8,128)(2,1)S(1)} %get-tuple-element.24), channel_id=1, source_target_pairs={{0,1},{1,0},{2,3},{3,2},{4,5},{5,4},{6,7},{7,6},{8,9},{9,8},{10,11... | collective-permute-start | bytes 104456 | tf_op jit(solution)/shard_map/ppermute | solution.py:46
  5.6 2.5 %collective-permute-start.2 = (bf16[136,128]{1,0:T(8,128)(2,1)S(1)}, bf16[136,128]{1,0:T(8,128)(2,1)S(1)}, u32[]{:S(2)}, u32[]{:S(2)}) collective-permute-start(bf16[136,128]{1,0:T(8,128)(2,1)S(1)} %get-tuple-element.25), channel_id=1, source_target_pairs={{0,3},{1,2},{2,1},{3,0},{4,7},{5,6},{6,5},{7,4},{8,11},{9,10},{10,... | collective-permute-start | bytes 104456 | tf_op jit(solution)/shard_map/ppermute | solution.py:47
  8.1 0.0 copy-done.7
  8.1 0.0 copy-done.3
  8.1 0.9 %spread_weights.1 = (bf16[9,256,192]{2,1,0:T(8,128)(2,1)S(1)}, bf16[9,256,192]{2,1,0:T(8,128)(2,1)S(1)}, bf16[2,256,512]{2,1,0:T(8,128)(2,1)S(1)}) custom-call(bf16[9,96,32]{2,1,0:T(8,128)(2,1)S(1)} %bitcast.3, bf16[9,96,32]{2,1,0:T(8,128)(2,1)S(1)} %bitcast.4, bf16[256,256]{1,0:T(8,128)(2,1)S(1)} %copy-done.7), custom_call_target="tpu_custom_call" | custom-call | tf_op jit(solution)/shard_map/spread_weights/pallas_call | solution.py:95
  9.0 0.0 collective-permute-done.1.refs_0_
  9.0 2.3 %collective-permute-done.2.refs_1_ = bf16[136,128]{1,0:T(8,128)(2,1)S(1)} collective-permute-done((bf16[136,128]{1,0:T(8,128)(2,1)S(1)}, bf16[136,128]{1,0:T(8,128)(2,1)S(1)}, u32[]{:S(2)}, u32[]{:S(2)}) %collective-permute-start.2) | collective-permute-done | bytes 34848 | tf_op jit(solution)/shard_map/ppermute | solution.py:47
  11.4 0.1 x_face.1
  11.5 1.6 %collective-permute-start.3 = (bf16[68,640]{1,0:T(8,128)(2,1)S(1)}, bf16[68,640]{1,0:T(8,128)(2,1)S(1)}, u32[]{:S(2)}, u32[]{:S(2)}) collective-permute-start(bf16[68,640]{1,0:T(8,128)(2,1)S(1)} %get-tuple-element.26), channel_id=1, source_target_pairs={{0,8},{8,0},{16,24},{24,16},{1,9},{9,1},{17,25},{25,17},{2,10},{10... | collective-permute-start | bytes 261128 | tf_op jit(solution)/shard_map/ppermute | solution.py:46
  13.1 1.5 %collective-permute-start.4 = (bf16[68,640]{1,0:T(8,128)(2,1)S(1)}, bf16[68,640]{1,0:T(8,128)(2,1)S(1)}, u32[]{:S(2)}, u32[]{:S(2)}) collective-permute-start(bf16[68,640]{1,0:T(8,128)(2,1)S(1)} %get-tuple-element.27), channel_id=1, source_target_pairs={{0,24},{8,16},{16,8},{24,0},{1,25},{9,17},{17,9},{25,1},{2,26},{10... | collective-permute-start | bytes 261128 | tf_op jit(solution)/shard_map/ppermute | solution.py:47
  14.6 1.2 %encode_middle.1 = (bf16[240,576]{1,0:T(8,128)(2,1)S(1)}, f32[80,576]{1,0:T(8,128)S(1)}) custom-call(bf16[256,512]{1,0:T(8,128)(2,1)S(1)} %pack.1.own, bf16[136,128]{1,0:T(8,128)(2,1)S(1)} %collective-permute-done.1.refs_0_, bf16[136,128]{1,0:T(8,128)(2,1)S(1)} %collective-permute-done.2.refs_1_, bf16[16,512]{1,0:T(8,128)(2,1)S(1)} %collective-permute-done.refs_0_.refs_2_, ...), custom_call_target="tpu_custom_call" | custom-call | tf_op jit(solution)/shard_map/encode_middle/pallas_call | solution.py:287
  15.8 1.2 %collective-permute-done.3.refs_3_ = bf16[68,640]{1,0:T(8,128)(2,1)S(1)} collective-permute-done((bf16[68,640]{1,0:T(8,128)(2,1)S(1)}, bf16[68,640]{1,0:T(8,128)(2,1)S(1)}, u32[]{:S(2)}, u32[]{:S(2)}) %collective-permute-start.3) | collective-permute-done | bytes 87072 | tf_op jit(solution)/shard_map/ppermute | solution.py:46
  17.0 1.6 %collective-permute-done.4.refs_4_ = bf16[68,640]{1,0:T(8,128)(2,1)S(1)} collective-permute-done((bf16[68,640]{1,0:T(8,128)(2,1)S(1)}, bf16[68,640]{1,0:T(8,128)(2,1)S(1)}, u32[]{:S(2)}, u32[]{:S(2)}) %collective-permute-start.4) | collective-permute-done | bytes 87072 | tf_op jit(solution)/shard_map/ppermute | solution.py:47
  18.5 0.0 copy-start.8
  18.5 1.2 %encode_ends.1 = (bf16[160,576]{1,0:T(8,128)(2,1)S(1)}, f32[32,8,256]{2,1,0:T(8,128)S(1)}) custom-call(bf16[256,512]{1,0:T(8,128)(2,1)S(1)} %pack.1.own, bf16[136,128]{1,0:T(8,128)(2,1)S(1)} %collective-permute-done.1.refs_0_, bf16[136,128]{1,0:T(8,128)(2,1)S(1)} %collective-permute-done.2.refs_1_, bf16[16,512]{1,0:T(8,128)(2,1)S(1)} %collective-permute-done.refs_0_.refs_2_, ...), custom_call_target="tpu_custom_call" | custom-call | tf_op jit(solution)/shard_map/encode_ends/pallas_call | solution.py:373
  19.7 13.8 %all_to_all.5.g = f32[32,8,256]{2,1,0:T(8,128)S(1)} all-to-all(f32[32,8,256]{2,1,0:T(8,128)S(1)} %get-tuple-element.30), channel_id=1, replica_groups=mesh['gx'=4,'gy'=2,'gz'=4] {'gx','gy','gz'}, dimensions={0} | all-to-all | bytes 524288 | tf_op jit(solution)/shard_map/all_to_all | solution.py:561
  33.6 0.0 copy-done.4
  33.6 4.4 %attend.1 = bf16[8,32,16,32]{3,2,1,0:T(8,128)(2,1)} custom-call(f32[32,8,256]{2,1,0:T(8,128)S(1)} %all_to_all.5.g, f32[1,256]{1,0:T(1,128)S(1)} %bitcast.5, bf16[256,256]{1,0:T(8,128)(2,1)S(1)} %copy-done.5, bf16[256,512]{1,0:T(8,128)(2,1)S(1)} %copy-done.1, bf16[256,256]{1,0:T(8,128)(2,1)S(1)} %copy-done.6, ...), custom_call_target="tpu_custom_call" | custom-call | tf_op jit(solution)/shard_map/attend/pallas_call | solution.py:529
  (13 shorter events, 0.0 us)
Async XLA Ops:
  0.0 1.7 %copy-start = (bf16[8,32,16,32]{3,2,1,0:T(8,128)(2,1)S(1)}, bf16[8,32,16,32]{3,2,1,0:T(8,128)(2,1)}, u32[]{:S(2)}) copy-start(bf16[8,32,16,32]{3,2,1,0:T(8,128)(2,1)} %vol.3) | copy-start | bytes 786436
  0.0 8.1 %copy-start.7 = (bf16[256,256]{1,0:T(8,128)(2,1)S(1)}, bf16[256,256]{1,0:T(8,128)(2,1)}, u32[]{:S(2)}) copy-start(bf16[256,256]{1,0:T(8,128)(2,1)} %up.1) | copy-start | bytes 393220
  0.0 8.1 %copy-start.3 = (bf16[3,3,3,32,32]{4,3,2,1,0:T(8,128)(2,1)S(1)}, bf16[3,3,3,32,32]{4,3,2,1,0:T(8,128)(2,1)}, u32[]{:S(2)}) copy-start(bf16[3,3,3,32,32]{4,3,2,1,0:T(8,128)(2,1)} %param.11) | copy-start | bytes 165892
  0.0 8.1 %copy-start.2 = (bf16[3,3,3,32,32]{4,3,2,1,0:T(8,128)(2,1)S(1)}, bf16[3,3,3,32,32]{4,3,2,1,0:T(8,128)(2,1)}, u32[]{:S(2)}) copy-start(bf16[3,3,3,32,32]{4,3,2,1,0:T(8,128)(2,1)} %param.10) | copy-start | bytes 165892
  1.2 1.4 %collective-permute-start = (bf16[16,512]{1,0:T(8,128)(2,1)S(1)}, bf16[16,512]{1,0:T(8,128)(2,1)S(1)}, u32[]{:S(2)}, u32[]{:S(2)}) collective-permute-start(bf16[16,512]{1,0:T(8,128)(2,1)S(1)} %y_face.1), channel_id=1, source_target_pairs={{0,4},{4,0},{1,5},{5,1},{2,6},{6,2},{3,7},{7,3},{8,12},{12,8},{9,1... | collective-permute-start | bytes 49160 | tf_op jit(solution)/shard_map/ppermute | solution.py:38
  2.7 6.4 %collective-permute-start.1 = (bf16[136,128]{1,0:T(8,128)(2,1)S(1)}, bf16[136,128]{1,0:T(8,128)(2,1)S(1)}, u32[]{:S(2)}, u32[]{:S(2)}) collective-permute-start(bf16[136,128]{1,0:T(8,128)(2,1)S(1)} %get-tuple-element.24), channel_id=1, source_target_pairs={{0,1},{1,0},{2,3},{3,2},{4,5},{5,4},{6,7},{7,6},{8,9},{9,8},{10,11... | collective-permute-start | bytes 104456 | tf_op jit(solution)/shard_map/ppermute | solution.py:46
  5.6 5.7 %collective-permute-start.2 = (bf16[136,128]{1,0:T(8,128)(2,1)S(1)}, bf16[136,128]{1,0:T(8,128)(2,1)S(1)}, u32[]{:S(2)}, u32[]{:S(2)}) collective-permute-start(bf16[136,128]{1,0:T(8,128)(2,1)S(1)} %get-tuple-element.25), channel_id=1, source_target_pairs={{0,3},{1,2},{2,1},{3,0},{4,7},{5,6},{6,5},{7,4},{8,11},{9,10},{10,... | collective-permute-start | bytes 104456 | tf_op jit(solution)/shard_map/ppermute | solution.py:47
  11.5 5.5 %collective-permute-start.3 = (bf16[68,640]{1,0:T(8,128)(2,1)S(1)}, bf16[68,640]{1,0:T(8,128)(2,1)S(1)}, u32[]{:S(2)}, u32[]{:S(2)}) collective-permute-start(bf16[68,640]{1,0:T(8,128)(2,1)S(1)} %get-tuple-element.26), channel_id=1, source_target_pairs={{0,8},{8,0},{16,24},{24,16},{1,9},{9,1},{17,25},{25,17},{2,10},{10... | collective-permute-start | bytes 261128 | tf_op jit(solution)/shard_map/ppermute | solution.py:46
  13.1 5.5 %collective-permute-start.4 = (bf16[68,640]{1,0:T(8,128)(2,1)S(1)}, bf16[68,640]{1,0:T(8,128)(2,1)S(1)}, u32[]{:S(2)}, u32[]{:S(2)}) collective-permute-start(bf16[68,640]{1,0:T(8,128)(2,1)S(1)} %get-tuple-element.27), channel_id=1, source_target_pairs={{0,24},{8,16},{16,8},{24,0},{1,25},{9,17},{17,9},{25,1},{2,26},{10... | collective-permute-start | bytes 261128 | tf_op jit(solution)/shard_map/ppermute | solution.py:47
  18.5 15.0 %copy-start.1 = (bf16[256,512]{1,0:T(8,128)(2,1)S(1)}, bf16[256,512]{1,0:T(8,128)(2,1)}, u32[]{:S(2)}) copy-start(bf16[256,512]{1,0:T(8,128)(2,1)} %kvw.1) | copy-start | bytes 786436
  18.5 15.0 %copy-start.4 = (bf16[640,80]{1,0:T(8,128)(2,1)S(1)}, bf16[640,80]{1,0:T(8,128)(2,1)}, u32[]{:S(2)}) copy-start(bf16[640,80]{1,0:T(8,128)(2,1)} %constant.2.clone.sel) | copy-start | bytes 307204
  18.5 15.0 %copy-start.5 = (bf16[256,256]{1,0:T(8,128)(2,1)S(1)}, bf16[256,256]{1,0:T(8,128)(2,1)}, u32[]{:S(2)}) copy-start(bf16[256,256]{1,0:T(8,128)(2,1)} %qw.1) | copy-start | bytes 393220
  18.5 15.0 %copy-start.6 = (bf16[256,256]{1,0:T(8,128)(2,1)S(1)}, bf16[256,256]{1,0:T(8,128)(2,1)}, u32[]{:S(2)}) copy-start(bf16[256,256]{1,0:T(8,128)(2,1)} %ow.1) | copy-start | bytes 393220
  18.5 15.1 %copy-start.8 = (f32[256]{0:T(256)S(1)}, f32[256]{0:T(256)}, u32[]{:S(2)}) copy-start(f32[256]{0:T(256)} %param.12) | copy-start | bytes 3076

commit v5 on v4

--- a/solution.py
+++ b/solution.py
@@ -11,6 +11,7 @@
 AXES = ("gx", "gy", "gz")
 OUT_Z = 6
 IN_Z = 8
+STATS = 128
 GROUPS = 2
 
 f32 = jnp.float32
@@ -223,17 +224,18 @@
     tall = rows * len(starts)
     for block in range(blocks):
         lane = block * OUT_Z * chan
+        pieces = []
+        for dx in range(3):
+            runs = [
+                source[at + dx * stride : at + dx * stride + rows, lane : lane + IN_Z * chan]
+                for at in starts
+            ]
+            piece = runs[0] if len(runs) == 1 else jnp.concatenate(runs, axis=0)
+            pieces.append(piece.astype(bf16))
         for dy in range(3):
             total = None
             for dx in range(3):
-                pieces = [
-                    source[at + dx * stride : at + dx * stride + rows, lane : lane + IN_Z * chan]
-                    for at in starts
-                ]
-                piece = pieces[0] if len(pieces) == 1 else jnp.concatenate(pieces, axis=0)
-                part = jnp.dot(
-                    piece.astype(bf16), weights[dx * 3 + dy], preferred_element_type=f32
-                )
+                part = jnp.dot(pieces[dx], weights[dx * 3 + dy], preferred_element_type=f32)
                 total = part if total is None else total + part
             sums[first_sum + block * 3 + dy, :tall, :] = total
         at = first_sum + block * 3
@@ -298,7 +300,14 @@
     )(rows, *zgot, *ygot, weights)
 
 
-def encode_outer(rows, zgot, ygot, xgot, weights, partial, shape, counts):
+def thirds(value):
+    first = value.astype(bf16)
+    second = (value - first.astype(f32)).astype(bf16)
+    third = (value - first.astype(f32) - second.astype(f32)).astype(bf16)
+    return [first.astype(f32), second.astype(f32), third.astype(f32)]
+
+
+def encode_outer(rows, zgot, ygot, xgot, weights, partial, gain, shape, counts):
     bx, by, bz, chan = shape
     nx, ny, nz = counts
     lanes = (bz + 4) * chan
@@ -315,7 +324,7 @@
         zrefs, refs = refs[:zparts], refs[zparts:]
         yrefs, refs = refs[:yparts], refs[yparts:]
         xrefs, refs = refs[:xparts], refs[xparts:]
-        w, part_ref, enc, tok_copies, grid, sums, plane_sum = refs
+        w, part_ref, gain_ref, enc, tok, tok_copies, grid, sums, plane_sum = refs
         ix, iy, iz = (lax.axis_index(axis) for axis in AXES)
         lane = lax.broadcasted_iota(jnp.int32, (1, lanes), 1)
         z_ok = ((lane >= 2 * chan) | (iz > 0)) & ((lane < (bz + 2) * chan) | (iz < nz - 1))
@@ -367,23 +376,34 @@
                     axis=1,
                 )
         own_tokens = jnp.concatenate([rows_of[i, k] for i in range(ti) for k in range(tk)], axis=0)
+        tok[...] = own_tokens
+        mean = jnp.mean(own_tokens, axis=1, keepdims=True)
+        center = own_tokens - mean
+        spread = jnp.mean(center * center, axis=1, keepdims=True) + 1e-05
+        normed = center * lax.rsqrt(spread) * gain_ref[...]
+        stat_lane = lax.broadcasted_iota(jnp.int32, (tokens, STATS), 1)
+        stats = jnp.zeros((tokens, STATS), f32)
+        for at, value in enumerate(thirds(mean) + thirds(jnp.sqrt(spread))):
+            stats = jnp.where(stat_lane == at, value, stats)
+        sent = jnp.concatenate([normed, stats], axis=1).astype(bf16)
         for device in range(devices):
-            tok_copies[device] = own_tokens
+            tok_copies[device] = sent
 
     return call(
         encode_ends,
         (
             jax.ShapeDtypeStruct((tall, (bz + 2) * chan), bf16),
-            jax.ShapeDtypeStruct((devices, tokens, width), f32),
+            jax.ShapeDtypeStruct((tokens, width), f32),
+            jax.ShapeDtypeStruct((devices, tokens, width + STATS), bf16),
         ),
         scratch=[
             pltpu.VMEM((8 * stride, lanes), f32),
             pltpu.VMEM((3 * ((bz + 2) // OUT_Z), tall + 8, OUT_Z * chan), f32),
             pltpu.VMEM((2 * tk, stride, 4 * chan), f32),
         ],
-        operands=3 + zparts + yparts + xparts,
+        operands=4 + zparts + yparts + xparts,
         limit=(16 if devices <= 64 else 32) << 20,
-    )(rows, *zgot, *ygot, *xgot, weights, partial)
+    )(rows, *zgot, *ygot, *xgot, weights, partial, gain)
 
 
 def sub_blocks(extent):
@@ -395,7 +415,7 @@
 
 
 def attend_and_join(
-    gathered, gain, q_weight, kv_weight, out_weight, upx, inner, outer, weights, shape, counts
+    gathered, own_tokens, gain, q_weight, kv_weight, out_weight, upx, inner, outer, weights, shape, counts
 ):
     bx, by, bz, chan = shape
     nx, ny, nz = counts
@@ -434,14 +454,10 @@
                 pick[row : row + many, place[dx, dy, dz, i, j, k]] = 1.0
 
     def attend(
-        g, gain_ref, qw, kvw, ow, upx_ref, sel, enc_in, enc_out, w, out, normed_all, mine, mine_n, grid, sums, done, sent
+        g, own, gain_ref, qw, kvw, ow, upx_ref, sel, enc_in, enc_out, w, out, mine, mine_n, grid, sums, done, sent
     ):
         ix, iy, iz = (lax.axis_index(axis) for axis in AXES)
-        t = g[...].reshape(every, width)
-        center = t - jnp.mean(t, axis=1, keepdims=True)
-        spread = jnp.mean(center * center, axis=1, keepdims=True)
-        normed = (center * lax.rsqrt(spread + 1e-05) * gain_ref[...]).astype(bf16)
-        normed_all[...] = normed.astype(f32)
+        normed = g[:, :, :width].astype(f32).reshape(every, width).astype(bf16)
         kv = jnp.dot(normed, kvw[...], preferred_element_type=f32).astype(bf16)
         keys, values = kv[:, :width], kv[:, width:]
         blocks_of = {}
@@ -452,16 +468,19 @@
                 y = jnp.clip(iy + dy, 0, ny - 1)
                 z = jnp.clip(iz + dz, 0, nz - 1)
                 device = (x * ny + y) * nz + z
-                at = pl.multiple_of(device * tokens, 8)
-                blocks_of[dx, dy, dz] = g[device], normed_all[pl.ds(at, tokens), :]
-            block, normed_block = blocks_of[dx, dy, dz]
-            mine[row : row + many, :] = block[first : first + many]
-            mine_n[row : row + many, :] = normed_block[first : first + many]
+                blocks_of[dx, dy, dz] = g[device].astype(f32)
+            mine_n[row : row + many, :] = blocks_of[dx, dy, dz][first : first + many]
             row += many
         if asked > row:
-            mine[row:, :] = jnp.zeros((asked - row, width), f32)
-            mine_n[row:, :] = jnp.zeros((asked - row, width), f32)
-        q = jnp.dot(mine_n[...].astype(bf16), qw[...], preferred_element_type=f32).astype(bf16)
+            mine_n[row:, :] = jnp.zeros((asked - row, width + STATS), f32)
+        stats = mine_n[:, width:]
+        stat_lane = lax.broadcasted_iota(jnp.int32, (1, STATS), 1)
+        mean = jnp.sum(jnp.where(stat_lane < 3, stats, 0.0), axis=1, keepdims=True)
+        deviation = jnp.sum(jnp.where(stat_lane >= 3, stats, 0.0), axis=1, keepdims=True)
+        mine[...] = mean + mine_n[:, :width] * (1.0 / gain_ref[...]) * deviation
+        home = min(place[at] for at in place if at[:3] == (0, 0, 0))
+        mine[home : home + tokens, :] = own[...]
+        q = jnp.dot(mine_n[:, :width].astype(bf16), qw[...], preferred_element_type=f32).astype(bf16)
         lane = lax.broadcasted_iota(jnp.int32, (1, width), 1) // head_size
         stacked = jnp.concatenate(
             [jnp.where(lane == h, q, jnp.zeros_like(q)) for h in range(HEADS)], axis=0
@@ -530,19 +549,18 @@
         attend,
         jax.ShapeDtypeStruct(shape, bf16),
         scratch=[
-            pltpu.VMEM((every, width), f32),
             pltpu.VMEM((asked, width), f32),
-            pltpu.VMEM((asked, width), f32),
+            pltpu.VMEM((asked, width + STATS), f32),
             pltpu.VMEM((tall, padded), f32),
             pltpu.VMEM((GROUPS * 3 * blocks, planes * stride + 8, OUT_Z * chan), f32),
             pltpu.VMEM(shape, bf16),
             pltpu.SemaphoreType.DMA((GROUPS,)),
         ],
         out_specs=pl.BlockSpec(memory_space=pltpu.HBM),
-        operands=10,
+        operands=11,
         limit=min(60, 18 + 16 * HEADS * every * asked // (1 << 20)) << 20,
     )(
-        gathered, gain, q_weight, kv_weight, out_weight, upx, jnp.asarray(pick, bf16), inner, outer, weights
+        gathered, own_tokens, gain, q_weight, kv_weight, out_weight, upx, jnp.asarray(pick, bf16), inner, outer, weights
     )
 
 
@@ -557,10 +575,13 @@
     rows, first_w, second_w, upx = lax.optimization_barrier((rows, first_w, second_w, upx))
     xgot = exchange(x_faces(rows, zgot, ygot, shape, counts), "gx")
     inner, partial = encode_inner(rows, zgot, ygot, first_w, shape, counts)
-    outer, copies = encode_outer(rows, zgot, ygot, xgot, first_w, partial, shape, counts)
+    gain = norm_gain[None]
+    outer, tokens, copies = encode_outer(
+        rows, zgot, ygot, xgot, first_w, partial, gain, shape, counts
+    )
     gathered = lax.all_to_all(copies, AXES, 0, 0, tiled=True)
     return attend_and_join(
-        gathered, norm_gain[None], q_weight, kv_weight, out_weight, upx, inner, outer, second_w, shape, counts
+        gathered, tokens, gain, q_weight, kv_weight, out_weight, upx, inner, outer, second_w, shape, counts
     )
 
 

time: 38.1 us -> 36.7 us (0.963)
  blocking collectives: 13.8 us -> 12.9 us
  Pallas kernels: 9.49 us -> 9.02 us
    all_to_all x1, blocking collectives: 13.8 us -> 12.9 us  [on_device(): gathered = lax.all_to_all(copies, AXES, 0, 0, tiled=True)]
    pallas_call x1, Pallas kernels: 4.4 us -> 3.79 us  [attend_and_join(): call(attend, jax.ShapeDtypeStruct(shape, bf16), scratch=[pltpu.VMEM((aske...]
where the time goes in v5:
time: 36.7 us; the launch traced here: 36.6 us
  blocking collectives  12.9 us (35%)
  starting transfers between devices  9.06 us (25%)
  Pallas kernels  9.02 us (25%)
  waiting for transfers between devices  5.44 us (15%)
    all_to_all x1, blocking collectives, on_device(): gathered = lax.all_to_all(copies, AXES, 0, 0, tiled=True)  12.9 us
    ppermute x2, starting transfers between devices, exchange(): lax.ppermute(faces[0], axis, [(i, i ^ 1) for i in range(count)])  4.53 us
    ppermute x2, starting transfers between devices, exchange(): lax.ppermute(faces[1], axis, [(i, (i + 1) % count if i % 2 else (i - 1) %...  3.97 us
    ppermute x2, waiting for transfers between devices, exchange(): lax.ppermute(faces[1], axis, [(i, (i + 1) % count if i % 2 else (i - 1) %...  3.88 us
    pallas_call x1, Pallas kernels, attend_and_join(): call(attend, jax.ShapeDtypeStruct(shape, bf16), scratch=[pltpu.VMEM((aske...  3.79 us
    pallas_call x1, Pallas kernels, encode_outer(): call(encode_ends, (jax.ShapeDtypeStruct((tall, (bz + 2) * chan), bf16), j...  1.34 us
    pallas_call x1, Pallas kernels, encode_inner(): call(encode_middle, (jax.ShapeDtypeStruct((tall, (bz + 2) * chan), bf16),...  1.18 us
    ppermute x2, waiting for transfers between devices, exchange(): lax.ppermute(faces[0], axis, [(i, i ^ 1) for i in range(count)])  1.17 us
  transfers between devices with their start and end apart: 5, of which 4 were waited for; matrix products, arithmetic and copies ran while one was open for 0% of the time, Pallas kernels for 7%

profile of v5, /device:TPU:0, one launch (start us, length us, event | category | flops | bytes accessed | tf_op | source)
XLA Modules:
  0.0 36.6 jit_solution(12446774731145559467)
XLA Ops:
  0.0 1.1 %y_face.1 = bf16[16,512]{1,0:T(8,128)(2,1)S(1)} custom-call(bf16[8,32,16,32]{3,2,1,0:T(8,128)(2,1)} %vol.3), custom_call_target="tpu_custom_call" | custom-call | tf_op jit(solution)/shard_map/y_face/pallas_call | solution.py:125
  1.2 0.6 %collective-permute-start = (bf16[16,512]{1,0:T(8,128)(2,1)S(1)}, bf16[16,512]{1,0:T(8,128)(2,1)S(1)}, u32[]{:S(2)}, u32[]{:S(2)}) collective-permute-start(bf16[16,512]{1,0:T(8,128)(2,1)S(1)} %y_face.1), channel_id=1, source_target_pairs={{0,4},{4,0},{1,5},{5,1},{2,6},{6,2},{3,7},{7,3},{8,12},{12,8},{9,1... | collective-permute-start | bytes 49160 | tf_op jit(solution)/shard_map/ppermute | solution.py:39
  1.7 0.0 copy-done
  1.7 0.5 %pack.1.own = bf16[256,512]{1,0:T(8,128)(2,1)S(1)} custom-call(bf16[8,32,16,32]{3,2,1,0:T(8,128)(2,1)S(1)} %copy-done), custom_call_target="tpu_custom_call" | custom-call | tf_op jit(solution)/shard_map/pack/pallas_call | solution.py:141
  2.2 0.4 %collective-permute-done.refs_0_.refs_2_ = bf16[16,512]{1,0:T(8,128)(2,1)S(1)} collective-permute-done((bf16[16,512]{1,0:T(8,128)(2,1)S(1)}, bf16[16,512]{1,0:T(8,128)(2,1)S(1)}, u32[]{:S(2)}, u32[]{:S(2)}) %collective-permute-start) | collective-permute-done | bytes 16416 | tf_op jit(solution)/shard_map/ppermute | solution.py:39
  2.6 0.1 z_face.1
  2.7 3.0 %collective-permute-start.1 = (bf16[136,128]{1,0:T(8,128)(2,1)S(1)}, bf16[136,128]{1,0:T(8,128)(2,1)S(1)}, u32[]{:S(2)}, u32[]{:S(2)}) collective-permute-start(bf16[136,128]{1,0:T(8,128)(2,1)S(1)} %get-tuple-element.25), channel_id=1, source_target_pairs={{0,1},{1,0},{2,3},{3,2},{4,5},{5,4},{6,7},{7,6},{8,9},{9,8},{10,11... | collective-permute-start | bytes 104456 | tf_op jit(solution)/shard_map/ppermute | solution.py:47
  5.6 2.5 %collective-permute-start.2 = (bf16[136,128]{1,0:T(8,128)(2,1)S(1)}, bf16[136,128]{1,0:T(8,128)(2,1)S(1)}, u32[]{:S(2)}, u32[]{:S(2)}) collective-permute-start(bf16[136,128]{1,0:T(8,128)(2,1)S(1)} %get-tuple-element.26), channel_id=1, source_target_pairs={{0,3},{1,2},{2,1},{3,0},{4,7},{5,6},{6,5},{7,4},{8,11},{9,10},{10,... | collective-permute-start | bytes 104456 | tf_op jit(solution)/shard_map/ppermute | solution.py:48
  8.1 0.9 %spread_weights.1 = (bf16[9,256,192]{2,1,0:T(8,128)(2,1)S(1)}, bf16[9,256,192]{2,1,0:T(8,128)(2,1)S(1)}, bf16[2,256,512]{2,1,0:T(8,128)(2,1)S(1)}) custom-call(bf16[9,96,32]{2,1,0:T(8,128)(2,1)S(1)} %bitcast.3, bf16[9,96,32]{2,1,0:T(8,128)(2,1)S(1)} %bitcast.4, bf16[256,256]{1,0:T(8,128)(2,1)S(1)} %copy-done.7), custom_call_target="tpu_custom_call" | custom-call | tf_op jit(solution)/shard_map/spread_weights/pallas_call | solution.py:96
  9.0 0.0 collective-permute-done.1.refs_0_
  9.0 2.3 %collective-permute-done.2.refs_1_ = bf16[136,128]{1,0:T(8,128)(2,1)S(1)} collective-permute-done((bf16[136,128]{1,0:T(8,128)(2,1)S(1)}, bf16[136,128]{1,0:T(8,128)(2,1)S(1)}, u32[]{:S(2)}, u32[]{:S(2)}) %collective-permute-start.2) | collective-permute-done | bytes 34848 | tf_op jit(solution)/shard_map/ppermute | solution.py:48
  11.4 0.1 x_face.1
  11.5 1.6 %collective-permute-start.3 = (bf16[68,640]{1,0:T(8,128)(2,1)S(1)}, bf16[68,640]{1,0:T(8,128)(2,1)S(1)}, u32[]{:S(2)}, u32[]{:S(2)}) collective-permute-start(bf16[68,640]{1,0:T(8,128)(2,1)S(1)} %get-tuple-element.27), channel_id=1, source_target_pairs={{0,8},{8,0},{16,24},{24,16},{1,9},{9,1},{17,25},{25,17},{2,10},{10... | collective-permute-start | bytes 261128 | tf_op jit(solution)/shard_map/ppermute | solution.py:47
  13.1 1.5 %collective-permute-start.4 = (bf16[68,640]{1,0:T(8,128)(2,1)S(1)}, bf16[68,640]{1,0:T(8,128)(2,1)S(1)}, u32[]{:S(2)}, u32[]{:S(2)}) collective-permute-start(bf16[68,640]{1,0:T(8,128)(2,1)S(1)} %get-tuple-element.28), channel_id=1, source_target_pairs={{0,24},{8,16},{16,8},{24,0},{1,25},{9,17},{17,9},{25,1},{2,26},{10... | collective-permute-start | bytes 261128 | tf_op jit(solution)/shard_map/ppermute | solution.py:48
  14.6 1.2 %encode_middle.1 = (bf16[240,576]{1,0:T(8,128)(2,1)S(1)}, f32[80,576]{1,0:T(8,128)S(1)}) custom-call(bf16[256,512]{1,0:T(8,128)(2,1)S(1)} %pack.1.own, bf16[136,128]{1,0:T(8,128)(2,1)S(1)} %collective-permute-done.1.refs_0_, bf16[136,128]{1,0:T(8,128)(2,1)S(1)} %collective-permute-done.2.refs_1_, bf16[16,512]{1,0:T(8,128)(2,1)S(1)} %collective-permute-done.refs_0_.refs_2_, ...), custom_call_target="tpu_custom_call" | custom-call | tf_op jit(solution)/shard_map/encode_middle/pallas_call | solution.py:289
  15.7 0.0 copy-start.1
  15.8 0.0 copy-start.4
  15.8 0.0 copy-start.5
  15.8 0.0 copy-start.6
  15.8 1.2 %collective-permute-done.3.refs_3_ = bf16[68,640]{1,0:T(8,128)(2,1)S(1)} collective-permute-done((bf16[68,640]{1,0:T(8,128)(2,1)S(1)}, bf16[68,640]{1,0:T(8,128)(2,1)S(1)}, u32[]{:S(2)}, u32[]{:S(2)}) %collective-permute-start.3) | collective-permute-done | bytes 87072 | tf_op jit(solution)/shard_map/ppermute | solution.py:47
  17.0 1.6 %collective-permute-done.4.refs_4_ = bf16[68,640]{1,0:T(8,128)(2,1)S(1)} collective-permute-done((bf16[68,640]{1,0:T(8,128)(2,1)S(1)}, bf16[68,640]{1,0:T(8,128)(2,1)S(1)}, u32[]{:S(2)}, u32[]{:S(2)}) %collective-permute-start.4) | collective-permute-done | bytes 87072 | tf_op jit(solution)/shard_map/ppermute | solution.py:48
  18.5 1.3 %encode_ends.1 = (bf16[160,576]{1,0:T(8,128)(2,1)S(1)}, f32[8,256]{1,0:T(8,128)S(1)}, bf16[32,8,384]{2,1,0:T(8,128)(2,1)S(1)}) custom-call(bf16[256,512]{1,0:T(8,128)(2,1)S(1)} %pack.1.own, bf16[136,128]{1,0:T(8,128)(2,1)S(1)} %collective-permute-done.1.refs_0_, bf16[136,128]{1,0:T(8,128)(2,1)S(1)} %collective-permute-done.2.refs_1_, ...), custom_call_target="tpu_custom_call" | custom-call | tf_op jit(solution)/shard_map/encode_ends/pallas_call | solution.py:392
  19.9 12.9 %all_to_all.5.g = bf16[32,8,384]{2,1,0:T(8,128)(2,1)S(1)} all-to-all(bf16[32,8,384]{2,1,0:T(8,128)(2,1)S(1)} %get-tuple-element.31), channel_id=1, replica_groups=mesh['gx'=4,'gy'=2,'gz'=4] {'gx','gy','gz'}, dimensions={0} | all-to-all | bytes 393216 | tf_op jit(solution)/shard_map/all_to_all | solution.py:582
  32.8 3.8 %attend.1 = bf16[8,32,16,32]{3,2,1,0:T(8,128)(2,1)} custom-call(bf16[32,8,384]{2,1,0:T(8,128)(2,1)S(1)} %all_to_all.5.g, f32[8,256]{1,0:T(8,128)S(1)} %get-tuple-element.32.own, f32[1,256]{1,0:T(1,128)S(1)} %bitcast.6, bf16[256,256]{1,0:T(8,128)(2,1)S(1)} %copy-done.5, bf16[256,512]{1,0:T(8,128)(2,1)S(1)} %copy-done.1, bf16[256,256]{1,0:T(8,128)(2,1)S(1)} %copy-done.6, ...), custom_call_target="tpu_custom_call" | custom-call | tf_op jit(solution)/shard_map/attend/pallas_call | solution.py:548
  (13 shorter events, 0.0 us)
Async XLA Ops:
  0.0 1.7 %copy-start = (bf16[8,32,16,32]{3,2,1,0:T(8,128)(2,1)S(1)}, bf16[8,32,16,32]{3,2,1,0:T(8,128)(2,1)}, u32[]{:S(2)}) copy-start(bf16[8,32,16,32]{3,2,1,0:T(8,128)(2,1)} %vol.3) | copy-start | bytes 786436
  0.0 8.1 %copy-start.7 = (bf16[256,256]{1,0:T(8,128)(2,1)S(1)}, bf16[256,256]{1,0:T(8,128)(2,1)}, u32[]{:S(2)}) copy-start(bf16[256,256]{1,0:T(8,128)(2,1)} %up.1) | copy-start | bytes 393220
  0.0 8.1 %copy-start.3 = (bf16[3,3,3,32,32]{4,3,2,1,0:T(8,128)(2,1)S(1)}, bf16[3,3,3,32,32]{4,3,2,1,0:T(8,128)(2,1)}, u32[]{:S(2)}) copy-start(bf16[3,3,3,32,32]{4,3,2,1,0:T(8,128)(2,1)} %param.11) | copy-start | bytes 165892
  0.0 8.1 %copy-start.2 = (bf16[3,3,3,32,32]{4,3,2,1,0:T(8,128)(2,1)S(1)}, bf16[3,3,3,32,32]{4,3,2,1,0:T(8,128)(2,1)}, u32[]{:S(2)}) copy-start(bf16[3,3,3,32,32]{4,3,2,1,0:T(8,128)(2,1)} %param.10) | copy-start | bytes 165892
  1.2 1.4 %collective-permute-start = (bf16[16,512]{1,0:T(8,128)(2,1)S(1)}, bf16[16,512]{1,0:T(8,128)(2,1)S(1)}, u32[]{:S(2)}, u32[]{:S(2)}) collective-permute-start(bf16[16,512]{1,0:T(8,128)(2,1)S(1)} %y_face.1), channel_id=1, source_target_pairs={{0,4},{4,0},{1,5},{5,1},{2,6},{6,2},{3,7},{7,3},{8,12},{12,8},{9,1... | collective-permute-start | bytes 49160 | tf_op jit(solution)/shard_map/ppermute | solution.py:39
  2.7 6.4 %collective-permute-start.1 = (bf16[136,128]{1,0:T(8,128)(2,1)S(1)}, bf16[136,128]{1,0:T(8,128)(2,1)S(1)}, u32[]{:S(2)}, u32[]{:S(2)}) collective-permute-start(bf16[136,128]{1,0:T(8,128)(2,1)S(1)} %get-tuple-element.25), channel_id=1, source_target_pairs={{0,1},{1,0},{2,3},{3,2},{4,5},{5,4},{6,7},{7,6},{8,9},{9,8},{10,11... | collective-permute-start | bytes 104456 | tf_op jit(solution)/shard_map/ppermute | solution.py:47
  5.6 5.7 %collective-permute-start.2 = (bf16[136,128]{1,0:T(8,128)(2,1)S(1)}, bf16[136,128]{1,0:T(8,128)(2,1)S(1)}, u32[]{:S(2)}, u32[]{:S(2)}) collective-permute-start(bf16[136,128]{1,0:T(8,128)(2,1)S(1)} %get-tuple-element.26), channel_id=1, source_target_pairs={{0,3},{1,2},{2,1},{3,0},{4,7},{5,6},{6,5},{7,4},{8,11},{9,10},{10,... | collective-permute-start | bytes 104456 | tf_op jit(solution)/shard_map/ppermute | solution.py:48
  8.1 10.4 %copy-start.8 = (f32[256]{0:T(256)S(1)}, f32[256]{0:T(256)}, u32[]{:S(2)}) copy-start(f32[256]{0:T(256)} %param.12) | copy-start | bytes 3076
  11.5 5.5 %collective-permute-start.3 = (bf16[68,640]{1,0:T(8,128)(2,1)S(1)}, bf16[68,640]{1,0:T(8,128)(2,1)S(1)}, u32[]{:S(2)}, u32[]{:S(2)}) collective-permute-start(bf16[68,640]{1,0:T(8,128)(2,1)S(1)} %get-tuple-element.27), channel_id=1, source_target_pairs={{0,8},{8,0},{16,24},{24,16},{1,9},{9,1},{17,25},{25,17},{2,10},{10... | collective-permute-start | bytes 261128 | tf_op jit(solution)/shard_map/ppermute | solution.py:47
  13.1 5.5 %collective-permute-start.4 = (bf16[68,640]{1,0:T(8,128)(2,1)S(1)}, bf16[68,640]{1,0:T(8,128)(2,1)S(1)}, u32[]{:S(2)}, u32[]{:S(2)}) collective-permute-start(bf16[68,640]{1,0:T(8,128)(2,1)S(1)} %get-tuple-element.28), channel_id=1, source_target_pairs={{0,24},{8,16},{16,8},{24,0},{1,25},{9,17},{17,9},{25,1},{2,26},{10... | collective-permute-start | bytes 261128 | tf_op jit(solution)/shard_map/ppermute | solution.py:48
  15.7 17.0 %copy-start.1 = (bf16[256,512]{1,0:T(8,128)(2,1)S(1)}, bf16[256,512]{1,0:T(8,128)(2,1)}, u32[]{:S(2)}) copy-start(bf16[256,512]{1,0:T(8,128)(2,1)} %kvw.1) | copy-start | bytes 786436
  15.8 17.0 %copy-start.4 = (bf16[640,80]{1,0:T(8,128)(2,1)S(1)}, bf16[640,80]{1,0:T(8,128)(2,1)}, u32[]{:S(2)}) copy-start(bf16[640,80]{1,0:T(8,128)(2,1)} %constant.2.clone.sel) | copy-start | bytes 307204
  15.8 17.0 %copy-start.5 = (bf16[256,256]{1,0:T(8,128)(2,1)S(1)}, bf16[256,256]{1,0:T(8,128)(2,1)}, u32[]{:S(2)}) copy-start(bf16[256,256]{1,0:T(8,128)(2,1)} %qw.1) | copy-start | bytes 393220
  15.8 17.0 %copy-start.6 = (bf16[256,256]{1,0:T(8,128)(2,1)S(1)}, bf16[256,256]{1,0:T(8,128)(2,1)}, u32[]{:S(2)}) copy-start(bf16[256,256]{1,0:T(8,128)(2,1)} %ow.1) | copy-start | bytes 393220

commit v6 on v5

--- a/solution.py
+++ b/solution.py
@@ -1,4 +1,5 @@
 import numpy as np
+
 
 import jax
 import jax.numpy as jnp
@@ -43,14 +44,13 @@
             lax.ppermute(faces[0], axis, up),
             lax.ppermute(faces[1], axis, [(j, i) for i, j in up]),
         ]
-    return [
-        lax.ppermute(faces[0], axis, [(i, i ^ 1) for i in range(count)]),
-        lax.ppermute(
-            faces[1],
-            axis,
-            [(i, (i + 1) % count if i % 2 else (i - 1) % count) for i in range(count)],
-        ),
-    ]
+    near = lax.ppermute(faces[0], axis, [(i, i ^ 1) for i in range(count)])
+    far = lax.ppermute(
+        faces[1],
+        axis,
+        [(i, (i + 1) % count if i % 2 else (i - 1) % count) for i in range(count)],
+    )
+    return [near, far]
 
 
 def received(got, index, count):
@@ -69,7 +69,6 @@
         in_specs=[pl.BlockSpec(memory_space=pltpu.VMEM)] * operands,
         scratch_shapes=list(scratch),
         compiler_params=pltpu.CompilerParams(vmem_limit_bytes=limit),
-        name=body.__name__,
         **more,
     )
 
@@ -168,7 +167,7 @@
 
 
 def full_rows(own, zrefs, plane, shape, count):
-    bx, by, bz, chan = shape
+    bx, by, _, chan = shape
     side, at = divmod(plane, bx // 2)
     parts = [
         r[at * by : (at + 1) * by, side * 2 * chan : (side + 1) * 2 * chan].astype(f32) for r in zrefs
@@ -178,7 +177,7 @@
 
 
 def full_edges(yrefs, zrefs, plane, shape, count):
-    bx, by, bz, chan = shape
+    bx, by, _, chan = shape
     side, at = divmod(plane, bx // 2)
     out = []
     for i, ref in enumerate(yrefs):
@@ -219,17 +218,13 @@
     return call(x_face, (face,) * many, operands=1 + zparts + yparts)(rows, *zgot, *ygot)
 
 
-def banded_conv(source, weights, sums, blocks, starts, rows, stride, chan, first_sum=0):
+def banded_conv(pieces_of, weights, sums, blocks, tall, chan):
     outs = []
-    tall = rows * len(starts)
     for block in range(blocks):
         lane = block * OUT_Z * chan
         pieces = []
         for dx in range(3):
-            runs = [
-                source[at + dx * stride : at + dx * stride + rows, lane : lane + IN_Z * chan]
-                for at in starts
-            ]
+            runs = pieces_of(dx, slice(lane, lane + IN_Z * chan))
             piece = runs[0] if len(runs) == 1 else jnp.concatenate(runs, axis=0)
             pieces.append(piece.astype(bf16))
         for dy in range(3):
@@ -237,8 +232,8 @@
             for dx in range(3):
                 part = jnp.dot(pieces[dx], weights[dx * 3 + dy], preferred_element_type=f32)
                 total = part if total is None else total + part
-            sums[first_sum + block * 3 + dy, :tall, :] = total
-        at = first_sum + block * 3
+            sums[block * 3 + dy, :tall, :] = total
+        at = block * 3
         outs.append(
             sums[at, 0:tall, :] + sums[at + 1, 1 : tall + 1, :] + sums[at + 2, 2 : tall + 2, :]
         )
@@ -246,8 +241,8 @@
 
 
 def put_plane(grid, row, own, zrefs, yrefs, plane, shape, counts):
-    bx, by, bz, chan = shape
-    nx, ny, nz = counts
+    _, by, bz, chan = shape
+    _, ny, nz = counts
     iy, iz = lax.axis_index("gy"), lax.axis_index("gz")
     lane = lax.broadcasted_iota(jnp.int32, (1, (bz + 4) * chan), 1)
     z_ok = ((lane >= 2 * chan) | (iz > 0)) & ((lane < (bz + 2) * chan) | (iz < nz - 1))
@@ -275,7 +270,10 @@
         yrefs, (w, enc, partial, grid, sums) = refs[:yparts], refs[yparts:]
         for p in range(bx):
             put_plane(grid, p * stride, own, zrefs, yrefs, p, shape, counts)
-        outs = banded_conv(grid, w, sums, (bz + 2) // OUT_Z, [0], tall, stride, chan)
+        outs = banded_conv(
+            lambda dx, span: [grid[dx * stride : dx * stride + tall, span]],
+            w, sums, (bz + 2) // OUT_Z, tall, chan,
+        )
         encoded = relu_rows(outs)
         enc[...] = encoded
         cells = encoded.astype(f32)
@@ -291,9 +289,9 @@
         (
             jax.ShapeDtypeStruct((tall, (bz + 2) * chan), bf16),
             jax.ShapeDtypeStruct((groups * stride, (bz + 2) * chan), f32),
+            jax.ShapeDtypeStruct((bx * stride, lanes), f32),
         ),
         scratch=[
-            pltpu.VMEM((bx * stride, lanes), f32),
             pltpu.VMEM((3 * ((bz + 2) // OUT_Z), tall + 8, OUT_Z * chan), f32),
         ],
         operands=2 + zparts + yparts,
@@ -307,7 +305,7 @@
     return [first.astype(f32), second.astype(f32), third.astype(f32)]
 
 
-def encode_outer(rows, zgot, ygot, xgot, weights, partial, gain, shape, counts):
+def encode_outer(xgot, weights, partial, middle, gain, shape, counts):
     bx, by, bz, chan = shape
     nx, ny, nz = counts
     lanes = (bz + 4) * chan
@@ -317,21 +315,17 @@
     ti, tj, tk = bx // 8, by // 8, bz // 8
     tokens = ti * tj * tk
     width = 8 * chan
-    zparts, yparts, xparts = len(zgot), len(ygot), len(xgot)
+    xparts, yparts = len(xgot), 1 if ny <= 2 else 2
     devices = nx * ny * nz
 
-    def encode_ends(own, *refs):
-        zrefs, refs = refs[:zparts], refs[zparts:]
-        yrefs, refs = refs[:yparts], refs[yparts:]
+    def encode_ends(*refs):
         xrefs, refs = refs[:xparts], refs[xparts:]
-        w, part_ref, gain_ref, enc, tok, tok_copies, grid, sums, plane_sum = refs
+        w, part_ref, own_grid, gain_ref, enc, tok, tok_copies, grid, sums, plane_sum = refs
         ix, iy, iz = (lax.axis_index(axis) for axis in AXES)
         lane = lax.broadcasted_iota(jnp.int32, (1, lanes), 1)
         z_ok = ((lane >= 2 * chan) | (iz > 0)) & ((lane < (bz + 2) * chan) | (iz < nz - 1))
-        for slot, plane in ((2, 0), (3, 1), (4, bx - 2), (5, bx - 1)):
-            put_plane(grid, slot * stride, own, zrefs, yrefs, plane, shape, counts)
         xm, xp = received([r[...].astype(f32) for r in xrefs], ix, nx)
-        for face, first, ok in ((xm, 0, ix > 0), (xp, 6, ix < nx - 1)):
+        for face, first, ok in ((xm, 0, ix > 0), (xp, 2, ix < nx - 1)):
             good = z_ok & ok
             for q in range(2):
                 base = (first + q) * stride
@@ -340,8 +334,16 @@
                 ym, yp = received([face[at + 4 * i : at + 4 * i + 2] for i in range(yparts)], iy, ny)
                 grid[base : base + 2, :] = jnp.where(good & (iy > 0), ym, 0.0)
                 grid[base + by + 2 : base + by + 4, :] = jnp.where(good & (iy < ny - 1), yp, 0.0)
+
+        def plane_rows(x, span):
+            if 2 <= x < bx + 2:
+                return own_grid[(x - 2) * stride : (x - 1) * stride, span]
+            slot = x if x < 2 else x - bx
+            return grid[slot * stride : (slot + 1) * stride, span]
+
         outs = banded_conv(
-            grid, w, sums, (bz + 2) // OUT_Z, [0, 4 * stride], 2 * stride, stride, chan
+            lambda dx, span: [plane_rows(x + dx, span) for x in (0, 1, bx, bx + 1)],
+            w, sums, (bz + 2) // OUT_Z, tall, chan,
         )
         encoded = relu_rows(outs)
         enc[...] = encoded
@@ -397,13 +399,13 @@
             jax.ShapeDtypeStruct((devices, tokens, width + STATS), bf16),
         ),
         scratch=[
-            pltpu.VMEM((8 * stride, lanes), f32),
+            pltpu.VMEM((4 * stride, lanes), f32),
             pltpu.VMEM((3 * ((bz + 2) // OUT_Z), tall + 8, OUT_Z * chan), f32),
             pltpu.VMEM((2 * tk, stride, 4 * chan), f32),
         ],
-        operands=4 + zparts + yparts + xparts,
+        operands=4 + xparts,
         limit=(16 if devices <= 64 else 32) << 20,
-    )(rows, *zgot, *ygot, *xgot, weights, partial, gain)
+    )(*xgot, weights, partial, middle, gain)
 
 
 def sub_blocks(extent):
@@ -420,7 +422,6 @@
     bx, by, bz, chan = shape
     nx, ny, nz = counts
     stride = by + 8
-    tall = (bx + 2) * stride
     planes = bx // GROUPS
     ti, tj, tk = bx // 8, by // 8, bz // 8
     tokens = ti * tj * tk
@@ -454,7 +455,7 @@
                 pick[row : row + many, place[dx, dy, dz, i, j, k]] = 1.0
 
     def attend(
-        g, own, gain_ref, qw, kvw, ow, upx_ref, sel, enc_in, enc_out, w, out, mine, mine_n, grid, sums, done, sent
+        g, own, gain_ref, qw, kvw, ow, upx_ref, sel, enc_in, enc_out, w, out, mine, mine_n, windows, done, sent
     ):
         ix, iy, iz = (lax.axis_index(axis) for axis in AXES)
         normed = g[:, :, :width].astype(f32).reshape(every, width).astype(bf16)
@@ -507,8 +508,6 @@
         z_ok = ((zl >= chan) | (iz > 0)) & ((zl < (bz + 1) * chan) | (iz < nz - 1))
         ok = y_ok & z_ok
         x_lo, x_hi = ix > 0, ix < nx - 1
-        if padded > wide:
-            grid[:, wide:] = jnp.zeros((tall, padded - wide), f32)
         step = len(zs) * stride
         for xi, (first, many, _, _, a) in enumerate(xs):
             raised = jnp.dot(
@@ -529,16 +528,34 @@
                     good = ok & x_hi
                 ref, at = (enc_in, x - 2) if 2 <= x < bx else (enc_out, x if x < 2 else x - bx + 2)
                 cells = ref[at * stride : (at + 1) * stride, :].astype(f32)
-                grid[x * stride : (x + 1) * stride, :wide] = jnp.where(good, cells + upward, 0.0)
+                joined = jnp.where(good, cells + upward, 0.0)
+                if padded > wide:
+                    joined = jnp.concatenate(
+                        [joined, jnp.zeros((stride, padded - wide), f32)], axis=1
+                    )
+                for block in range(blocks):
+                    lane0 = block * OUT_Z * chan
+                    window = joined[:, lane0 : lane0 + IN_Z * chan]
+                    for dy in range(3):
+                        windows[block * 3 + dy, x * by : (x + 1) * by, :] = window[
+                            dy : dy + by
+                        ].astype(bf16)
         copies = []
         for part in range(GROUPS):
             first = part * planes
-            outs = banded_conv(
-                grid, w, sums, blocks, [first * stride], planes * stride, stride, chan, part * 3 * blocks
-            )
+            outs = []
+            for block in range(blocks):
+                total = None
+                for dx in range(3):
+                    for dy in range(3):
+                        piece = windows[
+                            block * 3 + dy, (first + dx) * by : (first + dx + planes) * by, :
+                        ]
+                        one = jnp.dot(piece, w[dx * 3 + dy], preferred_element_type=f32)
+                        total = one if total is None else total + one
+                outs.append(total)
             final = jnp.concatenate(outs, axis=1)[:, : bz * chan].astype(bf16)
-            for x in range(planes):
-                done[first + x] = final[x * stride : x * stride + by].reshape(by, bz, chan)
+            done[first : first + planes] = final.reshape(planes, by, bz, chan)
             span = pl.ds(first, planes)
             copies.append(pltpu.make_async_copy(done.at[span], out.at[span], sent.at[part]))
             copies[-1].start()
@@ -551,8 +568,7 @@
         scratch=[
             pltpu.VMEM((asked, width), f32),
             pltpu.VMEM((asked, width + STATS), f32),
-            pltpu.VMEM((tall, padded), f32),
-            pltpu.VMEM((GROUPS * 3 * blocks, planes * stride + 8, OUT_Z * chan), f32),
+            pltpu.VMEM((3 * blocks, (bx + 2) * by, IN_Z * chan), bf16),
             pltpu.VMEM(shape, bf16),
             pltpu.SemaphoreType.DMA((GROUPS,)),
         ],
@@ -566,7 +582,7 @@
 
 def on_device(volume, conv_in, conv_out, norm_gain, q_weight, kv_weight, out_weight, up_weight):
     shape = volume.shape
-    bx, by, bz, chan = shape
+    _, _, _, chan = shape
     counts = tuple(lax.axis_size(axis) for axis in AXES)
     first_w, second_w, upx = band_weights(conv_in, conv_out, up_weight, chan)
     ygot = exchange(y_faces(volume, counts), "gy")
@@ -574,10 +590,10 @@
     zgot = exchange(z_faces(rows, ygot, shape, counts), "gz")
     rows, first_w, second_w, upx = lax.optimization_barrier((rows, first_w, second_w, upx))
     xgot = exchange(x_faces(rows, zgot, ygot, shape, counts), "gx")
-    inner, partial = encode_inner(rows, zgot, ygot, first_w, shape, counts)
+    inner, partial, middle = encode_inner(rows, zgot, ygot, first_w, shape, counts)
     gain = norm_gain[None]
     outer, tokens, copies = encode_outer(
-        rows, zgot, ygot, xgot, first_w, partial, gain, shape, counts
+        xgot, first_w, partial, middle, gain, shape, counts
     )
     gathered = lax.all_to_all(copies, AXES, 0, 0, tiled=True)
     return attend_and_join(
@@ -587,6 +603,5 @@
 
 def solution(mesh):
     placed = (P("gx", "gy", "gz", None), P(), P(), P(), P(), P(), P(), P())
-    return jax.shard_map(
-        on_device, mesh=mesh, in_specs=placed, out_specs=P("gx", "gy", "gz", None), check_vma=False
-    )
+
+    return jax.shard_map(on_device, mesh=mesh, in_specs=placed, out_specs=P("gx", "gy", "gz", None), check_vma=False)

time: 36.7 us -> 36.5 us (level)
  no operation moved by 1% of the time
where the time goes in v6:
time: 36.5 us; the launch traced here: 36.4 us
  blocking collectives  12.9 us (35%)
  starting transfers between devices  9.06 us (25%)
  Pallas kernels  8.78 us (24%)
  waiting for transfers between devices  5.47 us (15%)
    all_to_all x1, blocking collectives, on_device(): gathered = lax.all_to_all(copies, AXES, 0, 0, tiled=True)  12.9 us
    ppermute x2, starting transfers between devices, exchange(): near = lax.ppermute(faces[0], axis, [(i, i ^ 1) for i in range(count)])  4.53 us
    ppermute x2, starting transfers between devices, exchange(): lax.ppermute(faces[1], axis, [(i, (i + 1) % count if i % 2 else (i - 1) %...  3.97 us
    ppermute x2, waiting for transfers between devices, exchange(): lax.ppermute(faces[1], axis, [(i, (i + 1) % count if i % 2 else (i - 1) %...  3.88 us
    pallas_call x1, Pallas kernels, attend_and_join(): call(attend, jax.ShapeDtypeStruct(shape, bf16), scratch=[pltpu.VMEM((aske...  3.62 us
    pallas_call x1, Pallas kernels, encode_outer(): call(encode_ends, (jax.ShapeDtypeStruct((tall, (bz + 2) * chan), bf16), j...  1.26 us
    ppermute x2, waiting for transfers between devices, exchange(): near = lax.ppermute(faces[0], axis, [(i, i ^ 1) for i in range(count)])  1.21 us
    pallas_call x1, Pallas kernels, encode_inner(): call(encode_middle, (jax.ShapeDtypeStruct((tall, (bz + 2) * chan), bf16),...  1.19 us
  transfers between devices with their start and end apart: 5, of which 4 were waited for; matrix products, arithmetic and copies ran while one was open for 0% of the time, Pallas kernels for 7%

profile of v6, /device:TPU:0, one launch (start us, length us, event | category | flops | bytes accessed | tf_op | source)
XLA Modules:
  0.0 36.4 jit_solution(13420185896617174612)
XLA Ops:
  0.0 1.1 %y_face.1 = bf16[16,512]{1,0:T(8,128)(2,1)S(1)} custom-call(bf16[8,32,16,32]{3,2,1,0:T(8,128)(2,1)} %vol.3), custom_call_target="tpu_custom_call" | custom-call | tf_op jit(solution)/shard_map/y_face/pallas_call | solution.py:124
  1.2 0.6 %collective-permute-start = (bf16[16,512]{1,0:T(8,128)(2,1)S(1)}, bf16[16,512]{1,0:T(8,128)(2,1)S(1)}, u32[]{:S(2)}, u32[]{:S(2)}) collective-permute-start(bf16[16,512]{1,0:T(8,128)(2,1)S(1)} %y_face.1), channel_id=1, source_target_pairs={{0,4},{4,0},{1,5},{5,1},{2,6},{6,2},{3,7},{7,3},{8,12},{12,8},{9,1... | collective-permute-start | bytes 49160 | tf_op jit(solution)/shard_map/ppermute | solution.py:40
  1.7 0.0 copy-done
  1.7 0.5 %shard_map.91.own = bf16[256,512]{1,0:T(8,128)(2,1)S(1)} custom-call(bf16[8,32,16,32]{3,2,1,0:T(8,128)(2,1)S(1)} %copy-done), custom_call_target="tpu_custom_call" | custom-call | tf_op jit(solution)/shard_map/pallas_call | solution.py:140
  2.2 0.4 %collective-permute-done.refs_0_.refs_2_ = bf16[16,512]{1,0:T(8,128)(2,1)S(1)} collective-permute-done((bf16[16,512]{1,0:T(8,128)(2,1)S(1)}, bf16[16,512]{1,0:T(8,128)(2,1)S(1)}, u32[]{:S(2)}, u32[]{:S(2)}) %collective-permute-start) | collective-permute-done | bytes 16416 | tf_op jit(solution)/shard_map/ppermute | solution.py:40
  2.6 0.1 shard_map.93
  2.7 3.0 %collective-permute-start.1 = (bf16[136,128]{1,0:T(8,128)(2,1)S(1)}, bf16[136,128]{1,0:T(8,128)(2,1)S(1)}, u32[]{:S(2)}, u32[]{:S(2)}) collective-permute-start(bf16[136,128]{1,0:T(8,128)(2,1)S(1)} %get-tuple-element.26), channel_id=1, source_target_pairs={{0,1},{1,0},{2,3},{3,2},{4,5},{5,4},{6,7},{7,6},{8,9},{9,8},{10,11... | collective-permute-start | bytes 104456 | tf_op jit(solution)/shard_map/ppermute | solution.py:47
  5.6 2.5 %collective-permute-start.2 = (bf16[136,128]{1,0:T(8,128)(2,1)S(1)}, bf16[136,128]{1,0:T(8,128)(2,1)S(1)}, u32[]{:S(2)}, u32[]{:S(2)}) collective-permute-start(bf16[136,128]{1,0:T(8,128)(2,1)S(1)} %get-tuple-element.27), channel_id=1, source_target_pairs={{0,3},{1,2},{2,1},{3,0},{4,7},{5,6},{6,5},{7,4},{8,11},{9,10},{10,... | collective-permute-start | bytes 104456 | tf_op jit(solution)/shard_map/ppermute | solution.py:48
  8.1 0.0 copy-done.7
  8.1 0.0 copy-done.3
  8.1 0.0 copy-done.2
  8.1 0.9 %shard_map.92 = (bf16[9,256,192]{2,1,0:T(8,128)(2,1)S(1)}, bf16[9,256,192]{2,1,0:T(8,128)(2,1)S(1)}, bf16[2,256,512]{2,1,0:T(8,128)(2,1)S(1)}) custom-call(bf16[9,96,32]{2,1,0:T(8,128)(2,1)S(1)} %bitcast.3, bf16[9,96,32]{2,1,0:T(8,128)(2,1)S(1)} %bitcast.4, bf16[256,256]{1,0:T(8,128)(2,1)S(1)} %copy-done.7), custom_call_target="tpu_custom_call" | custom-call | tf_op jit(solution)/shard_map/pallas_call | solution.py:95
  9.0 0.0 collective-permute-done.1.refs_0_
  9.0 2.3 %collective-permute-done.2.refs_1_ = bf16[136,128]{1,0:T(8,128)(2,1)S(1)} collective-permute-done((bf16[136,128]{1,0:T(8,128)(2,1)S(1)}, bf16[136,128]{1,0:T(8,128)(2,1)S(1)}, u32[]{:S(2)}, u32[]{:S(2)}) %collective-permute-start.2) | collective-permute-done | bytes 34848 | tf_op jit(solution)/shard_map/ppermute | solution.py:48
  11.4 0.1 shard_map.94
  11.5 1.6 %collective-permute-start.3 = (bf16[68,640]{1,0:T(8,128)(2,1)S(1)}, bf16[68,640]{1,0:T(8,128)(2,1)S(1)}, u32[]{:S(2)}, u32[]{:S(2)}) collective-permute-start(bf16[68,640]{1,0:T(8,128)(2,1)S(1)} %get-tuple-element.28), channel_id=1, source_target_pairs={{0,8},{8,0},{16,24},{24,16},{1,9},{9,1},{17,25},{25,17},{2,10},{10... | collective-permute-start | bytes 261128 | tf_op jit(solution)/shard_map/ppermute | solution.py:47
  13.1 1.5 %collective-permute-start.4 = (bf16[68,640]{1,0:T(8,128)(2,1)S(1)}, bf16[68,640]{1,0:T(8,128)(2,1)S(1)}, u32[]{:S(2)}, u32[]{:S(2)}) collective-permute-start(bf16[68,640]{1,0:T(8,128)(2,1)S(1)} %get-tuple-element.29), channel_id=1, source_target_pairs={{0,24},{8,16},{16,8},{24,0},{1,25},{9,17},{17,9},{25,1},{2,26},{10... | collective-permute-start | bytes 261128 | tf_op jit(solution)/shard_map/ppermute | solution.py:48
  14.6 1.2 %shard_map.95 = (bf16[240,576]{1,0:T(8,128)(2,1)S(1)}, f32[80,576]{1,0:T(8,128)S(1)}, f32[320,640]{1,0:T(8,128)S(1)}) custom-call(bf16[256,512]{1,0:T(8,128)(2,1)S(1)} %shard_map.91.own, bf16[136,128]{1,0:T(8,128)(2,1)S(1)} %collective-permute-done.1.refs_0_, bf16[136,128]{1,0:T(8,128)(2,1)S(1)} %collective-permute-done.2.refs_1_, ...), custom_call_target="tpu_custom_call" | custom-call | tf_op jit(solution)/shard_map/pallas_call | solution.py:287
  15.8 1.2 %collective-permute-done.3.refs_0_ = bf16[68,640]{1,0:T(8,128)(2,1)S(1)} collective-permute-done((bf16[68,640]{1,0:T(8,128)(2,1)S(1)}, bf16[68,640]{1,0:T(8,128)(2,1)S(1)}, u32[]{:S(2)}, u32[]{:S(2)}) %collective-permute-start.3) | collective-permute-done | bytes 87072 | tf_op jit(solution)/shard_map/ppermute | solution.py:47
  17.0 1.6 %collective-permute-done.4.refs_1_ = bf16[68,640]{1,0:T(8,128)(2,1)S(1)} collective-permute-done((bf16[68,640]{1,0:T(8,128)(2,1)S(1)}, bf16[68,640]{1,0:T(8,128)(2,1)S(1)}, u32[]{:S(2)}, u32[]{:S(2)}) %collective-permute-start.4) | collective-permute-done | bytes 87072 | tf_op jit(solution)/shard_map/ppermute | solution.py:48
  18.5 0.0 copy-start.6
  18.5 1.3 %shard_map.96 = (bf16[160,576]{1,0:T(8,128)(2,1)S(1)}, f32[8,256]{1,0:T(8,128)S(1)}, bf16[32,8,384]{2,1,0:T(8,128)(2,1)S(1)}) custom-call(bf16[68,640]{1,0:T(8,128)(2,1)S(1)} %collective-permute-done.3.refs_0_, bf16[68,640]{1,0:T(8,128)(2,1)S(1)} %collective-permute-done.4.refs_1_, bf16[9,256,192]{2,1,0:T(8,128)(2,1)S(1)} %get-tuple-element.30.refs_3_.refs_2_, ...), custom_call_target="tpu_custom_call" | custom-call | tf_op jit(solution)/shard_map/pallas_call | solution.py:394
  19.8 12.9 %all_to_all.5.g = bf16[32,8,384]{2,1,0:T(8,128)(2,1)S(1)} all-to-all(bf16[32,8,384]{2,1,0:T(8,128)(2,1)S(1)} %get-tuple-element.33), channel_id=1, replica_groups=mesh['gx'=4,'gy'=2,'gz'=4] {'gx','gy','gz'}, dimensions={0} | all-to-all | bytes 393216 | tf_op jit(solution)/shard_map/all_to_all | solution.py:598
  32.7 3.6 %shard_map.97 = bf16[8,32,16,32]{3,2,1,0:T(8,128)(2,1)} custom-call(bf16[32,8,384]{2,1,0:T(8,128)(2,1)S(1)} %all_to_all.5.g, f32[8,256]{1,0:T(8,128)S(1)} %get-tuple-element.34.own, f32[1,256]{1,0:T(1,128)S(1)} %bitcast.6, bf16[256,256]{1,0:T(8,128)(2,1)S(1)} %copy-done.5, bf16[256,512]{1,0:T(8,128)(2,1)S(1)} %copy-done.1, bf16[256,256]{1,0:T(8,128)(2,1)S(1)} %copy-done.6, ...), custom_call_target="tpu_custom_call" | custom-call | tf_op jit(solution)/shard_map/pallas_call | solution.py:565
  (13 shorter events, 0.0 us)
Async XLA Ops:
  0.0 1.7 %copy-start = (bf16[8,32,16,32]{3,2,1,0:T(8,128)(2,1)S(1)}, bf16[8,32,16,32]{3,2,1,0:T(8,128)(2,1)}, u32[]{:S(2)}) copy-start(bf16[8,32,16,32]{3,2,1,0:T(8,128)(2,1)} %vol.3) | copy-start | bytes 786436
  0.0 8.1 %copy-start.7 = (bf16[256,256]{1,0:T(8,128)(2,1)S(1)}, bf16[256,256]{1,0:T(8,128)(2,1)}, u32[]{:S(2)}) copy-start(bf16[256,256]{1,0:T(8,128)(2,1)} %up.1) | copy-start | bytes 393220
  0.0 8.1 %copy-start.3 = (bf16[3,3,3,32,32]{4,3,2,1,0:T(8,128)(2,1)S(1)}, bf16[3,3,3,32,32]{4,3,2,1,0:T(8,128)(2,1)}, u32[]{:S(2)}) copy-start(bf16[3,3,3,32,32]{4,3,2,1,0:T(8,128)(2,1)} %param.11) | copy-start | bytes 165892
  0.0 8.1 %copy-start.2 = (bf16[3,3,3,32,32]{4,3,2,1,0:T(8,128)(2,1)S(1)}, bf16[3,3,3,32,32]{4,3,2,1,0:T(8,128)(2,1)}, u32[]{:S(2)}) copy-start(bf16[3,3,3,32,32]{4,3,2,1,0:T(8,128)(2,1)} %param.10) | copy-start | bytes 165892
  1.2 1.4 %collective-permute-start = (bf16[16,512]{1,0:T(8,128)(2,1)S(1)}, bf16[16,512]{1,0:T(8,128)(2,1)S(1)}, u32[]{:S(2)}, u32[]{:S(2)}) collective-permute-start(bf16[16,512]{1,0:T(8,128)(2,1)S(1)} %y_face.1), channel_id=1, source_target_pairs={{0,4},{4,0},{1,5},{5,1},{2,6},{6,2},{3,7},{7,3},{8,12},{12,8},{9,1... | collective-permute-start | bytes 49160 | tf_op jit(solution)/shard_map/ppermute | solution.py:40
  2.7 6.4 %collective-permute-start.1 = (bf16[136,128]{1,0:T(8,128)(2,1)S(1)}, bf16[136,128]{1,0:T(8,128)(2,1)S(1)}, u32[]{:S(2)}, u32[]{:S(2)}) collective-permute-start(bf16[136,128]{1,0:T(8,128)(2,1)S(1)} %get-tuple-element.26), channel_id=1, source_target_pairs={{0,1},{1,0},{2,3},{3,2},{4,5},{5,4},{6,7},{7,6},{8,9},{9,8},{10,11... | collective-permute-start | bytes 104456 | tf_op jit(solution)/shard_map/ppermute | solution.py:47
  5.6 5.7 %collective-permute-start.2 = (bf16[136,128]{1,0:T(8,128)(2,1)S(1)}, bf16[136,128]{1,0:T(8,128)(2,1)S(1)}, u32[]{:S(2)}, u32[]{:S(2)}) collective-permute-start(bf16[136,128]{1,0:T(8,128)(2,1)S(1)} %get-tuple-element.27), channel_id=1, source_target_pairs={{0,3},{1,2},{2,1},{3,0},{4,7},{5,6},{6,5},{7,4},{8,11},{9,10},{10,... | collective-permute-start | bytes 104456 | tf_op jit(solution)/shard_map/ppermute | solution.py:48
  8.1 10.4 %copy-start.8 = (f32[256]{0:T(256)S(1)}, f32[256]{0:T(256)}, u32[]{:S(2)}) copy-start(f32[256]{0:T(256)} %param.12) | copy-start | bytes 3076
  11.5 5.5 %collective-permute-start.3 = (bf16[68,640]{1,0:T(8,128)(2,1)S(1)}, bf16[68,640]{1,0:T(8,128)(2,1)S(1)}, u32[]{:S(2)}, u32[]{:S(2)}) collective-permute-start(bf16[68,640]{1,0:T(8,128)(2,1)S(1)} %get-tuple-element.28), channel_id=1, source_target_pairs={{0,8},{8,0},{16,24},{24,16},{1,9},{9,1},{17,25},{25,17},{2,10},{10... | collective-permute-start | bytes 261128 | tf_op jit(solution)/shard_map/ppermute | solution.py:47
  13.1 5.5 %collective-permute-start.4 = (bf16[68,640]{1,0:T(8,128)(2,1)S(1)}, bf16[68,640]{1,0:T(8,128)(2,1)S(1)}, u32[]{:S(2)}, u32[]{:S(2)}) collective-permute-start(bf16[68,640]{1,0:T(8,128)(2,1)S(1)} %get-tuple-element.29), channel_id=1, source_target_pairs={{0,24},{8,16},{16,8},{24,0},{1,25},{9,17},{17,9},{25,1},{2,26},{10... | collective-permute-start | bytes 261128 | tf_op jit(solution)/shard_map/ppermute | solution.py:48
  18.5 14.2 %copy-start.1 = (bf16[256,512]{1,0:T(8,128)(2,1)S(1)}, bf16[256,512]{1,0:T(8,128)(2,1)}, u32[]{:S(2)}) copy-start(bf16[256,512]{1,0:T(8,128)(2,1)} %kvw.1) | copy-start | bytes 786436
  18.5 14.2 %copy-start.4 = (bf16[640,80]{1,0:T(8,128)(2,1)S(1)}, bf16[640,80]{1,0:T(8,128)(2,1)}, u32[]{:S(2)}) copy-start(bf16[640,80]{1,0:T(8,128)(2,1)} %constant.2.clone.sel) | copy-start | bytes 307204
  18.5 14.2 %copy-start.5 = (bf16[256,256]{1,0:T(8,128)(2,1)S(1)}, bf16[256,256]{1,0:T(8,128)(2,1)}, u32[]{:S(2)}) copy-start(bf16[256,256]{1,0:T(8,128)(2,1)} %qw.1) | copy-start | bytes 393220
  18.5 14.2 %copy-start.6 = (bf16[256,256]{1,0:T(8,128)(2,1)S(1)}, bf16[256,256]{1,0:T(8,128)(2,1)}, u32[]{:S(2)}) copy-start(bf16[256,256]{1,0:T(8,128)(2,1)} %ow.1) | copy-start | bytes 393220

commit v7 on v6

--- a/solution.py
+++ b/solution.py
@@ -109,16 +109,21 @@
 
     def y_face(vol, *refs):
         outs, (here, arrived) = refs[:many], refs[many:]
+        starts = (0, by - 2)
+        if counts[1] == 2:
+            starts = ((1 - lax.axis_index("gy")) * (by - 2),)
         copies = [
             pltpu.make_async_copy(vol.at[:, pl.ds(y, 2)], here.at[side], arrived.at[side])
-            for side, y in enumerate((0, by - 2))
+            for side, y in enumerate(starts)
         ]
         for copy in copies:
             copy.start()
         for copy in copies:
             copy.wait()
-        low, high = (here[side].astype(f32).reshape(bx * 2, bz * chan) for side in range(2))
-        for ref, face in zip(outs, sends(low, high, lax.axis_index("gy"), counts[1])):
+        faces = [here[side].astype(f32).reshape(bx * 2, bz * chan) for side in range(len(starts))]
+        if len(faces) == 2:
+            faces = sends(faces[0], faces[1], lax.axis_index("gy"), counts[1])
+        for ref, face in zip(outs, faces):
             ref[...] = face.astype(bf16)
 
     return pl.pallas_call(
@@ -254,7 +259,7 @@
 
 
 def relu_rows(outs):
-    return jnp.maximum(jnp.concatenate(outs, axis=1), 0.0).astype(bf16)
+    return jnp.concatenate([jnp.maximum(out, 0.0).astype(bf16) for out in outs], axis=1)
 
 
 def encode_inner(rows, zgot, ygot, weights, shape, counts):
@@ -455,10 +460,10 @@
                 pick[row : row + many, place[dx, dy, dz, i, j, k]] = 1.0
 
     def attend(
-        g, own, gain_ref, qw, kvw, ow, upx_ref, sel, enc_in, enc_out, w, out, mine, mine_n, windows, done, sent
+        g, g_rows, own, gain_ref, qw, kvw, ow, upx_ref, sel, enc_in, enc_out, w, out, mine, mine_n, windows, done, sent
     ):
         ix, iy, iz = (lax.axis_index(axis) for axis in AXES)
-        normed = g[:, :, :width].astype(f32).reshape(every, width).astype(bf16)
+        normed = g_rows[:, :width]
         kv = jnp.dot(normed, kvw[...], preferred_element_type=f32).astype(bf16)
         keys, values = kv[:, :width], kv[:, width:]
         blocks_of = {}
@@ -492,10 +497,14 @@
         )
         e = jnp.exp(scores - jnp.max(scores, axis=1, keepdims=True))
         total = jnp.sum(e, axis=1, keepdims=True)
-        ratio = jnp.dot(e.astype(bf16), values, preferred_element_type=f32) / total
-        attended = jnp.zeros((asked, width), f32)
+        num = jnp.dot(e.astype(bf16), values, preferred_element_type=f32)
+        top = jnp.zeros((asked, width), f32)
+        bottom = jnp.ones((asked, width), f32)
         for h in range(HEADS):
-            attended = jnp.where(lane == h, ratio[h * asked : (h + 1) * asked], attended)
+            at = slice(h * asked, (h + 1) * asked)
+            top = jnp.where(lane == h, num[at], top)
+            bottom = jnp.where(lane == h, total[at], bottom)
+        attended = top / bottom
         mixture = (
             mine[...] + jnp.dot(attended.astype(bf16), ow[...], preferred_element_type=f32)
         ).astype(bf16)
@@ -533,13 +542,13 @@
                     joined = jnp.concatenate(
                         [joined, jnp.zeros((stride, padded - wide), f32)], axis=1
                     )
-                for block in range(blocks):
-                    lane0 = block * OUT_Z * chan
-                    window = joined[:, lane0 : lane0 + IN_Z * chan]
-                    for dy in range(3):
-                        windows[block * 3 + dy, x * by : (x + 1) * by, :] = window[
-                            dy : dy + by
-                        ].astype(bf16)
+                for dy in range(3):
+                    line = joined[dy : dy + by].astype(bf16)
+                    for block in range(blocks):
+                        lane0 = block * OUT_Z * chan
+                        windows[block * 3 + dy, x * by : (x + 1) * by, :] = line[
+                            :, lane0 : lane0 + IN_Z * chan
+                        ]
         copies = []
         for part in range(GROUPS):
             first = part * planes
@@ -553,8 +562,8 @@
                         ]
                         one = jnp.dot(piece, w[dx * 3 + dy], preferred_element_type=f32)
                         total = one if total is None else total + one
-                outs.append(total)
-            final = jnp.concatenate(outs, axis=1)[:, : bz * chan].astype(bf16)
+                outs.append(total.astype(bf16))
+            final = jnp.concatenate(outs, axis=1)[:, : bz * chan]
             done[first : first + planes] = final.reshape(planes, by, bz, chan)
             span = pl.ds(first, planes)
             copies.append(pltpu.make_async_copy(done.at[span], out.at[span], sent.at[part]))
@@ -573,10 +582,10 @@
             pltpu.SemaphoreType.DMA((GROUPS,)),
         ],
         out_specs=pl.BlockSpec(memory_space=pltpu.HBM),
-        operands=11,
+        operands=12,
         limit=min(60, 18 + 16 * HEADS * every * asked // (1 << 20)) << 20,
     )(
-        gathered, own_tokens, gain, q_weight, kv_weight, out_weight, upx, jnp.asarray(pick, bf16), inner, outer, weights
+        gathered, gathered.reshape(every, width + STATS), own_tokens, gain, q_weight, kv_weight, out_weight, upx, jnp.asarray(pick, bf16), inner, outer, weights
     )
 
 

time: 36.5 us -> 36.4 us (level)
  no operation moved by 1% of the time
where the time goes in v7:
time: 36.4 us; the launch traced here: 36.3 us
  blocking collectives  12.9 us (35%)
  starting transfers between devices  9.06 us (25%)
  Pallas kernels  8.7 us (24%)
  waiting for transfers between devices  5.47 us (15%)
    all_to_all x1, blocking collectives, on_device(): gathered = lax.all_to_all(copies, AXES, 0, 0, tiled=True)  12.9 us
    ppermute x2, starting transfers between devices, exchange(): near = lax.ppermute(faces[0], axis, [(i, i ^ 1) for i in range(count)])  4.53 us
    ppermute x2, starting transfers between devices, exchange(): lax.ppermute(faces[1], axis, [(i, (i + 1) % count if i % 2 else (i - 1) %...  3.97 us
    ppermute x2, waiting for transfers between devices, exchange(): lax.ppermute(faces[1], axis, [(i, (i + 1) % count if i % 2 else (i - 1) %...  3.88 us
    pallas_call x1, Pallas kernels, attend_and_join(): call(attend, jax.ShapeDtypeStruct(shape, bf16), scratch=[pltpu.VMEM((aske...  3.6 us
    pallas_call x1, Pallas kernels, encode_outer(): call(encode_ends, (jax.ShapeDtypeStruct((tall, (bz + 2) * chan), bf16), j...  1.26 us
    ppermute x2, waiting for transfers between devices, exchange(): near = lax.ppermute(faces[0], axis, [(i, i ^ 1) for i in range(count)])  1.21 us
    pallas_call x1, Pallas kernels, encode_inner(): call(encode_middle, (jax.ShapeDtypeStruct((tall, (bz + 2) * chan), bf16),...  1.19 us
  transfers between devices with their start and end apart: 5, of which 4 were waited for; matrix products, arithmetic and copies ran while one was open for 0% of the time, Pallas kernels for 7%

profile of v7, /device:TPU:0, one launch (start us, length us, event | category | flops | bytes accessed | tf_op | source)
XLA Modules:
  0.0 36.3 jit_solution(10297519080014229729)
XLA Ops:
  0.0 1.1 %y_face.1 = bf16[16,512]{1,0:T(8,128)(2,1)S(1)} custom-call(bf16[8,32,16,32]{3,2,1,0:T(8,128)(2,1)} %vol.3), custom_call_target="tpu_custom_call" | custom-call | tf_op jit(solution)/shard_map/y_face/pallas_call | solution.py:129
  1.1 0.6 %collective-permute-start = (bf16[16,512]{1,0:T(8,128)(2,1)S(1)}, bf16[16,512]{1,0:T(8,128)(2,1)S(1)}, u32[]{:S(2)}, u32[]{:S(2)}) collective-permute-start(bf16[16,512]{1,0:T(8,128)(2,1)S(1)} %y_face.1), channel_id=1, source_target_pairs={{0,4},{4,0},{1,5},{5,1},{2,6},{6,2},{3,7},{7,3},{8,12},{12,8},{9,1... | collective-permute-start | bytes 49160 | tf_op jit(solution)/shard_map/ppermute | solution.py:40
  1.7 0.0 copy-done
  1.7 0.5 %shard_map.91.own = bf16[256,512]{1,0:T(8,128)(2,1)S(1)} custom-call(bf16[8,32,16,32]{3,2,1,0:T(8,128)(2,1)S(1)} %copy-done), custom_call_target="tpu_custom_call" | custom-call | tf_op jit(solution)/shard_map/pallas_call | solution.py:145
  2.1 0.4 %collective-permute-done.refs_0_.refs_2_ = bf16[16,512]{1,0:T(8,128)(2,1)S(1)} collective-permute-done((bf16[16,512]{1,0:T(8,128)(2,1)S(1)}, bf16[16,512]{1,0:T(8,128)(2,1)S(1)}, u32[]{:S(2)}, u32[]{:S(2)}) %collective-permute-start) | collective-permute-done | bytes 16416 | tf_op jit(solution)/shard_map/ppermute | solution.py:40
  2.5 0.1 shard_map.93
  2.6 3.0 %collective-permute-start.1 = (bf16[136,128]{1,0:T(8,128)(2,1)S(1)}, bf16[136,128]{1,0:T(8,128)(2,1)S(1)}, u32[]{:S(2)}, u32[]{:S(2)}) collective-permute-start(bf16[136,128]{1,0:T(8,128)(2,1)S(1)} %get-tuple-element.26), channel_id=1, source_target_pairs={{0,1},{1,0},{2,3},{3,2},{4,5},{5,4},{6,7},{7,6},{8,9},{9,8},{10,11... | collective-permute-start | bytes 104456 | tf_op jit(solution)/shard_map/ppermute | solution.py:47
  5.6 2.5 %collective-permute-start.2 = (bf16[136,128]{1,0:T(8,128)(2,1)S(1)}, bf16[136,128]{1,0:T(8,128)(2,1)S(1)}, u32[]{:S(2)}, u32[]{:S(2)}) collective-permute-start(bf16[136,128]{1,0:T(8,128)(2,1)S(1)} %get-tuple-element.27), channel_id=1, source_target_pairs={{0,3},{1,2},{2,1},{3,0},{4,7},{5,6},{6,5},{7,4},{8,11},{9,10},{10,... | collective-permute-start | bytes 104456 | tf_op jit(solution)/shard_map/ppermute | solution.py:48
  8.1 0.0 copy-done.2
  8.1 0.9 %shard_map.92 = (bf16[9,256,192]{2,1,0:T(8,128)(2,1)S(1)}, bf16[9,256,192]{2,1,0:T(8,128)(2,1)S(1)}, bf16[2,256,512]{2,1,0:T(8,128)(2,1)S(1)}) custom-call(bf16[9,96,32]{2,1,0:T(8,128)(2,1)S(1)} %bitcast.5, bf16[9,96,32]{2,1,0:T(8,128)(2,1)S(1)} %bitcast.6, bf16[256,256]{1,0:T(8,128)(2,1)S(1)} %copy-done.7), custom_call_target="tpu_custom_call" | custom-call | tf_op jit(solution)/shard_map/pallas_call | solution.py:95
  9.0 0.0 collective-permute-done.1.refs_0_
  9.0 2.3 %collective-permute-done.2.refs_1_ = bf16[136,128]{1,0:T(8,128)(2,1)S(1)} collective-permute-done((bf16[136,128]{1,0:T(8,128)(2,1)S(1)}, bf16[136,128]{1,0:T(8,128)(2,1)S(1)}, u32[]{:S(2)}, u32[]{:S(2)}) %collective-permute-start.2) | collective-permute-done | bytes 34848 | tf_op jit(solution)/shard_map/ppermute | solution.py:48
  11.3 0.1 shard_map.94
  11.5 1.6 %collective-permute-start.3 = (bf16[68,640]{1,0:T(8,128)(2,1)S(1)}, bf16[68,640]{1,0:T(8,128)(2,1)S(1)}, u32[]{:S(2)}, u32[]{:S(2)}) collective-permute-start(bf16[68,640]{1,0:T(8,128)(2,1)S(1)} %get-tuple-element.28), channel_id=1, source_target_pairs={{0,8},{8,0},{16,24},{24,16},{1,9},{9,1},{17,25},{25,17},{2,10},{10... | collective-permute-start | bytes 261128 | tf_op jit(solution)/shard_map/ppermute | solution.py:47
  13.0 1.5 %collective-permute-start.4 = (bf16[68,640]{1,0:T(8,128)(2,1)S(1)}, bf16[68,640]{1,0:T(8,128)(2,1)S(1)}, u32[]{:S(2)}, u32[]{:S(2)}) collective-permute-start(bf16[68,640]{1,0:T(8,128)(2,1)S(1)} %get-tuple-element.29), channel_id=1, source_target_pairs={{0,24},{8,16},{16,8},{24,0},{1,25},{9,17},{17,9},{25,1},{2,26},{10... | collective-permute-start | bytes 261128 | tf_op jit(solution)/shard_map/ppermute | solution.py:48
  14.5 1.2 %shard_map.95 = (bf16[240,576]{1,0:T(8,128)(2,1)S(1)}, f32[80,576]{1,0:T(8,128)S(1)}, f32[320,640]{1,0:T(8,128)S(1)}) custom-call(bf16[256,512]{1,0:T(8,128)(2,1)S(1)} %shard_map.91.own, bf16[136,128]{1,0:T(8,128)(2,1)S(1)} %collective-permute-done.1.refs_0_, bf16[136,128]{1,0:T(8,128)(2,1)S(1)} %collective-permute-done.2.refs_1_, ...), custom_call_target="tpu_custom_call" | custom-call | tf_op jit(solution)/shard_map/pallas_call | solution.py:292
  15.7 1.2 %collective-permute-done.3.refs_0_ = bf16[68,640]{1,0:T(8,128)(2,1)S(1)} collective-permute-done((bf16[68,640]{1,0:T(8,128)(2,1)S(1)}, bf16[68,640]{1,0:T(8,128)(2,1)S(1)}, u32[]{:S(2)}, u32[]{:S(2)}) %collective-permute-start.3) | collective-permute-done | bytes 87072 | tf_op jit(solution)/shard_map/ppermute | solution.py:47
  16.9 1.6 %collective-permute-done.4.refs_1_ = bf16[68,640]{1,0:T(8,128)(2,1)S(1)} collective-permute-done((bf16[68,640]{1,0:T(8,128)(2,1)S(1)}, bf16[68,640]{1,0:T(8,128)(2,1)S(1)}, u32[]{:S(2)}, u32[]{:S(2)}) %collective-permute-start.4) | collective-permute-done | bytes 87072 | tf_op jit(solution)/shard_map/ppermute | solution.py:48
  18.5 0.0 copy-done.8
  18.5 0.0 copy-start.6
  18.5 1.3 %shard_map.96 = (bf16[160,576]{1,0:T(8,128)(2,1)S(1)}, f32[8,256]{1,0:T(8,128)S(1)}, bf16[32,8,384]{2,1,0:T(8,128)(2,1)S(1)}) custom-call(bf16[68,640]{1,0:T(8,128)(2,1)S(1)} %collective-permute-done.3.refs_0_, bf16[68,640]{1,0:T(8,128)(2,1)S(1)} %collective-permute-done.4.refs_1_, bf16[9,256,192]{2,1,0:T(8,128)(2,1)S(1)} %get-tuple-element.30.refs_3_.refs_2_, ...), custom_call_target="tpu_custom_call" | custom-call | tf_op jit(solution)/shard_map/pallas_call | solution.py:399
  19.8 12.9 %all_to_all.5.g = bf16[32,8,384]{2,1,0:T(8,128)(2,1)S(1)} all-to-all(bf16[32,8,384]{2,1,0:T(8,128)(2,1)S(1)} %get-tuple-element.33), channel_id=1, replica_groups=mesh['gx'=4,'gy'=2,'gz'=4] {'gx','gy','gz'}, dimensions={0} | all-to-all | bytes 393216 | tf_op jit(solution)/shard_map/all_to_all | solution.py:607
  32.7 0.0 copy-done.4
  32.7 3.6 %shard_map.97 = bf16[8,32,16,32]{3,2,1,0:T(8,128)(2,1)} custom-call(bf16[32,8,384]{2,1,0:T(8,128)(2,1)S(1)} %all_to_all.5.g, bf16[256,384]{1,0:T(8,128)(2,1)S(1)} %bitcast.4, f32[8,256]{1,0:T(8,128)S(1)} %get-tuple-element.34.own, f32[1,256]{1,0:T(1,128)S(1)} %bitcast.8, bf16[256,256]{1,0:T(8,128)(2,1)S(1)} %copy-done.5, bf16[256,512]{1,0:T(8,128)(2,1)S(1)} %copy-done.1, ...), custom_call_target="tpu_custom_call" | custom-call | tf_op jit(solution)/shard_map/pallas_call | solution.py:574
  (13 shorter events, 0.0 us)
Async XLA Ops:
  0.0 1.7 %copy-start = (bf16[8,32,16,32]{3,2,1,0:T(8,128)(2,1)S(1)}, bf16[8,32,16,32]{3,2,1,0:T(8,128)(2,1)}, u32[]{:S(2)}) copy-start(bf16[8,32,16,32]{3,2,1,0:T(8,128)(2,1)} %vol.3) | copy-start | bytes 786436
  0.0 8.1 %copy-start.7 = (bf16[256,256]{1,0:T(8,128)(2,1)S(1)}, bf16[256,256]{1,0:T(8,128)(2,1)}, u32[]{:S(2)}) copy-start(bf16[256,256]{1,0:T(8,128)(2,1)} %up.1) | copy-start | bytes 393220
  0.0 8.1 %copy-start.3 = (bf16[3,3,3,32,32]{4,3,2,1,0:T(8,128)(2,1)S(1)}, bf16[3,3,3,32,32]{4,3,2,1,0:T(8,128)(2,1)}, u32[]{:S(2)}) copy-start(bf16[3,3,3,32,32]{4,3,2,1,0:T(8,128)(2,1)} %param.11) | copy-start | bytes 165892
  0.0 8.1 %copy-start.2 = (bf16[3,3,3,32,32]{4,3,2,1,0:T(8,128)(2,1)S(1)}, bf16[3,3,3,32,32]{4,3,2,1,0:T(8,128)(2,1)}, u32[]{:S(2)}) copy-start(bf16[3,3,3,32,32]{4,3,2,1,0:T(8,128)(2,1)} %param.10) | copy-start | bytes 165892
  1.1 1.4 %collective-permute-start = (bf16[16,512]{1,0:T(8,128)(2,1)S(1)}, bf16[16,512]{1,0:T(8,128)(2,1)S(1)}, u32[]{:S(2)}, u32[]{:S(2)}) collective-permute-start(bf16[16,512]{1,0:T(8,128)(2,1)S(1)} %y_face.1), channel_id=1, source_target_pairs={{0,4},{4,0},{1,5},{5,1},{2,6},{6,2},{3,7},{7,3},{8,12},{12,8},{9,1... | collective-permute-start | bytes 49160 | tf_op jit(solution)/shard_map/ppermute | solution.py:40
  2.6 6.4 %collective-permute-start.1 = (bf16[136,128]{1,0:T(8,128)(2,1)S(1)}, bf16[136,128]{1,0:T(8,128)(2,1)S(1)}, u32[]{:S(2)}, u32[]{:S(2)}) collective-permute-start(bf16[136,128]{1,0:T(8,128)(2,1)S(1)} %get-tuple-element.26), channel_id=1, source_target_pairs={{0,1},{1,0},{2,3},{3,2},{4,5},{5,4},{6,7},{7,6},{8,9},{9,8},{10,11... | collective-permute-start | bytes 104456 | tf_op jit(solution)/shard_map/ppermute | solution.py:47
  5.6 5.7 %collective-permute-start.2 = (bf16[136,128]{1,0:T(8,128)(2,1)S(1)}, bf16[136,128]{1,0:T(8,128)(2,1)S(1)}, u32[]{:S(2)}, u32[]{:S(2)}) collective-permute-start(bf16[136,128]{1,0:T(8,128)(2,1)S(1)} %get-tuple-element.27), channel_id=1, source_target_pairs={{0,3},{1,2},{2,1},{3,0},{4,7},{5,6},{6,5},{7,4},{8,11},{9,10},{10,... | collective-permute-start | bytes 104456 | tf_op jit(solution)/shard_map/ppermute | solution.py:48
  8.1 10.4 %copy-start.8 = (f32[256]{0:T(256)S(1)}, f32[256]{0:T(256)}, u32[]{:S(2)}) copy-start(f32[256]{0:T(256)} %param.12) | copy-start | bytes 3076
  11.5 5.5 %collective-permute-start.3 = (bf16[68,640]{1,0:T(8,128)(2,1)S(1)}, bf16[68,640]{1,0:T(8,128)(2,1)S(1)}, u32[]{:S(2)}, u32[]{:S(2)}) collective-permute-start(bf16[68,640]{1,0:T(8,128)(2,1)S(1)} %get-tuple-element.28), channel_id=1, source_target_pairs={{0,8},{8,0},{16,24},{24,16},{1,9},{9,1},{17,25},{25,17},{2,10},{10... | collective-permute-start | bytes 261128 | tf_op jit(solution)/shard_map/ppermute | solution.py:47
  13.0 5.5 %collective-permute-start.4 = (bf16[68,640]{1,0:T(8,128)(2,1)S(1)}, bf16[68,640]{1,0:T(8,128)(2,1)S(1)}, u32[]{:S(2)}, u32[]{:S(2)}) collective-permute-start(bf16[68,640]{1,0:T(8,128)(2,1)S(1)} %get-tuple-element.29), channel_id=1, source_target_pairs={{0,24},{8,16},{16,8},{24,0},{1,25},{9,17},{17,9},{25,1},{2,26},{10... | collective-permute-start | bytes 261128 | tf_op jit(solution)/shard_map/ppermute | solution.py:48
  18.5 14.2 %copy-start.1 = (bf16[256,512]{1,0:T(8,128)(2,1)S(1)}, bf16[256,512]{1,0:T(8,128)(2,1)}, u32[]{:S(2)}) copy-start(bf16[256,512]{1,0:T(8,128)(2,1)} %kvw.1) | copy-start | bytes 786436
  18.5 14.2 %copy-start.4 = (bf16[640,80]{1,0:T(8,128)(2,1)S(1)}, bf16[640,80]{1,0:T(8,128)(2,1)}, u32[]{:S(2)}) copy-start(bf16[640,80]{1,0:T(8,128)(2,1)} %constant.2.clone.sel) | copy-start | bytes 307204
  18.5 14.2 %copy-start.5 = (bf16[256,256]{1,0:T(8,128)(2,1)S(1)}, bf16[256,256]{1,0:T(8,128)(2,1)}, u32[]{:S(2)}) copy-start(bf16[256,256]{1,0:T(8,128)(2,1)} %qw.1) | copy-start | bytes 393220
  18.5 14.2 %copy-start.6 = (bf16[256,256]{1,0:T(8,128)(2,1)S(1)}, bf16[256,256]{1,0:T(8,128)(2,1)}, u32[]{:S(2)}) copy-start(bf16[256,256]{1,0:T(8,128)(2,1)} %ow.1) | copy-start | bytes 393220
